TPU v7x, 32 devices: a whole 2x2x4 slice. The times are simulated.
32 devices in a mesh: groups: 2 (over y), ep: 4 (over x, core), tp: 4 (over z).
Axes of the slice: x: 2, y: 2, z: 4, core: 2. Of those that a mesh axis runs over, the one named last changes fastest.
Arguments:
- hidden_in: bfloat16 [32, 4, 3584], P(('groups', 'ep', 'tp')), parts along dimension 0, may hold values from -12 to 12
- queries: bfloat16 [32, 4, 128, 576], P(('groups', 'ep', 'tp')), parts along dimension 0, may hold values from -100 to 100
- kv_cache: bfloat16 [32, 2048, 576], P(('groups', 'ep', 'tp')), parts along dimension 0, may hold values from -6 to 6
- new_kv: bfloat16 [32, 4, 576], P(('groups', 'ep', 'tp')), parts along dimension 0, may hold values from -8 to 8
- lengths: int32 [32], P(('groups', 'ep', 'tp')), parts along dimension 0, may hold values from 128 to 2048, as said below
- expert_ids: int32 [32, 4, 2], P(('groups', 'ep')), parts along dimension 0, may hold values from 0 to 3, all different within a row; in each aligned block of 16 rows (0 to 15, 16 to 31, ..., all dimensions but the last counted through in order) at most 12 rows name the same one
- value_up: bfloat16 [128, 512, 128], P(('ep', 'tp')), may hold values from -3 to 3
- out_proj: bfloat16 [128, 128, 3584], P(('ep', 'tp')), may hold values from -0.046875 to 0.046875
- norm_gain: bfloat16 [3584], replicated, may hold values from 0.099609375 to 1.8984375
- router: bfloat16 [3584, 4], replicated, may hold values from -0.09375 to 0.09375
- expert_in: bfloat16 [4, 2, 3584, 2048], P('ep', None, None, 'tp'), may hold values from -0.09375 to 0.09375
- expert_out: bfloat16 [4, 2048, 3584], P('ep', 'tp'), may hold values from -0.125 to 0.125
- shared_in: bfloat16 [2, 3584, 1024], P(None, None, 'tp'), may hold values from -0.09375 to 0.09375
- shared_out: bfloat16 [1024, 3584], P('tp'), may hold values from -0.1875 to 0.1875
Outputs:
- layer_out: bfloat16 [32, 4, 3584], P(('groups', 'ep', 'tp')), parts along dimension 0
There are 2 independent parts, one for each index of `groups`. A program takes and returns all parts, laid end to end along the dimension named above; an argument that names none is the same for every part. Nothing has to cross between parts.
Inputs may be any that keep to these rules, and one draw needn't show every extreme that they name: `expert_ids`: each row and step names 2 distinct experts; within the rows of one index of ep, over all 4 steps, no expert is named more than 12 times, and in every draw some expert is named exactly 12 times there. `lengths`: some row uses all 2048 cached positions.
All inputs are finite; a program needn't handle non-finite values.
Results may differ from a plain program's by a relative error of at most 0.014.
Values may be sent and summed in bfloat16 or wider, within the bound.
No kernel may reach another device: no remote copies, remote signals or barrier semaphores. Data moves between devices by JAX's collectives and lax.ppermute only.
A program may use at most 64 MiB of HBM per device.

v0:
```python
import jax
import jax.numpy as jnp
from jax import lax
from jax.sharding import PartitionSpec as P

LAT = 512


score_scale = 192.0 ** (-0.5)
route_scale = 2.5
norm_eps = 1e-06


def attend_block(queries, kv_cache, new_kv, lengths):
    rows_here, steps_here, heads_here, kv_width = queries.shape
    positions = kv_cache.shape[1]
    cached = (
        jnp.einsum("rshk,rck->rshc", queries, kv_cache, preferred_element_type=jnp.float32)
        * score_scale
    )
    recent = (
        jnp.einsum("rshk,rjk->rshj", queries, new_kv, preferred_element_type=jnp.float32)
        * score_scale
    )
    cache_live = lax.broadcasted_iota(jnp.int32, (rows_here, positions), 1) < lengths[:, None]
    causal = lax.broadcasted_iota(jnp.int32, (steps_here, steps_here), 1) <= lax.broadcasted_iota(
        jnp.int32, (steps_here, steps_here), 0
    )
    cached = jnp.where(cache_live[:, None, None, :], cached, -1e30)
    recent = jnp.where(causal[None, :, None, :], recent, -1e30)
    highest = jnp.maximum(cached.max(-1), recent.max(-1))[..., None]
    cached_exp = jnp.exp(cached - highest)
    recent_exp = jnp.exp(recent - highest)
    denominator = cached_exp.sum(-1, keepdims=True) + recent_exp.sum(-1, keepdims=True)
    cached_prob = (cached_exp / denominator).astype(jnp.bfloat16)
    recent_prob = (recent_exp / denominator).astype(jnp.bfloat16)
    combined = jnp.einsum(
        "rshc,rck->rshk", cached_prob, kv_cache, preferred_element_type=jnp.float32
    )
    combined = combined + jnp.einsum(
        "rshj,rjk->rshk", recent_prob, new_kv, preferred_element_type=jnp.float32
    )
    return combined[..., :LAT].astype(jnp.bfloat16)


def on_device(
    hidden_in,
    queries,
    kv_cache,
    new_kv,
    lengths,
    expert_ids,
    value_up,
    out_proj,
    norm_gain,
    router,
    expert_in,
    expert_out,
    shared_in,
    shared_out,
):
    rows_here = hidden_in.shape[0]
    steps_here = hidden_in.shape[1]
    model_width = hidden_in.shape[2]
    latent_out = attend_block(queries, kv_cache, new_kv, lengths)
    by_head = lax.all_to_all(latent_out, ("ep", "tp"), split_axis=2, concat_axis=0, tiled=True)
    head_vals = jnp.einsum(
        "rshl,hlv->rshv", by_head, value_up, preferred_element_type=jnp.float32
    ).astype(jnp.bfloat16)
    attention = lax.psum_scatter(
        jnp.einsum("rshv,hvd->rsd", head_vals, out_proj, preferred_element_type=jnp.float32),
        ("ep", "tp"),
        scatter_dimension=0,
        tiled=True,
    )
    residual = hidden_in.astype(jnp.float32) + attention
    mean_square = jnp.mean(residual * residual, axis=-1, keepdims=True)
    normed = (residual * lax.rsqrt(mean_square + norm_eps) * norm_gain.astype(jnp.float32)).astype(
        jnp.bfloat16
    )
    block_items = lax.all_gather(
        normed.reshape(rows_here * steps_here, model_width), "tp", axis=0, tiled=True
    )
    item_count = block_items.shape[0]
    expert_count = router.shape[1]
    capacity = 3 * item_count // 4
    affinity = jax.nn.sigmoid(jnp.dot(block_items, router, preferred_element_type=jnp.float32))
    picked = expert_ids.reshape(item_count, expert_ids.shape[2])
    expert_iota = lax.broadcasted_iota(jnp.int32, (1, 1, expert_count), 2)
    chosen = jnp.sum((picked[:, :, None] == expert_iota).astype(jnp.int32), axis=1)
    scored = chosen.astype(jnp.float32) * affinity
    gate_weight = route_scale * scored / jnp.sum(scored, axis=-1, keepdims=True)
    slot_index = jnp.cumsum(chosen, axis=0) - chosen
    slot_iota = lax.broadcasted_iota(jnp.int32, (1, 1, capacity), 2)
    slot_hit = (slot_index[:, :, None] == slot_iota) & (chosen[:, :, None] > 0)
    outgoing = jnp.einsum(
        "mux,mt->uxt",
        slot_hit.astype(jnp.bfloat16),
        block_items,
        preferred_element_type=jnp.float32,
    ).astype(jnp.bfloat16)
    arrived = lax.all_to_all(outgoing, "ep", split_axis=0, concat_axis=0, tiled=True)
    gate_part = jnp.einsum(
        "scd,df->scf", arrived, expert_in[0, 0], preferred_element_type=jnp.float32
    )
    up_part = jnp.einsum(
        "scd,df->scf", arrived, expert_in[0, 1], preferred_element_type=jnp.float32
    )
    activated = (jax.nn.silu(gate_part) * up_part).astype(jnp.bfloat16)
    produced = jnp.einsum(
        "scf,fd->scd", activated, expert_out[0], preferred_element_type=jnp.float32
    )
    returned_slots = lax.all_to_all(
        produced.astype(jnp.bfloat16), "ep", split_axis=0, concat_axis=0, tiled=True
    ).astype(produced.dtype)
    combine = jnp.where(slot_hit, gate_weight[:, :, None], 0.0)
    routed_part = jnp.einsum(
        "jpo,pos->js",
        combine,
        returned_slots,
        precision=lax.Precision.HIGHEST,
        preferred_element_type=jnp.float32,
    )
    shared_gate = jnp.dot(block_items, shared_in[0], preferred_element_type=jnp.float32)
    shared_up = jnp.dot(block_items, shared_in[1], preferred_element_type=jnp.float32)
    shared_act = (jax.nn.silu(shared_gate) * shared_up).astype(jnp.bfloat16)
    shared_part = jnp.dot(shared_act, shared_out, preferred_element_type=jnp.float32)
    expert_sum = lax.psum_scatter(
        (routed_part + shared_part).astype(jnp.bfloat16), "tp", scatter_dimension=0, tiled=True
    ).astype(jnp.float32)
    layer_out = (residual + expert_sum.reshape(rows_here, steps_here, model_width)).astype(
        jnp.bfloat16
    )
    return layer_out


def solution(mesh):
    in_specs = (
        P(("groups", "ep", "tp"), None, None),
        P(("groups", "ep", "tp"), None, None, None),
        P(("groups", "ep", "tp"), None, None),
        P(("groups", "ep", "tp"), None, None),
        P(("groups", "ep", "tp")),
        P(("groups", "ep"), None, None),
        P(("ep", "tp"), None, None),
        P(("ep", "tp"), None, None),
        P(),
        P(),
        P("ep", None, None, "tp"),
        P("ep", "tp", None),
        P(None, None, "tp"),
        P("tp", None),
    )
    out_specs = P(("groups", "ep", "tp"), None, None)
    return jax.shard_map(
        on_device, mesh=mesh, in_specs=in_specs, out_specs=out_specs, check_vma=False
    )
```

profile of v0, /device:TPU:0, one launch (start us, length us, event | category | flops | bytes accessed | tf_op | source)
XLA Modules:
  0.0 234.1 jit_solution(7596553311977979096)
XLA Ops:
  6.5 0.0 copy-start
  6.5 0.0 copy-start.1
  6.5 0.0 copy-start.3
  6.5 0.0 all-reduce.5.cloned.1.call-start
  7.4 0.8 copy-done
  8.2 3.2 %fusion.6 = (f32[4,128]{1,0:T(4,128)S(1)}, f32[4,128,2048]{2,1,0:T(8,128)S(1)}) fusion(pred[2048]{0:T(1024)(128)(4,1)S(1)} %iota_compare_fusion.1, bf16[1,2048,576]{1,2,0:T(8,128)(2,1)S(1)} %copy-done, bf16[1,4,128,576]{2,3,1,0:T(8,128)(2,1)} %param.15), kind=kOutput, calls=%fused_computation.11 | convolution fusion | flops 1211104768 | bytes 7147520 | tf_op jit(solution)/shard_map/rshk,rck->rshc/dot_general | solution.py:18
  11.4 0.0 copy-done.1
  11.4 0.0 copy-done.3
  11.4 0.2 fusion.97
  11.6 0.9 fusion.14
  12.6 1.7 fusion.15
  14.3 0.4 fusion.27
  14.7 0.4 copy.40
  15.1 22.8 %all_to_all.28 = bf16[1,4,128,512]{3,1,0,2:T(4,128)(2,1)} all-to-all(bf16[1,4,128,512]{3,1,0,2:T(4,128)(2,1)S(1)} %copy.40), channel_id=1, replica_groups=mesh['groups'=2,'ep'=4,'tp'=4] {'ep','tp'}, dimensions={2} | all-to-all | bytes 1048576 | tf_op jit(solution)/shard_map/all_to_all | solution.py:66
  38.0 0.0 copy-start.4
  38.0 0.0 copy-start.5
  38.0 0.0 copy-start.8
  38.0 0.0 copy-start.2
  38.0 5.3 %fusion.2 = f32[16,4,3584]{2,0,1:T(8,128)S(1)} fusion(bf16[8,128,3584]{2,1,0:T(8,128)(2,1)} %param.21, bf16[8,512,128]{2,1,0:T(8,128)(2,1)} %param.20, bf16[1,4,16,8,512]{4,1,3,2,0:T(4,128)(2,1)} %bitcast.112), kind=kOutput, calls=%fused_computation.2 | convolution fusion | flops 536936448 | bytes 9830400 | tf_op jit(solution)/shard_map/rshv,hvd->rsd/dot_general | solution.py:71
  43.3 0.0 copy-start.6
  43.3 1.6 copy.43
  44.9 0.0 all-reduce.5.cloned.1.call-update
  44.9 0.0 copy-done.4
  44.9 0.0 copy-done.5
  44.9 0.1 eq.28
  45.0 0.1 copy.45
  45.2 0.1 copy.47
  45.3 0.0 copy-done.8
  45.3 0.6 dynamic-slice
  45.9 90.4 %all-reduce.5.cloned.1.call-done = f32[16,4,3584]{2,1,0:T(4,128)} async-done(((f32[16,4,3584]{2,1,0:T(4,128)}), f32[16,4,3584]{2,1,0:T(4,128)}) %all-reduce.5.cloned.1.call-update) | async-done | bytes 917520
  136.2 0.0 copy-done.2
  136.2 1.5 multiply_reduce_fusion
  137.8 1.5 multiply_convert_fusion
  139.3 14.3 %all-gather = bf16[1,16,3584]{2,0,1:T(2,128)(2,1)S(1)} all-gather(bf16[1,4,3584]{2,0,1:T(2,128)(2,1)S(1)} %copy.48), channel_id=2, replica_groups=mesh['groups'=2,'ep'=4,'tp'=4] {'tp'}, dimensions={1}, use_global_device_ids=true | all-gather | bytes 143360 | tf_op jit(solution)/shard_map/all_gather | solution.py:81
  153.7 1.2 convolution_convert_fusion.1
  154.8 3.5 %all-to-all-start.1 = ((bf16[4,12,3584]{2,1,0:T(8,128)(2,1)}), bf16[4,12,3584]{2,1,0:T(8,128)(2,1)S(1)}, u32[]{:S(2)}, u32[]{:S(2)}) async-start(bf16[4,12,3584]{2,1,0:T(8,128)(2,1)} %convolution_convert_fusion.1), calls=%async_computation.1 | async-start | bytes 917504 | tf_op jit(solution)/shard_map/all_to_all | solution.py:102
  158.3 0.0 copy-done.6
  158.3 0.2 fusion.98
  158.5 7.9 %all-to-all-done.1 = bf16[4,12,3584]{2,1,0:T(8,128)(2,1)S(1)} async-done(((bf16[4,12,3584]{2,1,0:T(8,128)(2,1)}), bf16[4,12,3584]{2,1,0:T(8,128)(2,1)S(1)}, u32[]{:S(2)}, u32[]{:S(2)}) %all-to-all-start.1) | async-done | bytes 344096 | tf_op jit(solution)/shard_map/all_to_all | solution.py:102
  166.4 2.8 %fusion.9 = f32[4,12,512]{2,1,0:T(8,128)S(1)} fusion(bf16[4,12,3584]{2,1,0:T(8,128)(2,1)S(1)} %all-to-all-done.1, bf16[1,2,3584,512]{3,2,1,0:T(8,128)(2,1)} %param.24), kind=kOutput, calls=%fused_computation.14 | convolution fusion | flops 176160768 | bytes 4112384 | tf_op jit(solution)/shard_map/scd,df->scf/dot_general | solution.py:103
  169.2 5.4 %convolution_convert_fusion = bf16[4,12,3584]{2,1,0:T(8,128)(2,1)} fusion(bf16[1,512,3584]{2,1,0:T(8,128)(2,1)} %param.25, bf16[4,12,3584]{2,1,0:T(8,128)(2,1)S(1)} %all-to-all-done.1, bf16[1,2,3584,512]{3,2,1,0:T(8,128)(2,1)} %param.24, f32[4,12,512]{2,1,0:T(8,128)S(1)} %fusion.9), kind=kOutput, calls=%fused_computation.3 | convolution fusion | flops 352641024 | bytes 8126464 | tf_op jit(solution)/shard_map/scf,fd->scd/dot_general | solution.py:110
  174.6 3.5 %all-to-all-start.2 = ((bf16[4,12,3584]{2,1,0:T(8,128)(2,1)}), bf16[4,12,3584]{2,1,0:T(8,128)(2,1)S(1)}, u32[]{:S(2)}, u32[]{:S(2)}) async-start(bf16[4,12,3584]{2,1,0:T(8,128)(2,1)} %convolution_convert_fusion), calls=%async_computation.2 | async-start | bytes 917504 | tf_op jit(solution)/shard_map/all_to_all | solution.py:113
  178.0 0.0 copy-start.7
  178.1 0.0 all-reduce.7.cloned.1.call-start
  178.1 1.8 fusion.22
  180.0 6.2 %all-to-all-done.2 = bf16[4,12,3584]{2,1,0:T(8,128)(2,1)S(1)} async-done(((bf16[4,12,3584]{2,1,0:T(8,128)(2,1)}), bf16[4,12,3584]{2,1,0:T(8,128)(2,1)S(1)}, u32[]{:S(2)}, u32[]{:S(2)}) %all-to-all-start.2) | async-done | bytes 344096 | tf_op jit(solution)/shard_map/all_to_all | solution.py:113
  186.1 0.7 convolution_bitcast_fusion
  186.8 3.9 %fusion.5 = bf16[16,3584]{1,0:T(8,128)(2,1)} fusion(f32[16,3584]{1,0:T(8,128)S(1)} %convolution_bitcast_fusion, bf16[256,3584]{1,0:T(8,128)(2,1)} %param.27, bf16[2,3584,256]{2,1,0:T(8,128)(2,1)} %param.26, bf16[1,16,3584]{2,1,0:T(8,128)(2,1)S(1)} %copy.54, f32[16,256]{1,0:T(8,128)S(1)} %fusion.22), kind=kOutput, calls=%fused_computation.7 | convolution fusion | flops 58859520 | bytes 4145152 | tf_op jit(solution)/shard_map/dot_general | solution.py:127
  190.7 0.0 all-reduce.7.cloned.1.call-update
  190.7 0.0 copy-done.7
  190.7 0.6 dynamic-slice.2
  191.9 33.3 %all-reduce.7.cloned.1.call-done = bf16[16,3584]{1,0:T(8,128)(2,1)} async-done(((bf16[16,3584]{1,0:T(8,128)(2,1)}), bf16[16,3584]{1,0:T(8,128)(2,1)}) %all-reduce.7.cloned.1.call-update) | async-done | bytes 114704
  225.2 2.1 fusion.70
  (16 shorter events, 0.2 us)
Async XLA Ops:
  6.5 1.7 copy-start
  6.5 4.8 %copy-start.1 = (bf16[1,4,128,576]{2,3,1,0:T(8,128)(2,1)S(1)}, bf16[1,4,128,576]{2,3,1,0:T(8,128)(2,1)}, u32[]{:S(2)}) copy-start(bf16[1,4,128,576]{2,3,1,0:T(8,128)(2,1)} %param.15) | copy-start | bytes 1769476
  6.5 4.8 %copy-start.3 = (bf16[1,4,576]{2,1,0:T(4,128)(2,1)S(1)}, bf16[1,4,576]{2,1,0:T(4,128)(2,1)}, u32[]{:S(2)}) copy-start(bf16[1,4,576]{2,1,0:T(4,128)(2,1)} %param.17) | copy-start | bytes 13828
  6.5 129.7 %all-reduce.5.cloned.1.call-start = ((), (), s32[]{:S(2)}) async-start(), calls=%async_computation.3 | async-start | bytes 1835008
  38.0 6.9 %copy-start.4 = (bf16[3584]{0:T(1024)(128)(2,1)S(1)}, bf16[3584]{0:T(1024)(128)(2,1)}, u32[]{:S(2)}) copy-start(bf16[3584]{0:T(1024)(128)(2,1)} %param.22) | copy-start | bytes 21508
  38.0 7.0 %copy-start.5 = (s32[4,4,2]{1,2,0:T(2,128)S(1)}, s32[4,4,2]{1,2,0:T(2,128)}, u32[]{:S(2)}) copy-start(s32[4,4,2]{1,2,0:T(2,128)} %param.19) | copy-start | bytes 388
  38.0 7.3 %copy-start.8 = (u32[32]{0:T(128)S(1)}, u32[32]{0:T(128)}, u32[]{:S(2)}) copy-start(u32[32]{0:T(128)} %constant.40) | copy-start | bytes 388
  38.0 98.3 %copy-start.2 = (bf16[1,4,3584]{2,1,0:T(4,128)(2,1)S(1)}, bf16[1,4,3584]{2,1,0:T(4,128)(2,1)}, u32[]{:S(2)}) copy-start(bf16[1,4,3584]{2,1,0:T(4,128)(2,1)} %param.14) | copy-start | bytes 86020
  43.3 115.0 %copy-start.6 = (bf16[3584,4]{0,1:T(4,128)(2,1)S(1)}, bf16[3584,4]{0,1:T(4,128)(2,1)}, u32[]{:S(2)}) copy-start(bf16[3584,4]{0,1:T(4,128)(2,1)} %param.23) | copy-start | bytes 86020
  154.8 11.6 %all-to-all-start.1 = ((bf16[4,12,3584]{2,1,0:T(8,128)(2,1)}), bf16[4,12,3584]{2,1,0:T(8,128)(2,1)S(1)}, u32[]{:S(2)}, u32[]{:S(2)}) async-start(bf16[4,12,3584]{2,1,0:T(8,128)(2,1)} %convolution_convert_fusion.1), calls=%async_computation.1 | async-start | bytes 917504 | tf_op jit(solution)/shard_map/all_to_all | solution.py:102
  174.6 11.6 %all-to-all-start.2 = ((bf16[4,12,3584]{2,1,0:T(8,128)(2,1)}), bf16[4,12,3584]{2,1,0:T(8,128)(2,1)S(1)}, u32[]{:S(2)}, u32[]{:S(2)}) async-start(bf16[4,12,3584]{2,1,0:T(8,128)(2,1)} %convolution_convert_fusion), calls=%async_computation.2 | async-start | bytes 917504 | tf_op jit(solution)/shard_map/all_to_all | solution.py:113
  178.0 12.7 %copy-start.7 = (u32[32]{0:T(128)S(1)}, u32[32]{0:T(128)}, u32[]{:S(2)}) copy-start(u32[32]{0:T(128)} %constant.44) | copy-start | bytes 388
  178.1 47.2 %all-reduce.7.cloned.1.call-start = ((), (), s32[]{:S(2)}) async-start(), calls=%async_computation.4 | async-start | bytes 229376
Sparse Core Ops, SparseCore 0:
  45.0 91.1 all-reduce.4
  190.8 34.3 all-reduce.6
where the time goes:
time: 235 us; the launch traced here: 234 us
  waiting for transfers between devices  138 us (59%)
  blocking collectives  37.2 us (16%)
  matrix products  26.6 us (11%)
  between operations  15.1 us (6%)
  starting transfers between devices  6.97 us (3%)
  other arithmetic  6.16 us (3%)
  local copies, waits for them, and re-layouts  4.37 us (2%)
    unnamed x4, waiting for transfers between devices  124 us
    all_to_all x1, blocking collectives, on_device(): lax.all_to_all(latent_out, ('ep', 'tp'), split_axis=2, concat_axis=0, til...  22.8 us
    all_gather x1, blocking collectives, on_device(): lax.all_gather(normed.reshape(rows_here * steps_here, model_width), 'tp',...  14.3 us
    all_to_all x1, waiting for transfers between devices, on_device(): lax.all_to_all(outgoing, 'ep', split_axis=0, concat_axis=0, tiled=True)  7.89 us
    all_to_all x1, waiting for transfers between devices, on_device(): lax.all_to_all(produced.astype(jnp.bfloat16), 'ep', split_axis=0, concat_...  6.17 us
    dot_general x1, matrix products, on_device(): jnp.einsum('scf,fd->scd', activated, expert_out[0], preferred_element_typ...  5.4 us
    dot_general x1, matrix products, on_device(): jnp.einsum('rshv,hvd->rsd', head_vals, out_proj, preferred_element_type=j...  5.31 us
  transfers between devices with their start and end apart: 4, of which 4 were waited for; matrix products, arithmetic and copies ran while one was open for 2% of the time, Pallas kernels for 0%

commit v1 on v0

v1 whole, which is shorter than its diff:
```python
import jax
import jax.numpy as jnp
from jax import lax
from jax.sharding import Mesh
from jax.sharding import PartitionSpec as P

LAT = 512


score_scale = 192.0 ** (-0.5)
route_scale = 2.5
norm_eps = 1e-06

CHIPS = ("epx", "tp")
ALL = ("epx", "core", "tp")


def attend_block(queries, kv_cache, new_kv, lengths):
    rows_here, steps_here, heads_here, kv_width = queries.shape
    positions = kv_cache.shape[1]
    cached = (
        jnp.einsum("rshk,rck->rshc", queries, kv_cache, preferred_element_type=jnp.float32)
        * score_scale
    )
    recent = (
        jnp.einsum("rshk,rjk->rshj", queries, new_kv, preferred_element_type=jnp.float32)
        * score_scale
    )
    cache_live = lax.broadcasted_iota(jnp.int32, (rows_here, positions), 1) < lengths[:, None]
    causal = lax.broadcasted_iota(jnp.int32, (steps_here, steps_here), 1) <= lax.broadcasted_iota(
        jnp.int32, (steps_here, steps_here), 0
    )
    cached = jnp.where(cache_live[:, None, None, :], cached, -1e30)
    recent = jnp.where(causal[None, :, None, :], recent, -1e30)
    highest = jnp.maximum(cached.max(-1), recent.max(-1))[..., None]
    cached_exp = jnp.exp(cached - highest)
    recent_exp = jnp.exp(recent - highest)
    denominator = cached_exp.sum(-1, keepdims=True) + recent_exp.sum(-1, keepdims=True)
    cached_prob = (cached_exp / denominator).astype(jnp.bfloat16)
    recent_prob = (recent_exp / denominator).astype(jnp.bfloat16)
    combined = jnp.einsum(
        "rshc,rck->rshk", cached_prob, kv_cache, preferred_element_type=jnp.float32
    )
    combined = combined + jnp.einsum(
        "rshj,rjk->rshk", recent_prob, new_kv, preferred_element_type=jnp.float32
    )
    return combined[..., :LAT].astype(jnp.bfloat16)


def swap_cores(x):
    return lax.ppermute(x, "core", [(0, 1), (1, 0)])


def chip_exchange(x):
    return lax.all_to_all(x, CHIPS, split_axis=0, concat_axis=0, tiled=True)


def sum_at_rows(kept, sent, chips):
    half = kept + swap_cores(sent.astype(jnp.bfloat16)).astype(jnp.float32)
    width = half.shape[1]
    parts = chip_exchange(half.astype(jnp.bfloat16).reshape(chips, -1, width))
    return jnp.sum(parts.astype(jnp.float32), axis=0)


def on_device(
    hidden_in,
    queries,
    kv_cache,
    new_kv,
    lengths,
    expert_ids,
    value_up,
    out_proj,
    norm_gain,
    router,
    expert_in,
    expert_out,
    shared_in,
    shared_out,
):
    rows_here, steps_here, model_width = hidden_in.shape
    items = rows_here * steps_here
    columns = lax.axis_size("epx")
    depth = lax.axis_size("tp")
    chips = columns * depth
    core = lax.axis_index("core")
    column = lax.axis_index("epx")
    place = lax.axis_index("tp")
    expert_count = router.shape[1]

    latent_out = attend_block(queries, kv_cache, new_kv, lengths)
    by_head = lax.all_to_all(latent_out, ALL, split_axis=2, concat_axis=0, tiled=True)
    head_vals = jnp.einsum(
        "rshl,hlv->rshv", by_head, value_up, preferred_element_type=jnp.float32
    ).astype(jnp.bfloat16)
    partial = jnp.einsum(
        "rshv,hvd->rsd", head_vals, out_proj, preferred_element_type=jnp.float32
    ).reshape(columns, 2, depth * items, model_width)
    kept = lax.dynamic_index_in_dim(partial, core, 1, keepdims=False)
    sent = lax.dynamic_index_in_dim(partial, 1 - core, 1, keepdims=False)
    attention = sum_at_rows(
        kept.reshape(-1, model_width), sent.reshape(-1, model_width), chips
    )
    residual = hidden_in.reshape(items, model_width).astype(jnp.float32) + attention
    mean_square = jnp.mean(residual * residual, axis=-1, keepdims=True)
    normed = (residual * lax.rsqrt(mean_square + norm_eps) * norm_gain.astype(jnp.float32)).astype(
        jnp.bfloat16
    )
    affinity = jax.nn.sigmoid(jnp.dot(normed, router, preferred_element_type=jnp.float32))
    picked = lax.dynamic_slice_in_dim(expert_ids, place * rows_here, rows_here, 0).reshape(
        items, expert_ids.shape[2]
    )
    expert_iota = lax.broadcasted_iota(jnp.int32, (1, 1, expert_count), 2)
    chosen = jnp.sum((picked[:, :, None] == expert_iota).astype(jnp.float32), axis=1)
    scored = chosen * affinity
    gate_weight = route_scale * scored / jnp.sum(scored, axis=-1, keepdims=True)
    gate_high = gate_weight.astype(jnp.bfloat16)
    gate_low = (gate_weight - gate_high.astype(jnp.float32)).astype(jnp.bfloat16)
    spare = -(2 * expert_count) % 128
    payload = jnp.concatenate(
        [normed, gate_high, gate_low, jnp.zeros((items, spare), jnp.bfloat16)], axis=1
    )
    mine = chip_exchange(jnp.broadcast_to(payload[None], (chips,) + payload.shape)).reshape(
        chips * items, -1
    )
    tokens = jnp.concatenate([mine, swap_cores(mine)], axis=0)
    block_items = tokens[:, :model_width]
    expert_here = column * 2 + core
    gate_pairs = tokens[:, model_width : model_width + 2 * expert_count].astype(jnp.float32)
    gates = gate_pairs[:, :expert_count] + gate_pairs[:, expert_count:]
    gate_here = lax.dynamic_slice_in_dim(gates, expert_here, 1, 1)

    gate_part = jnp.dot(block_items, expert_in[0, 0], preferred_element_type=jnp.float32)
    up_part = jnp.dot(block_items, expert_in[0, 1], preferred_element_type=jnp.float32)
    activated = (jax.nn.silu(gate_part) * up_part).astype(jnp.bfloat16)
    routed = gate_here * jnp.dot(activated, expert_out[0], preferred_element_type=jnp.float32)

    own = lax.dynamic_slice_in_dim(mine, column * depth * items, depth * items, 0)[
        :, :model_width
    ]
    shared_gate = jnp.dot(own, shared_in[0], preferred_element_type=jnp.float32)
    shared_up = jnp.dot(own, shared_in[1], preferred_element_type=jnp.float32)
    shared_act = (jax.nn.silu(shared_gate) * shared_up).astype(jnp.bfloat16)
    shared_part = jnp.dot(shared_act, shared_out, preferred_element_type=jnp.float32)

    kept = routed[: chips * items].reshape(columns, depth * items, model_width)
    at_column = lax.broadcasted_iota(jnp.int32, (columns, 1, 1), 0) == column
    kept = kept + jnp.where(at_column, shared_part[None], 0.0)
    expert_sum = sum_at_rows(
        kept.reshape(-1, model_width), routed[chips * items :], chips
    )
    layer_out = (residual + expert_sum).astype(jnp.bfloat16)
    return layer_out.reshape(rows_here, steps_here, model_width)


def solution(mesh):
    sizes = mesh.shape
    fine = Mesh(
        mesh.devices.reshape(sizes["groups"], sizes["ep"] // 2, 2, sizes["tp"]),
        ("groups", "epx", "core", "tp"),
    )
    ep = ("epx", "core")
    rows = ("groups", "epx", "core", "tp")
    in_specs = (
        P(rows, None, None),
        P(rows, None, None, None),
        P(rows, None, None),
        P(rows, None, None),
        P(rows),
        P(("groups",) + ep, None, None),
        P(ALL, None, None),
        P(ALL, None, None),
        P(),
        P(),
        P(ep, None, None, "tp"),
        P(ep, "tp", None),
        P(None, None, "tp"),
        P("tp", None),
    )
    out_specs = P(rows, None, None)
    return jax.shard_map(
        on_device, mesh=fine, in_specs=in_specs, out_specs=out_specs, check_vma=False
    )
```

time: 235 us -> 106 us (0.45)
  waiting for transfers between devices: 138 us -> 33.1 us
  blocking collectives: 37.2 us -> 12 us
  between operations: 15.1 us -> 1.04 us
  starting transfers between devices: 6.97 us -> 14.8 us
  local copies, waits for them, and re-layouts: 4.37 us -> 12 us
    unnamed x4 -> x0, waiting for transfers between devices: 124 us -> none
    all_to_all x2 -> x3, waiting for transfers between devices: 14.1 us -> 32.7 us  [the longest x2 17.1 us: chip_exchange(): return lax.all_to_all(x, CHIPS, split_axis=0, concat_axis=0, tiled=True)]
    all_gather x1 -> x0, blocking collectives: 14.3 us -> none  [on_device(): lax.all_gather(normed.reshape(rows_here * steps_here, model_width), 'tp',...]
    all_to_all x1, blocking collectives: 22.8 us -> 12 us  [chip_exchange(): return lax.all_to_all(x, CHIPS, split_axis=0, concat_axis=0, tiled=True)]
    all_to_all x2 -> x3, starting transfers between devices: 6.93 us -> 14.2 us  [the longest x1 7.39 us: on_device(): lax.all_to_all(latent_out, ALL, split_axis=2, concat_axis=0, tiled=True)]
    reshape x0 -> x4, local copies, waits for them, and re-layouts: none -> 3.03 us  [the longest x2 1.73 us: sum_at_rows(): parts = chip_exchange(half.astype(jnp.bfloat16).reshape(chips, -1, width))]
    dot_general x6 -> x4, matrix products: 12 us -> 11.2 us  [the longest x1 4.82 us: on_device(): jnp.dot(activated, expert_out[0], preferred_element_type=jnp.float32)]
  transfers between devices with their start and end apart: 4 -> 6, of which waited for: 4 -> 4; matrix products, arithmetic and copies ran while one was open for 2% -> 8% of each run, Pallas kernels for 0% -> 0%
where the time goes in v1:
time: 106 us; the launch traced here: 105 us
  waiting for transfers between devices  33.1 us (31%)
  matrix products  26.6 us (25%)
  starting transfers between devices  14.8 us (14%)
  local copies, waits for them, and re-layouts  12 us (11%)
  blocking collectives  12 us (11%)
  other arithmetic  5.18 us (5%)
    all_to_all x2, waiting for transfers between devices, chip_exchange(): return lax.all_to_all(x, CHIPS, split_axis=0, concat_axis=0, tiled=True)  17.1 us
    all_to_all x1, waiting for transfers between devices, on_device(): lax.all_to_all(latent_out, ALL, split_axis=2, concat_axis=0, tiled=True)  15.6 us
    all_to_all x1, blocking collectives, chip_exchange(): return lax.all_to_all(x, CHIPS, split_axis=0, concat_axis=0, tiled=True)  12 us
    all_to_all x1, starting transfers between devices, on_device(): lax.all_to_all(latent_out, ALL, split_axis=2, concat_axis=0, tiled=True)  7.39 us
    all_to_all x2, starting transfers between devices, chip_exchange(): return lax.all_to_all(x, CHIPS, split_axis=0, concat_axis=0, tiled=True)  6.8 us
    dot_general x1, matrix products, on_device(): jnp.einsum('rshv,hvd->rsd', head_vals, out_proj, preferred_element_type=j...  6.05 us
    dot_general x1, matrix products, on_device(): jnp.dot(activated, expert_out[0], preferred_element_type=jnp.float32)  4.82 us
    dot_general x1, matrix products, on_device(): jnp.dot(shared_act, shared_out, preferred_element_type=jnp.float32)  3.91 us
  transfers between devices with their start and end apart: 6, of which 4 were waited for; matrix products, arithmetic and copies ran while one was open for 8% of the time, Pallas kernels for 0%

profile of v1, /device:TPU:0, one launch (start us, length us, event | category | flops | bytes accessed | tf_op | source)
XLA Modules:
  0.0 104.7 jit_solution(3958041317438843610)
XLA Ops:
  0.0 0.0 copy-start
  0.0 0.0 copy-start.1
  0.0 0.0 copy-start.5
  0.8 0.9 copy-done
  1.7 3.2 %fusion.5 = (f32[4,128]{1,0:T(4,128)S(1)}, f32[4,128,2048]{2,1,0:T(8,128)S(1)}) fusion(pred[2048]{0:T(1024)(128)(4,1)S(1)} %iota_compare_fusion, bf16[1,2048,576]{1,2,0:T(8,128)(2,1)S(1)} %copy-done, bf16[1,4,128,576]{2,3,1,0:T(8,128)(2,1)} %param.15), kind=kOutput, calls=%fused_computation.7 | convolution fusion | flops 1211104768 | bytes 7147520 | tf_op jit(solution)/shard_map/rshk,rck->rshc/dot_general | solution.py:22
  4.8 0.0 copy-done.1
  4.8 0.0 copy-done.5
  4.9 0.2 fusion.92
  5.1 0.9 fusion.13
  6.1 1.7 %fusion.14 = f32[4,128,576]{1,2,0:T(8,128)S(1)} fusion(bf16[1,2048,576]{1,2,0:T(8,128)(2,1)S(1)} %copy-done, f32[4,128,2048]{2,1,0:T(8,128)S(1)} %get-tuple-element.10, f32[4,128]{1,0:T(4,128)S(1)} %add.76, f32[4,128]{1,0:T(4,128)S(1)} %max.9, pred[2048]{0:T(1024)(128)(4,1)S(1)} %iota_compare_fusion), kind=kOutput, calls=%fused_computation.16 | convolution fusion | flops 1213202432 | bytes 7739392 | tf_op jit(solution)/shard_map/rshc,rck->rshk/dot_general | solution.py:41
  7.8 0.4 fusion.26
  8.2 1.2 %copy.29 = bf16[1,4,128,512]{3,1,0,2:T(4,128)(2,1)} copy(bf16[1,4,128,512]{2,3,1,0:T(8,128)(2,1)S(1)} %slice.50) | data formatting | bytes 1048576 | tf_op jit(solution)/shard_map/slice | solution.py:47
  9.4 7.4 %all-to-all-start = ((bf16[1,4,128,512]{3,1,0,2:T(4,128)(2,1)}), bf16[1,4,128,512]{3,1,0,2:T(4,128)(2,1)S(1)}, u32[]{:S(2)}, u32[]{:S(2)}) async-start(bf16[1,4,128,512]{3,1,0,2:T(4,128)(2,1)} %copy.29), calls=%async_computation | async-start | bytes 1048576 | tf_op jit(solution)/shard_map/all_to_all | solution.py:92
  16.8 15.6 %all-to-all-done = bf16[1,4,128,512]{3,1,0,2:T(4,128)(2,1)S(1)} async-done(((bf16[1,4,128,512]{3,1,0,2:T(4,128)(2,1)}), bf16[1,4,128,512]{3,1,0,2:T(4,128)(2,1)S(1)}, u32[]{:S(2)}, u32[]{:S(2)}) %all-to-all-start) | async-done | bytes 524320 | tf_op jit(solution)/shard_map/all_to_all | solution.py:92
  32.3 6.0 %fusion.2 = f32[16,4,3584]{2,0,1:T(8,128)} fusion(bf16[8,128,3584]{2,1,0:T(8,128)(2,1)} %param.21, bf16[8,512,128]{2,1,0:T(8,128)(2,1)} %param.20, bf16[1,4,16,8,512]{4,1,3,2,0:T(4,128)(2,1)S(1)} %bitcast.104), kind=kOutput, calls=%fused_computation.3 | convolution fusion | flops 536936448 | bytes 9830400 | tf_op jit(solution)/shard_map/rshv,hvd->rsd/dot_general | solution.py:96
  38.4 0.0 copy-start.6
  38.4 0.0 copy-start.7
  38.4 1.8 %copy.32 = f32[16,4,3584]{2,1,0:T(4,128)S(1)} copy(f32[16,4,3584]{2,0,1:T(8,128)} %fusion.2) | data formatting | bytes 1835008 | tf_op jit(solution)/shard_map/rshv,hvd->rsd/dot_general | solution.py:96
  40.2 1.2 %reshape.136 = f32[2,2,16,3584]{3,2,1,0:T(8,128)} reshape(f32[16,4,3584]{2,1,0:T(4,128)S(1)} %copy.32) | data formatting | bytes 1835008 | tf_op jit(solution)/shard_map/reshape | solution.py:98
  41.4 1.0 dynamic-slice_convert_fusion
  42.5 0.1 collective-permute-start
  42.5 1.1 %constant_dynamic-slice_fusion.1 = f32[2,1,16,3584]{3,2,1,0:T(8,128)S(1)} fusion(f32[2,2,16,3584]{3,2,1,0:T(8,128)} %reshape.136, s32[]{:T(128)S(6)} %select_n.33), kind=kLoop, calls=%fused_computation.97 | loop fusion | bytes 917508 | tf_op jit(solution)/shard_map/jit(dynamic_index_in_dim)/dynamic_slice | solution.py:99
  43.6 0.4 collective-permute-done
  44.0 0.1 fusion.53
  44.1 0.7 reshape.138
  44.8 3.4 %all-to-all-start.1 = ((bf16[8,4,3584]{2,1,0:T(4,128)(2,1)}), bf16[8,4,3584]{2,1,0:T(4,128)(2,1)S(1)}, u32[]{:S(2)}, u32[]{:S(2)}) async-start(bf16[8,4,3584]{2,1,0:T(4,128)(2,1)} %reshape.138), calls=%async_computation.1 | async-start | bytes 458752 | tf_op jit(solution)/shard_map/all_to_all | solution.py:55
  48.2 0.0 copy-done.6
  48.2 0.7 fusion.86
  48.9 0.1 convert_reduce_fusion.2
  49.0 8.8 %all-to-all-done.1 = bf16[8,4,3584]{2,1,0:T(4,128)(2,1)S(1)} async-done(((bf16[8,4,3584]{2,1,0:T(4,128)(2,1)}), bf16[8,4,3584]{2,1,0:T(4,128)(2,1)S(1)}, u32[]{:S(2)}, u32[]{:S(2)}) %all-to-all-start.1) | async-done | bytes 229408 | tf_op jit(solution)/shard_map/all_to_all | solution.py:55
  57.8 0.1 convert_reduce_fusion.1
  57.9 0.0 copy-done.4
  57.9 0.0 copy-start.3
  57.9 0.1 multiply_reduce_fusion
  58.1 0.5 copy-done.3
  58.5 0.1 multiply_convert_fusion.2
  58.6 0.0 copy-done.7
  58.6 0.3 fusion.93
  58.9 0.1 subtract_convert_fusion
  59.0 0.1 concatenate.6
  59.1 0.7 broadcast_in_dim.74
  59.8 3.4 %all-to-all-start.2 = ((bf16[8,4,3712]{2,1,0:T(4,128)(2,1)}), bf16[8,4,3712]{2,1,0:T(4,128)(2,1)S(1)}, u32[]{:S(2)}, u32[]{:S(2)}) async-start(bf16[8,4,3712]{2,1,0:T(4,128)(2,1)} %broadcast_in_dim.74), calls=%async_computation.2 | async-start | bytes 475136 | tf_op jit(solution)/shard_map/all_to_all | solution.py:55
  63.3 0.1 broadcast_in_dim.75
  63.3 0.1 broadcast_in_dim.76
  63.4 8.4 %all-to-all-done.2 = bf16[8,4,3712]{2,1,0:T(4,128)(2,1)S(1)} async-done(((bf16[8,4,3712]{2,1,0:T(4,128)(2,1)}), bf16[8,4,3712]{2,1,0:T(4,128)(2,1)S(1)}, u32[]{:S(2)}, u32[]{:S(2)}) %all-to-all-start.2) | async-done | bytes 237600 | tf_op jit(solution)/shard_map/all_to_all | solution.py:55
  71.8 0.1 reshape.139
  71.9 0.1 collective-permute-start.1
  72.0 2.5 %fusion.21 = f32[16,256]{1,0:T(8,128)} fusion(bf16[2,3584,256]{2,1,0:T(8,128)(2,1)} %param.26, bf16[32,3712]{1,0:T(8,128)(2,1)S(1)} %reshape.139, s32[]{:T(128)S(6)} %select_n.37), kind=kOutput, calls=%fused_computation.23 | convolution fusion | flops 29360128 | bytes 1966084 | tf_op jit(solution)/shard_map/dot_general | solution.py:141
  74.4 0.0 collective-permute-done.1
  74.4 0.0 copy-start.2
  74.5 3.6 %fusion.7 = f32[64,512]{1,0:T(8,128)} fusion(bf16[1,2,3584,512]{3,2,1,0:T(8,128)(2,1)} %param.24, bf16[64,3712]{1,0:T(8,128)(2,1)S(1)} %constant_dynamic-update-slice_fusion), kind=kOutput, calls=%fused_computation.9 | convolution fusion | flops 234881024 | bytes 4259840 | tf_op jit(solution)/shard_map/dot_general | solution.py:134
  78.1 0.1 fusion.91
  78.2 0.0 copy-done.2
  78.2 0.2 fusion.71
  78.3 4.8 %convolution_multiply_fusion = f32[64,3584]{1,0:T(8,128)S(1)} fusion(bf16[1,512,3584]{2,1,0:T(8,128)(2,1)} %param.25, f32[64]{0:T(128)S(1)} %fusion.71, f32[64,512]{1,0:T(8,128)} %fusion.7, bf16[1,2,3584,512]{3,2,1,0:T(8,128)(2,1)} %param.24, bf16[64,3712]{1,0:T(8,128)(2,1)} %copy-done.2), kind=kOutput, calls=%fused_computation.2 | convolution fusion | flops 470188032 | bytes 8847616 | tf_op jit(solution)/shard_map/dot_general | solution.py:136
  83.2 0.7 slice.98
  83.9 0.5 collective-permute-start.2
  84.4 3.9 %fusion.35 = f32[16,3584]{1,0:T(8,128)} fusion(bf16[256,3584]{1,0:T(8,128)(2,1)} %param.27, bf16[2,3584,256]{2,1,0:T(8,128)(2,1)} %param.26, bf16[32,3712]{1,0:T(8,128)(2,1)S(1)} %reshape.139, s32[]{:T(128)S(6)} %select_n.37, f32[16,256]{1,0:T(8,128)} %fusion.21), kind=kOutput, calls=%fused_computation.34 | convolution fusion | flops 58744832 | bytes 4030468 | tf_op jit(solution)/shard_map/dot_general | solution.py:144
  88.3 0.0 collective-permute-done.2
  88.3 1.9 %fusion.52 = bf16[32,3584]{1,0:T(8,128)(2,1)} fusion(f32[64,3584]{1,0:T(8,128)S(1)} %convolution_multiply_fusion, bf16[32,3584]{1,0:T(8,128)(2,1)} %collective-permute-done.2, f32[16,3584]{1,0:T(8,128)} %fusion.35, pred[32]{0:T(512)(128)(4,1)S(1)} %broadcast_in_dim.76), kind=kLoop, calls=%fused_computation.50 | loop fusion | flops 573440 | bytes 1146912 | tf_op jit(solution)/shard_map/convert_element_type | solution.py:61
  90.2 1.0 reshape.140
  91.2 12.0 %all_to_all.33 = bf16[8,4,3584]{2,1,0:T(4,128)(2,1)S(1)} all-to-all(bf16[8,4,3584]{2,1,0:T(4,128)(2,1)S(1)} %reshape.140), channel_id=1, replica_groups=mesh['groups'=2,'epx'=2,'core'=2,'tp'=4] {'epx','tp'}, dimensions={0} | all-to-all | bytes 458752 | tf_op jit(solution)/shard_map/all_to_all | solution.py:55
  103.1 0.1 convert_reduce_fusion
  103.2 1.5 %fusion.69 = bf16[1,4,3584]{2,1,0:T(4,128)(2,1)} fusion(bf16[1,4,3584]{2,1,0:T(4,128)(2,1)S(1)} %copy-done.4, f32[4,3584]{1,0:T(4,128)S(1)} %convert_reduce_fusion, f32[4,3584]{1,0:T(4,128)} %copy-done.3), kind=kLoop, calls=%fused_computation.66 | loop fusion | flops 57344 | bytes 172032 | tf_op jit(solution)/shard_map/convert_element_type | solution.py:152
  (14 shorter events, 0.2 us)
Async XLA Ops:
  0.0 1.7 %copy-start = (bf16[1,2048,576]{1,2,0:T(8,128)(2,1)S(1)}, bf16[1,2048,576]{1,2,0:T(8,128)(2,1)}, u32[]{:S(2)}) copy-start(bf16[1,2048,576]{1,2,0:T(8,128)(2,1)} %param.16) | copy-start | bytes 7077892
  0.0 4.8 %copy-start.1 = (bf16[1,4,128,576]{2,3,1,0:T(8,128)(2,1)S(1)}, bf16[1,4,128,576]{2,3,1,0:T(8,128)(2,1)}, u32[]{:S(2)}) copy-start(bf16[1,4,128,576]{2,3,1,0:T(8,128)(2,1)} %param.15) | copy-start | bytes 1769476
  0.0 4.8 %copy-start.5 = (bf16[1,4,576]{2,1,0:T(4,128)(2,1)S(1)}, bf16[1,4,576]{2,1,0:T(4,128)(2,1)}, u32[]{:S(2)}) copy-start(bf16[1,4,576]{2,1,0:T(4,128)(2,1)} %param.17) | copy-start | bytes 13828
  9.4 22.9 %all-to-all-start = ((bf16[1,4,128,512]{3,1,0,2:T(4,128)(2,1)}), bf16[1,4,128,512]{3,1,0,2:T(4,128)(2,1)S(1)}, u32[]{:S(2)}, u32[]{:S(2)}) async-start(bf16[1,4,128,512]{3,1,0,2:T(4,128)(2,1)} %copy.29), calls=%async_computation | async-start | bytes 1048576 | tf_op jit(solution)/shard_map/all_to_all | solution.py:92
  38.4 9.8 %copy-start.6 = (bf16[3584]{0:T(1024)(128)(2,1)S(1)}, bf16[3584]{0:T(1024)(128)(2,1)}, u32[]{:S(2)}) copy-start(bf16[3584]{0:T(1024)(128)(2,1)} %param.22) | copy-start | bytes 21508
  38.4 19.5 %copy-start.4 = (bf16[1,4,3584]{2,1,0:T(4,128)(2,1)S(1)}, bf16[1,4,3584]{2,1,0:T(4,128)(2,1)}, u32[]{:S(2)}) copy-start(bf16[1,4,3584]{2,1,0:T(4,128)(2,1)} %param.14) | copy-start | bytes 86020
  38.4 20.2 %copy-start.7 = (bf16[3584,4]{0,1:T(4,128)(2,1)S(1)}, bf16[3584,4]{0,1:T(4,128)(2,1)}, u32[]{:S(2)}) copy-start(bf16[3584,4]{0,1:T(4,128)(2,1)} %param.23) | copy-start | bytes 86020
  42.5 1.6 %collective-permute-start = (bf16[32,3584]{1,0:T(8,128)(2,1)S(1)}, bf16[32,3584]{1,0:T(8,128)(2,1)S(1)}, u32[]{:S(2)}, u32[]{:S(2)}) collective-permute-start(bf16[32,3584]{1,0:T(8,128)(2,1)S(1)} %bitcast.105), channel_id=1, source_target_pairs={{0,4},{4,0},{1,5},{5,1},{2,6},{6,2},{3,7},{7,3},{8,12},{12,8},{9,1... | collective-permute-start | bytes 688136 | tf_op jit(solution)/shard_map/ppermute | solution.py:51
  44.8 13.0 %all-to-all-start.1 = ((bf16[8,4,3584]{2,1,0:T(4,128)(2,1)}), bf16[8,4,3584]{2,1,0:T(4,128)(2,1)S(1)}, u32[]{:S(2)}, u32[]{:S(2)}) async-start(bf16[8,4,3584]{2,1,0:T(4,128)(2,1)} %reshape.138), calls=%async_computation.1 | async-start | bytes 458752 | tf_op jit(solution)/shard_map/all_to_all | solution.py:55
  57.9 0.6 copy-start.3
  59.8 12.0 %all-to-all-start.2 = ((bf16[8,4,3712]{2,1,0:T(4,128)(2,1)}), bf16[8,4,3712]{2,1,0:T(4,128)(2,1)S(1)}, u32[]{:S(2)}, u32[]{:S(2)}) async-start(bf16[8,4,3712]{2,1,0:T(4,128)(2,1)} %broadcast_in_dim.74), calls=%async_computation.2 | async-start | bytes 475136 | tf_op jit(solution)/shard_map/all_to_all | solution.py:55
  71.9 2.5 %collective-permute-start.1 = (bf16[32,3712]{1,0:T(8,128)(2,1)S(1)}, bf16[32,3712]{1,0:T(8,128)(2,1)S(1)}, u32[]{:S(2)}, u32[]{:S(2)}) collective-permute-start(bf16[32,3712]{1,0:T(8,128)(2,1)S(1)} %reshape.139), channel_id=1, source_target_pairs={{0,4},{4,0},{1,5},{5,1},{2,6},{6,2},{3,7},{7,3},{8,12},{12,8},{9,1... | collective-permute-start | bytes 712712 | tf_op jit(solution)/shard_map/ppermute | solution.py:51
  74.4 3.7 %copy-start.2 = (bf16[64,3712]{1,0:T(8,128)(2,1)}, bf16[64,3712]{1,0:T(8,128)(2,1)S(1)}, u32[]{:S(2)}) copy-start(bf16[64,3712]{1,0:T(8,128)(2,1)S(1)} %constant_dynamic-update-slice_fusion) | copy-start | bytes 1425412
  83.9 4.4 %collective-permute-start.2 = (bf16[32,3584]{1,0:T(8,128)(2,1)}, bf16[32,3584]{1,0:T(8,128)(2,1)}, u32[]{:S(2)}, u32[]{:S(2)}) collective-permute-start(bf16[32,3584]{1,0:T(8,128)(2,1)} %slice.98), channel_id=1, source_target_pairs={{0,4},{4,0},{1,5},{5,1},{2,6},{6,2},{3,7},{7,3},{8,12},{12,8},{9,1... | collective-permute-start | bytes 688136 | tf_op jit(solution)/shard_map/ppermute | solution.py:51

commit v2 on v1

--- a/solution.py
+++ b/solution.py
@@ -1,6 +1,10 @@
+import functools
+
 import jax
 import jax.numpy as jnp
 from jax import lax
+from jax.experimental import pallas as pl
+from jax.experimental.pallas import tpu as pltpu
 from jax.sharding import Mesh
 from jax.sharding import PartitionSpec as P
 
@@ -8,11 +12,344 @@
 
 
 score_scale = 192.0 ** (-0.5)
+log2_e = 1.4426950408889634
 route_scale = 2.5
 norm_eps = 1e-06
 
 CHIPS = ("epx", "tp")
 ALL = ("epx", "core", "tp")
+VMEM = pl.BlockSpec(memory_space=pltpu.VMEM)
+SMEM = pl.BlockSpec(memory_space=pltpu.SMEM)
+ANY = pl.BlockSpec(memory_space=pl.ANY)
+
+
+def params(mib):
+    return pltpu.CompilerParams(vmem_limit_bytes=mib << 20)
+
+
+def attend_kernel(
+    length_ref, q_hbm, kv_hbm, new_ref, out_ref,
+    q_t, q_rows, kv_t, new_rows, scores, recent, weights, row_max, sems, *, chunk, block,
+):
+    steps, width, heads = q_t.shape
+    positions = kv_t.shape[1]
+    rows = steps * heads
+    q_copy = pltpu.make_async_copy(q_hbm, q_t, sems.at[0])
+    q_copy.start()
+    copies = []
+    for c in range(positions // chunk):
+        span = pl.ds(c * chunk, chunk)
+        copies.append(
+            pltpu.make_async_copy(kv_hbm.at[:, span], kv_t.at[:, span], sems.at[1 + c])
+        )
+        copies[-1].start()
+    new_rows[...] = jnp.zeros_like(new_rows)
+    new_rows[0:steps, :] = new_ref[...]
+    q_copy.wait()
+    for s in range(steps):
+        q_rows[s * heads : (s + 1) * heads, :] = q_t[s].T
+    length = length_ref[0]
+    lanes = new_rows.shape[0]
+    fresh = lax.dot_general(
+        q_rows[...], new_rows[...], (((1,), (1,)), ((), ())),
+        preferred_element_type=jnp.float32,
+    )
+    step_of = lax.broadcasted_iota(jnp.int32, (rows, lanes), 0) // heads
+    fresh = jnp.where(
+        lax.broadcasted_iota(jnp.int32, (rows, lanes), 1) <= step_of, fresh, -1e30
+    )
+    recent[...] = fresh
+    row_max[...] = fresh
+    for c in range(positions // chunk):
+        copies[c].wait()
+        live = (lax.broadcasted_iota(jnp.int32, (1, chunk), 1) + c * chunk) < length
+        for b in range(rows // block):
+            span = slice(b * block, (b + 1) * block)
+            s = jnp.dot(
+                q_rows[span, :], kv_t[:, c * chunk : (c + 1) * chunk],
+                preferred_element_type=jnp.float32,
+            )
+            s = jnp.where(live, s, -1e30)
+            scores[span, c * chunk : (c + 1) * chunk] = s
+            best = row_max[span, :]
+            for j in range(chunk // lanes):
+                best = jnp.maximum(best, s[:, j * lanes : (j + 1) * lanes])
+            row_max[span, :] = best
+    rate = score_scale * log2_e
+    per_owner = out_ref.shape[1] // steps
+    for b in range(rows // block):
+        span = slice(b * block, (b + 1) * block)
+        top = jnp.max(row_max[span, :], axis=1, keepdims=True) * rate
+        fresh = jnp.exp2(recent[span, :] * rate - top)
+        total = fresh
+        fresh = fresh.astype(jnp.bfloat16)
+        for c in range(positions // chunk):
+            e = jnp.exp2(scores[span, c * chunk : (c + 1) * chunk] * rate - top)
+            for j in range(chunk // lanes):
+                total = total + e[:, j * lanes : (j + 1) * lanes]
+            weights[span, c * chunk : (c + 1) * chunk] = e.astype(jnp.bfloat16)
+        mixed = lax.dot_general(
+            weights[span, :], kv_t[0:LAT, :], (((1,), (1,)), ((), ())),
+            preferred_element_type=jnp.float32,
+        ) + jnp.dot(fresh, new_rows[:, 0:LAT], preferred_element_type=jnp.float32)
+        mixed = mixed / jnp.sum(total, axis=1, keepdims=True)
+        for i in range(block // heads):
+            s = b * (block // heads) + i
+            part = mixed[i * heads : (i + 1) * heads, :]
+            out_ref[:, s * per_owner : (s + 1) * per_owner, :] = part.reshape(
+                heads // per_owner, per_owner, LAT
+            ).astype(jnp.bfloat16)
+
+
+def attend(queries, kv_cache, new_kv, lengths, owners):
+    _, steps, heads, width = queries.shape
+    positions = kv_cache.shape[1]
+    rows = steps * heads
+    chunk = 512
+    lanes = 128
+    block = 2 * heads
+    return pl.pallas_call(
+        functools.partial(attend_kernel, chunk=chunk, block=block),
+        out_shape=jax.ShapeDtypeStruct((owners, rows // owners, LAT), jnp.bfloat16),
+        in_specs=[SMEM, ANY, ANY, VMEM],
+        out_specs=VMEM,
+        scratch_shapes=[
+            pltpu.VMEM((steps, width, heads), jnp.bfloat16),
+            pltpu.VMEM((rows, width), jnp.bfloat16),
+            pltpu.VMEM((width, positions), jnp.bfloat16),
+            pltpu.VMEM((lanes, width), jnp.bfloat16),
+            pltpu.VMEM((rows, positions), jnp.float32),
+            pltpu.VMEM((rows, lanes), jnp.float32),
+            pltpu.VMEM((rows, positions), jnp.bfloat16),
+            pltpu.VMEM((rows, lanes), jnp.float32),
+            pltpu.SemaphoreType.DMA((1 + positions // chunk,)),
+        ],
+        compiler_params=params(24),
+        name="attend",
+    )(
+        lengths,
+        jnp.swapaxes(queries[0], 1, 2),
+        jnp.swapaxes(kv_cache[0], 0, 1),
+        new_kv[0],
+    )
+
+
+def project_kernel(
+    core_ref, latent_ref, up_ref, down_ref, kept_ref, sent_ref, latents, *, depth, strip
+):
+    sources, owned, _ = latent_ref.shape
+    heads = up_ref.shape[0]
+    steps = owned // heads
+    items = sources * steps
+    core = core_ref[0]
+    place = 0
+    for side in (core, 1 - core):
+        for column in range(sources // (2 * depth)):
+            for t in range(depth):
+                source = (column * 2 + side) * depth + t
+                block = latent_ref[source].astype(jnp.float32)
+                for j in range(LAT // 128):
+                    latents[j, place * owned : (place + 1) * owned, :] = block[
+                        :, j * 128 : (j + 1) * 128
+                    ]
+                place += 1
+    vals = []
+    for h in range(heads):
+        x = jnp.concatenate(
+            [latents[j, pl.ds(h, items, stride=heads), :] for j in range(LAT // 128)], axis=1
+        ).astype(jnp.bfloat16)
+        vals.append(
+            jnp.dot(x, up_ref[h], preferred_element_type=jnp.float32).astype(jnp.bfloat16)
+        )
+    vals = jnp.concatenate(vals, axis=1)
+    width = down_ref.shape[1]
+    half = items // 2
+    for n in range(width // strip):
+        cols = slice(n * strip, (n + 1) * strip)
+        part = jnp.dot(vals, down_ref[:, cols], preferred_element_type=jnp.float32)
+        kept_ref[:, cols] = part[:half]
+        sent_ref[:, cols] = part[half:].astype(jnp.bfloat16)
+
+
+def project(by_head, value_up, out_proj, core, depth):
+    sources, owned, _ = by_head.shape
+    heads, _, value_width = value_up.shape
+    width = out_proj.shape[2]
+    half = sources * owned // heads // 2
+    return pl.pallas_call(
+        functools.partial(project_kernel, depth=depth, strip=512),
+        out_shape=(
+            jax.ShapeDtypeStruct((half, width), jnp.float32),
+            jax.ShapeDtypeStruct((half, width), jnp.bfloat16),
+        ),
+        in_specs=[SMEM, VMEM, VMEM, VMEM],
+        out_specs=(VMEM, VMEM),
+        scratch_shapes=[pltpu.VMEM((LAT // 128, sources * owned, 128), jnp.float32)],
+        compiler_params=params(24),
+        name="project",
+    )(core, by_head, value_up, out_proj.reshape(heads * value_width, width))
+
+
+def merge_kernel(kept_ref, got_ref, out_ref):
+    chips, items, _ = out_ref.shape
+    total = kept_ref[...] + got_ref[...].astype(jnp.float32)
+    for j in range(chips):
+        out_ref[j] = total[j * items : (j + 1) * items, :].astype(jnp.bfloat16)
+
+
+def merge(kept, got, chips):
+    rows, width = kept.shape
+    return pl.pallas_call(
+        merge_kernel,
+        out_shape=jax.ShapeDtypeStruct((chips, rows // chips, width), jnp.bfloat16),
+        in_specs=[VMEM, VMEM],
+        out_specs=VMEM,
+        compiler_params=params(8),
+        name="merge",
+    )(kept, got)
+
+
+def norm_kernel(ids_ref, parts_ref, hidden_ref, gain_ref, router_ref, residual_ref, out_ref):
+    chips, items, _ = parts_ref.shape
+    width = hidden_ref.shape[1]
+    experts = router_ref.shape[0]
+    spare = out_ref.shape[2] - width
+    total = hidden_ref[...].astype(jnp.float32)
+    attention = parts_ref[0].astype(jnp.float32)
+    for j in range(1, chips):
+        attention = attention + parts_ref[j].astype(jnp.float32)
+    residual = total + attention
+    residual_ref[...] = residual
+    square = jnp.mean(residual * residual, axis=1, keepdims=True)
+    normed = (residual * lax.rsqrt(square + norm_eps) * gain_ref[...].astype(jnp.float32)).astype(
+        jnp.bfloat16
+    )
+    logits = lax.dot_general(
+        normed, router_ref[...], (((1,), (1,)), ((), ())), preferred_element_type=jnp.float32
+    )
+    affinity = 1.0 / (1.0 + jnp.exp(-logits))
+    item = lax.broadcasted_iota(jnp.int32, (items, experts), 0)
+    lane = lax.broadcasted_iota(jnp.int32, (items, experts), 1)
+    chosen = jnp.zeros((items, experts), jnp.float32)
+    for i in range(items):
+        for k in range(ids_ref.shape[1]):
+            chosen = chosen + jnp.where((item == i) & (lane == ids_ref[i, k]), 1.0, 0.0)
+    scored = chosen * affinity
+    gates = route_scale * scored / jnp.sum(scored, axis=1, keepdims=True)
+    high = gates.astype(jnp.bfloat16)
+    low = (gates - high.astype(jnp.float32)).astype(jnp.bfloat16)
+    tail = jnp.concatenate(
+        [high.astype(jnp.float32), low.astype(jnp.float32),
+         jnp.zeros((items, spare - 2 * experts), jnp.float32)], axis=1
+    ).astype(jnp.bfloat16)
+    for j in range(chips):
+        out_ref[j, :, 0:width] = normed
+        out_ref[j, :, width:] = tail
+
+
+def norm_rows(ids, parts, hidden, gain, router):
+    chips, items, width = parts.shape
+    experts = router.shape[1]
+    spare = -(-2 * experts // 128) * 128
+    return pl.pallas_call(
+        norm_kernel,
+        out_shape=(
+            jax.ShapeDtypeStruct((items, width), jnp.float32),
+            jax.ShapeDtypeStruct((chips, items, width + spare), jnp.bfloat16),
+        ),
+        in_specs=[SMEM, VMEM, VMEM, VMEM, VMEM],
+        out_specs=(VMEM, VMEM),
+        compiler_params=params(8),
+        name="norm_rows",
+    )(ids, parts, hidden, gain.reshape(1, width), router.T)
+
+
+def experts_kernel(
+    place_ref, mine_ref, other_ref, in_ref, out_w_ref, s_in_ref, s_out_ref,
+    kept_ref, sent_ref, tokens, tails, own, *, depth, experts, strip,
+):
+    chips, items, padded = mine_ref.shape
+    width = out_w_ref.shape[1]
+    half = chips * items
+    core, column = place_ref[0], place_ref[1]
+    for side, ref in enumerate((mine_ref, other_ref)):
+        for j in range(chips):
+            rows = slice(side * half + j * items, side * half + (j + 1) * items)
+            block = ref[j].astype(jnp.float32)
+            tokens[rows, :] = block[:, :width]
+            tails[rows, :] = block[:, width:]
+    x = tokens[...].astype(jnp.bfloat16)
+    here = column * 2 + core
+    lane = lax.broadcasted_iota(jnp.int32, tails.shape, 1)
+    gate = jnp.sum(
+        jnp.where((lane == here) | (lane == here + experts), tails[...], 0.0),
+        axis=1, keepdims=True,
+    )
+    g = jnp.dot(x, in_ref[0], preferred_element_type=jnp.float32)
+    u = jnp.dot(x, in_ref[1], preferred_element_type=jnp.float32)
+    act = (g / (1.0 + jnp.exp(-g)) * u).astype(jnp.bfloat16)
+    start = pl.multiple_of(column * (depth * items), depth * items)
+    xs = tokens[pl.ds(start, depth * items), :].astype(jnp.bfloat16)
+    sg = jnp.dot(xs, s_in_ref[0], preferred_element_type=jnp.float32)
+    su = jnp.dot(xs, s_in_ref[1], preferred_element_type=jnp.float32)
+    s_act = (sg / (1.0 + jnp.exp(-sg)) * su).astype(jnp.bfloat16)
+    for n in range(width // strip):
+        cols = slice(n * strip, (n + 1) * strip)
+        y = gate * jnp.dot(act, out_w_ref[:, cols], preferred_element_type=jnp.float32)
+        ys = jnp.dot(s_act, s_out_ref[:, cols], preferred_element_type=jnp.float32)
+        sent_ref[:, cols] = y[half:].astype(jnp.bfloat16)
+        kept_ref[:, cols] = y[:half]
+        kept_ref[pl.ds(start, depth * items), cols] = (
+            kept_ref[pl.ds(start, depth * items), cols] + ys
+        )
+
+
+def run_experts(mine, other, expert_in, expert_out, shared_in, shared_out, place, depth, experts):
+    chips, items, padded = mine.shape
+    width = expert_out.shape[2]
+    half = chips * items
+    return pl.pallas_call(
+        functools.partial(experts_kernel, depth=depth, experts=experts, strip=512),
+        out_shape=(
+            jax.ShapeDtypeStruct((half, width), jnp.float32),
+            jax.ShapeDtypeStruct((half, width), jnp.bfloat16),
+        ),
+        in_specs=[SMEM] + [VMEM] * 6,
+        out_specs=(VMEM, VMEM),
+        scratch_shapes=[
+            pltpu.VMEM((2 * half, width), jnp.float32),
+            pltpu.VMEM((2 * half, padded - width), jnp.float32),
+            pltpu.VMEM((depth * items, width), jnp.bfloat16),
+        ],
+        compiler_params=params(32),
+        name="experts",
+    )(place, mine, other, expert_in[0], expert_out[0], shared_in, shared_out)
+
+
+def finish_kernel(parts_ref, residual_ref, out_ref):
+    total = residual_ref[...]
+    for j in range(parts_ref.shape[0]):
+        total = total + parts_ref[j].astype(jnp.float32)
+    out_ref[...] = total.astype(jnp.bfloat16)
+
+
+def finish(parts, residual):
+    return pl.pallas_call(
+        finish_kernel,
+        out_shape=jax.ShapeDtypeStruct(residual.shape, jnp.bfloat16),
+        in_specs=[VMEM, VMEM],
+        out_specs=VMEM,
+        compiler_params=params(8),
+        name="finish",
+    )(parts, residual)
+
+
+def swap_cores(x):
+    return lax.ppermute(x, "core", [(0, 1), (1, 0)])
+
+
+def chip_exchange(x):
+    return lax.all_to_all(x, CHIPS, split_axis=0, concat_axis=0, tiled=True)
 
 
 def attend_block(queries, kv_cache, new_kv, lengths):
@@ -47,14 +384,6 @@
     return combined[..., :LAT].astype(jnp.bfloat16)
 
 
-def swap_cores(x):
-    return lax.ppermute(x, "core", [(0, 1), (1, 0)])
-
-
-def chip_exchange(x):
-    return lax.all_to_all(x, CHIPS, split_axis=0, concat_axis=0, tiled=True)
-
-
 def sum_at_rows(kept, sent, chips):
     half = kept + swap_cores(sent.astype(jnp.bfloat16)).astype(jnp.float32)
     width = half.shape[1]
@@ -62,7 +391,7 @@
     return jnp.sum(parts.astype(jnp.float32), axis=0)
 
 
-def on_device(
+def plain_device(
     hidden_in,
     queries,
     kv_cache,
@@ -153,6 +482,59 @@
     return layer_out.reshape(rows_here, steps_here, model_width)
 
 
+def on_device(
+    hidden_in,
+    queries,
+    kv_cache,
+    new_kv,
+    lengths,
+    expert_ids,
+    value_up,
+    out_proj,
+    norm_gain,
+    router,
+    expert_in,
+    expert_out,
+    shared_in,
+    shared_out,
+):
+    rows_here, steps_here, model_width = hidden_in.shape
+    items = rows_here * steps_here
+    columns = lax.axis_size("epx")
+    depth = lax.axis_size("tp")
+    chips = columns * depth
+    owners = 2 * chips
+    core = lax.axis_index("core").astype(jnp.int32)
+    column = lax.axis_index("epx").astype(jnp.int32)
+    place = lax.axis_index("tp")
+    experts = router.shape[1]
+
+    latent_out = attend(queries, kv_cache, new_kv, lengths, owners)
+    by_head = lax.all_to_all(latent_out, ALL, split_axis=0, concat_axis=0, tiled=True)
+    kept, sent = project(by_head, value_up, out_proj, core.reshape(1), depth)
+    parts = chip_exchange(merge(kept, swap_cores(sent), chips))
+    ids = lax.dynamic_slice_in_dim(expert_ids, place * rows_here, rows_here, 0).reshape(
+        items, expert_ids.shape[2]
+    )
+    residual, handed = norm_rows(
+        ids, parts, hidden_in.reshape(items, model_width), norm_gain, router
+    )
+    mine = chip_exchange(handed)
+    kept, sent = run_experts(
+        mine, swap_cores(mine), expert_in, expert_out, shared_in, shared_out,
+        jnp.stack([core, column]), depth, experts,
+    )
+    parts = chip_exchange(merge(kept, swap_cores(sent), chips))
+    return finish(parts, residual).reshape(rows_here, steps_here, model_width)
+
+
+def choose(*args):
+    owners = 2 * lax.axis_size("epx") * lax.axis_size("tp")
+    queries = args[1]
+    whole_tiles = queries.shape[0] == 1 and queries.shape[2] % (8 * owners) == 0
+    return on_device(*args) if whole_tiles else plain_device(*args)
+
+
 def solution(mesh):
     sizes = mesh.shape
     fine = Mesh(
@@ -179,5 +561,5 @@
     )
     out_specs = P(rows, None, None)
     return jax.shard_map(
-        on_device, mesh=fine, in_specs=in_specs, out_specs=out_specs, check_vma=False
-    )
+        choose, mesh=fine, in_specs=in_specs, out_specs=out_specs, check_vma=False
+    )

time: 106 us -> 92.7 us (0.87)
  matrix products: 26.6 us -> 0 us
  Pallas kernels: 0 us -> 13.7 us
  blocking collectives: 12 us -> 23.4 us
  other arithmetic: 5.18 us -> 0.07 us
  waiting for transfers between devices: 33.1 us -> 29.2 us
  starting transfers between devices: 14.8 us -> 11.1 us
  local copies, waits for them, and re-layouts: 12 us -> 13.8 us
    dot_general x10 -> x0, matrix products: 26.6 us -> none  [the longest x1 6.05 us: on_device(): jnp.einsum('rshv,hvd->rsd', head_vals, out_proj, preferred_element_type=j...]
    pallas_call x0 -> x7, Pallas kernels: none -> 13.7 us  [the longest x1 6.16 us: attend(): pl.pallas_call(functools.partial(attend_kernel, chunk=chunk, block=block)...]
    unnamed x17 -> x26, local copies, waits for them, and re-layouts: 1.36 us -> 13.7 us
    all_to_all x1 -> x2, blocking collectives: 12 us -> 23.4 us  [chip_exchange(): return lax.all_to_all(x, CHIPS, split_axis=0, concat_axis=0, tiled=True)]
    all_to_all x2 -> x1, waiting for transfers between devices: 17.1 us -> 9.44 us  [chip_exchange(): return lax.all_to_all(x, CHIPS, split_axis=0, concat_axis=0, tiled=True)]
    ppermute x3, waiting for transfers between devices: 0.42 us -> 4.25 us  [swap_cores(): return lax.ppermute(x, 'core', [(0, 1), (1, 0)])]
    convert_element_type x7 -> x0, other arithmetic: 3.56 us -> none  [the longest x2 1.93 us: sum_at_rows(): parts = chip_exchange(half.astype(jnp.bfloat16).reshape(chips, -1, width))]
    all_to_all x2 -> x1, starting transfers between devices: 6.8 us -> 3.4 us  [chip_exchange(): return lax.all_to_all(x, CHIPS, split_axis=0, concat_axis=0, tiled=True)]
  transfers between devices with their start and end apart: 6 -> 5, of which waited for: 4 -> 5; matrix products, arithmetic and copies ran while one was open for 8% -> 0% of each run, Pallas kernels for 0% -> 0%
where the time goes in v2:
time: 92.7 us; the launch traced here: 92 us
  waiting for transfers between devices  29.2 us (31%)
  blocking collectives  23.4 us (25%)
  local copies, waits for them, and re-layouts  13.8 us (15%)
  Pallas kernels  13.7 us (15%)
  starting transfers between devices  11.1 us (12%)
    all_to_all x2, blocking collectives, chip_exchange(): return lax.all_to_all(x, CHIPS, split_axis=0, concat_axis=0, tiled=True)  23.4 us
    all_to_all x1, waiting for transfers between devices, on_device(): lax.all_to_all(latent_out, ALL, split_axis=0, concat_axis=0, tiled=True)  15.6 us
    unnamed x26, local copies, waits for them, and re-layouts  13.7 us
    all_to_all x1, waiting for transfers between devices, chip_exchange(): return lax.all_to_all(x, CHIPS, split_axis=0, concat_axis=0, tiled=True)  9.44 us
    all_to_all x1, starting transfers between devices, on_device(): lax.all_to_all(latent_out, ALL, split_axis=0, concat_axis=0, tiled=True)  7.4 us
    pallas_call x1, Pallas kernels, attend(): pl.pallas_call(functools.partial(attend_kernel, chunk=chunk, block=block)...  6.16 us
    ppermute x3, waiting for transfers between devices, swap_cores(): return lax.ppermute(x, 'core', [(0, 1), (1, 0)])  4.25 us
    all_to_all x1, starting transfers between devices, chip_exchange(): return lax.all_to_all(x, CHIPS, split_axis=0, concat_axis=0, tiled=True)  3.4 us
  transfers between devices with their start and end apart: 5, of which 5 were waited for; matrix products, arithmetic and copies ran while one was open for 0% of the time, Pallas kernels for 0%

profile of v2, /device:TPU:0, one launch (start us, length us, event | category | flops | bytes accessed | tf_op | source)
XLA Modules:
  0.0 92.0 jit_solution(12688577809674703272)
XLA Ops:
  0.0 0.0 copy-start
  0.7 0.0 copy-start.5
  0.7 1.7 %copy-done.5 = bf16[1,2048,576]{1,2,0:T(8,128)(2,1)S(1)} copy-done((bf16[1,2048,576]{1,2,0:T(8,128)(2,1)S(1)}, bf16[1,2048,576]{1,2,0:T(8,128)(2,1)}, u32[]{:S(2)}) %copy-start.5) | copy-done | bytes 2359320
  2.3 0.0 copy-start.8
  2.3 1.1 %copy-done.8 = bf16[1,4,128,576]{2,3,1,0:T(8,128)(2,1)S(1)} copy-done((bf16[1,4,128,576]{2,3,1,0:T(8,128)(2,1)S(1)}, bf16[1,4,128,576]{2,3,1,0:T(8,128)(2,1)}, u32[]{:S(2)}) %copy-start.8) | copy-done | bytes 589848
  3.4 0.0 copy-start.11
  3.4 0.7 copy-done.11
  4.1 0.0 copy-start.7
  4.1 6.2 %attend.1 = bf16[16,32,512]{2,1,0:T(8,128)(2,1)} custom-call(s32[1]{0:T(128)S(6)} %copy.16.length_ref, bf16[4,576,128]{2,1,0:T(8,128)(2,1)S(1)} %bitcast.21, bf16[576,2048]{1,0:T(8,128)(2,1)S(1)} %bitcast.20, bf16[4,576]{1,0:T(4,128)(2,1)S(1)} %bitcast.24), custom_call_target="tpu_custom_call" | custom-call | tf_op jit(solution)/shard_map/attend/pallas_call | solution.py:111
  10.3 7.4 %all-to-all-start = ((bf16[16,32,512]{2,1,0:T(8,128)(2,1)}), bf16[16,32,512]{2,1,0:T(8,128)(2,1)S(1)}, u32[]{:S(2)}, u32[]{:S(2)}) async-start(bf16[16,32,512]{2,1,0:T(8,128)(2,1)} %attend.1), calls=%async_computation | async-start | bytes 1048576 | tf_op jit(solution)/shard_map/all_to_all | solution.py:513
  17.7 15.6 %all-to-all-done.latent_ref = bf16[16,32,512]{2,1,0:T(8,128)(2,1)S(1)} async-done(((bf16[16,32,512]{2,1,0:T(8,128)(2,1)}), bf16[16,32,512]{2,1,0:T(8,128)(2,1)S(1)}, u32[]{:S(2)}, u32[]{:S(2)}) %all-to-all-start) | async-done | bytes 524320 | tf_op jit(solution)/shard_map/all_to_all | solution.py:513
  33.2 0.0 copy-done.7
  33.2 0.0 copy-start.1
  33.2 3.1 %copy-done.1 = bf16[8,128,3584]{2,1,0:T(8,128)(2,1)S(1)} copy-done((bf16[8,128,3584]{2,1,0:T(8,128)(2,1)S(1)}, bf16[8,128,3584]{2,1,0:T(8,128)(2,1)}, u32[]{:S(2)}) %copy-start.1) | copy-done | bytes 7340056
  36.3 0.0 copy-start.12
  36.3 0.0 copy-start.9
  36.3 0.0 copy-start.10
  36.3 0.0 copy-start.6
  36.3 1.7 %project.1 = (f32[32,3584]{1,0:T(8,128)S(1)}, bf16[32,3584]{1,0:T(8,128)(2,1)S(1)}) custom-call(s32[1]{0:T(128)} %bitcast.core_ref, bf16[16,32,512]{2,1,0:T(8,128)(2,1)S(1)} %all-to-all-done.latent_ref, bf16[8,512,128]{2,1,0:T(8,128)(2,1)S(1)} %copy-done.7, bf16[1024,3584]{1,0:T(8,128)(2,1)S(1)} %bitcast.17), custom_call_target="tpu_custom_call" | custom-call | tf_op jit(solution)/shard_map/project/pallas_call | solution.py:179
  38.0 0.1 collective-permute-start
  38.1 1.5 %collective-permute-done.got_ref = bf16[32,3584]{1,0:T(8,128)(2,1)S(1)} collective-permute-done((bf16[32,3584]{1,0:T(8,128)(2,1)S(1)}, bf16[32,3584]{1,0:T(8,128)(2,1)S(1)}, u32[]{:S(2)}, u32[]{:S(2)}) %collective-permute-start) | collective-permute-done | bytes 229408 | tf_op jit(solution)/shard_map/ppermute | solution.py:348
  39.6 0.8 merge.2
  40.3 3.4 %all-to-all-start.1 = ((bf16[8,4,3584]{2,1,0:T(4,128)(2,1)}), bf16[8,4,3584]{2,1,0:T(4,128)(2,1)S(1)}, u32[]{:S(2)}, u32[]{:S(2)}) async-start(bf16[8,4,3584]{2,1,0:T(4,128)(2,1)} %merge.2), calls=%async_computation.1 | async-start | bytes 458752 | tf_op jit(solution)/shard_map/all_to_all | solution.py:352
  43.8 0.0 copy-done
  43.8 0.1 copy.15.ids_ref
  43.9 0.0 copy-done.12
  43.9 9.4 %all-to-all-done.1.parts_ref = bf16[8,4,3584]{2,1,0:T(4,128)(2,1)S(1)} async-done(((bf16[8,4,3584]{2,1,0:T(4,128)(2,1)}), bf16[8,4,3584]{2,1,0:T(4,128)(2,1)S(1)}, u32[]{:S(2)}, u32[]{:S(2)}) %all-to-all-start.1) | async-done | bytes 229408 | tf_op jit(solution)/shard_map/all_to_all | solution.py:352
  53.3 0.0 copy-done.9
  53.3 0.0 copy-done.10
  53.3 1.0 %norm_rows.1 = (f32[4,3584]{1,0:T(4,128)S(1)}, bf16[8,4,3712]{2,1,0:T(4,128)(2,1)S(1)}) custom-call(s32[4,2]{1,0:T(4,128)S(1)} %copy.15.ids_ref, bf16[8,4,3584]{2,1,0:T(4,128)(2,1)S(1)} %all-to-all-done.1.parts_ref, bf16[4,3584]{1,0:T(4,128)(2,1)S(1)} %bitcast.22, bf16[1,3584]{1,0:T(2,128)(2,1)S(1)} %reshape.19.gain_ref, bf16[4,3584]{1,0:T(4,128)(2,1)S(1)} %bitcast.23), custom_call_target="tpu_custom_call" | custom-call | tf_op jit(solution)/shard_map/norm_rows/pallas_call | solution.py:254
  54.4 11.3 %all_to_all.20.mine_ref = bf16[8,4,3712]{2,1,0:T(4,128)(2,1)S(1)} all-to-all(bf16[8,4,3712]{2,1,0:T(4,128)(2,1)S(1)} %get-tuple-element.13), channel_id=1, replica_groups=mesh['groups'=2,'epx'=2,'core'=2,'tp'=4] {'epx','tp'}, dimensions={0} | all-to-all | bytes 475136 | tf_op jit(solution)/shard_map/all_to_all | solution.py:352
  65.7 0.0 collective-permute-start.1
  65.7 0.1 pad_add_fusion.place_ref
  65.8 1.4 %collective-permute-done.1.other_ref = bf16[8,4,3712]{2,1,0:T(4,128)(2,1)S(1)} collective-permute-done((bf16[8,4,3712]{2,1,0:T(4,128)(2,1)S(1)}, bf16[8,4,3712]{2,1,0:T(4,128)(2,1)S(1)}, u32[]{:S(2)}, u32[]{:S(2)}) %collective-permute-start.1) | collective-permute-done | bytes 237600 | tf_op jit(solution)/shard_map/ppermute | solution.py:348
  67.2 0.0 copy-done.6
  67.2 0.0 copy-start.2
  67.2 3.1 %copy-done.2 = bf16[1,2,3584,512]{3,2,1,0:T(8,128)(2,1)S(1)} copy-done((bf16[1,2,3584,512]{3,2,1,0:T(8,128)(2,1)S(1)}, bf16[1,2,3584,512]{3,2,1,0:T(8,128)(2,1)}, u32[]{:S(2)}) %copy-start.2) | copy-done | bytes 7340056
  70.3 0.0 copy-start.3
  70.3 2.0 %copy-done.3 = bf16[1,512,3584]{2,1,0:T(8,128)(2,1)S(1)} copy-done((bf16[1,512,3584]{2,1,0:T(8,128)(2,1)S(1)}, bf16[1,512,3584]{2,1,0:T(8,128)(2,1)}, u32[]{:S(2)}) %copy-start.3) | copy-done | bytes 3670040
  72.3 0.0 copy-start.4
  72.3 2.0 %copy-done.4 = bf16[2,3584,256]{2,1,0:T(8,128)(2,1)S(1)} copy-done((bf16[2,3584,256]{2,1,0:T(8,128)(2,1)S(1)}, bf16[2,3584,256]{2,1,0:T(8,128)(2,1)}, u32[]{:S(2)}) %copy-start.4) | copy-done | bytes 3670040
  74.4 3.3 %experts.1 = (f32[32,3584]{1,0:T(8,128)S(1)}, bf16[32,3584]{1,0:T(8,128)(2,1)S(1)}) custom-call(s32[2]{0:T(128)S(1)} %pad_add_fusion.place_ref, bf16[8,4,3712]{2,1,0:T(4,128)(2,1)S(1)} %all_to_all.20.mine_ref, bf16[8,4,3712]{2,1,0:T(4,128)(2,1)S(1)} %collective-permute-done.1.other_ref, bf16[2,3584,512]{2,1,0:T(8,128)(2,1)S(1)} %bitcast.18, ...), custom_call_target="tpu_custom_call" | custom-call | tf_op jit(solution)/shard_map/experts/pallas_call | solution.py:311
  77.7 0.2 collective-permute-start.2
  77.9 1.3 %collective-permute-done.2.got_ref = bf16[32,3584]{1,0:T(8,128)(2,1)S(1)} collective-permute-done((bf16[32,3584]{1,0:T(8,128)(2,1)S(1)}, bf16[32,3584]{1,0:T(8,128)(2,1)S(1)}, u32[]{:S(2)}, u32[]{:S(2)}) %collective-permute-start.2) | collective-permute-done | bytes 229408 | tf_op jit(solution)/shard_map/ppermute | solution.py:348
  79.2 0.1 merge.3
  79.3 12.1 %all_to_all.21.parts_ref = bf16[8,4,3584]{2,1,0:T(4,128)(2,1)S(1)} all-to-all(bf16[8,4,3584]{2,1,0:T(4,128)(2,1)S(1)} %merge.3), channel_id=1, replica_groups=mesh['groups'=2,'epx'=2,'core'=2,'tp'=4] {'epx','tp'}, dimensions={0} | all-to-all | bytes 458752 | tf_op jit(solution)/shard_map/all_to_all | solution.py:352
  91.4 0.7 finish.1
  (2 shorter events, 0.0 us)
Async XLA Ops:
  0.0 43.8 %copy-start = (s32[4,4,2]{1,2,0:T(2,128)S(1)}, s32[4,4,2]{1,2,0:T(2,128)}, u32[]{:S(2)}) copy-start(s32[4,4,2]{1,2,0:T(2,128)} %param.19) | copy-start | bytes 388
  0.7 1.7 %copy-start.5 = (bf16[1,2048,576]{1,2,0:T(8,128)(2,1)S(1)}, bf16[1,2048,576]{1,2,0:T(8,128)(2,1)}, u32[]{:S(2)}) copy-start(bf16[1,2048,576]{1,2,0:T(8,128)(2,1)} %param.16) | copy-start | bytes 7077892
  2.3 1.1 %copy-start.8 = (bf16[1,4,128,576]{2,3,1,0:T(8,128)(2,1)S(1)}, bf16[1,4,128,576]{2,3,1,0:T(8,128)(2,1)}, u32[]{:S(2)}) copy-start(bf16[1,4,128,576]{2,3,1,0:T(8,128)(2,1)} %param.15) | copy-start | bytes 1769476
  3.4 0.7 copy-start.11
  4.1 29.1 %copy-start.7 = (bf16[8,512,128]{2,1,0:T(8,128)(2,1)S(1)}, bf16[8,512,128]{2,1,0:T(8,128)(2,1)}, u32[]{:S(2)}) copy-start(bf16[8,512,128]{2,1,0:T(8,128)(2,1)} %up_ref.1) | copy-start | bytes 3145732
  10.3 23.0 %all-to-all-start = ((bf16[16,32,512]{2,1,0:T(8,128)(2,1)}), bf16[16,32,512]{2,1,0:T(8,128)(2,1)S(1)}, u32[]{:S(2)}, u32[]{:S(2)}) async-start(bf16[16,32,512]{2,1,0:T(8,128)(2,1)} %attend.1), calls=%async_computation | async-start | bytes 1048576 | tf_op jit(solution)/shard_map/all_to_all | solution.py:513
  33.2 3.1 %copy-start.1 = (bf16[8,128,3584]{2,1,0:T(8,128)(2,1)S(1)}, bf16[8,128,3584]{2,1,0:T(8,128)(2,1)}, u32[]{:S(2)}) copy-start(bf16[8,128,3584]{2,1,0:T(8,128)(2,1)} %param.21) | copy-start | bytes 22020100
  36.3 7.6 %copy-start.12 = (bf16[3584]{0:T(1024)(128)(2,1)S(1)}, bf16[3584]{0:T(1024)(128)(2,1)}, u32[]{:S(2)}) copy-start(bf16[3584]{0:T(1024)(128)(2,1)} %param.22) | copy-start | bytes 21508
  36.3 17.0 %copy-start.9 = (bf16[1,4,3584]{2,1,0:T(4,128)(2,1)S(1)}, bf16[1,4,3584]{2,1,0:T(4,128)(2,1)}, u32[]{:S(2)}) copy-start(bf16[1,4,3584]{2,1,0:T(4,128)(2,1)} %param.14) | copy-start | bytes 86020
  36.3 17.0 %copy-start.10 = (bf16[3584,4]{0,1:T(4,128)(2,1)S(1)}, bf16[3584,4]{0,1:T(4,128)(2,1)}, u32[]{:S(2)}) copy-start(bf16[3584,4]{0,1:T(4,128)(2,1)} %param.23) | copy-start | bytes 86020
  36.3 30.9 %copy-start.6 = (bf16[256,3584]{1,0:T(8,128)(2,1)S(1)}, bf16[256,3584]{1,0:T(8,128)(2,1)}, u32[]{:S(2)}) copy-start(bf16[256,3584]{1,0:T(8,128)(2,1)} %s_out_ref.1) | copy-start | bytes 5505028
  38.0 1.6 %collective-permute-start = (bf16[32,3584]{1,0:T(8,128)(2,1)S(1)}, bf16[32,3584]{1,0:T(8,128)(2,1)S(1)}, u32[]{:S(2)}, u32[]{:S(2)}) collective-permute-start(bf16[32,3584]{1,0:T(8,128)(2,1)S(1)} %get-tuple-element.12), channel_id=1, source_target_pairs={{0,4},{4,0},{1,5},{5,1},{2,6},{6,2},{3,7},{7,3},{8,12},{12,8},{9,1... | collective-permute-start | bytes 688136 | tf_op jit(solution)/shard_map/ppermute | solution.py:348
  40.3 13.0 %all-to-all-start.1 = ((bf16[8,4,3584]{2,1,0:T(4,128)(2,1)}), bf16[8,4,3584]{2,1,0:T(4,128)(2,1)S(1)}, u32[]{:S(2)}, u32[]{:S(2)}) async-start(bf16[8,4,3584]{2,1,0:T(4,128)(2,1)} %merge.2), calls=%async_computation.1 | async-start | bytes 458752 | tf_op jit(solution)/shard_map/all_to_all | solution.py:352
  65.7 1.5 %collective-permute-start.1 = (bf16[8,4,3712]{2,1,0:T(4,128)(2,1)S(1)}, bf16[8,4,3712]{2,1,0:T(4,128)(2,1)S(1)}, u32[]{:S(2)}, u32[]{:S(2)}) collective-permute-start(bf16[8,4,3712]{2,1,0:T(4,128)(2,1)S(1)} %all_to_all.20.mine_ref), channel_id=1, source_target_pairs={{0,4},{4,0},{1,5},{5,1},{2,6},{6,2},{3,7},{7,3},{8,12},{12,8},{9,1... | collective-permute-start | bytes 712712 | tf_op jit(solution)/shard_map/ppermute | solution.py:348
  67.2 3.1 %copy-start.2 = (bf16[1,2,3584,512]{3,2,1,0:T(8,128)(2,1)S(1)}, bf16[1,2,3584,512]{3,2,1,0:T(8,128)(2,1)}, u32[]{:S(2)}) copy-start(bf16[1,2,3584,512]{3,2,1,0:T(8,128)(2,1)} %param.24) | copy-start | bytes 22020100
  70.3 2.0 %copy-start.3 = (bf16[1,512,3584]{2,1,0:T(8,128)(2,1)S(1)}, bf16[1,512,3584]{2,1,0:T(8,128)(2,1)}, u32[]{:S(2)}) copy-start(bf16[1,512,3584]{2,1,0:T(8,128)(2,1)} %param.25) | copy-start | bytes 11010052
  72.3 2.0 %copy-start.4 = (bf16[2,3584,256]{2,1,0:T(8,128)(2,1)S(1)}, bf16[2,3584,256]{2,1,0:T(8,128)(2,1)}, u32[]{:S(2)}) copy-start(bf16[2,3584,256]{2,1,0:T(8,128)(2,1)} %s_in_ref.1) | copy-start | bytes 11010052
  77.7 1.5 %collective-permute-start.2 = (bf16[32,3584]{1,0:T(8,128)(2,1)S(1)}, bf16[32,3584]{1,0:T(8,128)(2,1)S(1)}, u32[]{:S(2)}, u32[]{:S(2)}) collective-permute-start(bf16[32,3584]{1,0:T(8,128)(2,1)S(1)} %get-tuple-element.15), channel_id=1, source_target_pairs={{0,4},{4,0},{1,5},{5,1},{2,6},{6,2},{3,7},{7,3},{8,12},{12,8},{9,1... | collective-permute-start | bytes 688136 | tf_op jit(solution)/shard_map/ppermute | solution.py:348

commit v3 on v2

--- a/solution.py
+++ b/solution.py
@@ -20,22 +20,43 @@
 ALL = ("epx", "core", "tp")
 VMEM = pl.BlockSpec(memory_space=pltpu.VMEM)
 SMEM = pl.BlockSpec(memory_space=pltpu.SMEM)
-ANY = pl.BlockSpec(memory_space=pl.ANY)
+HBM = pl.BlockSpec(memory_space=pltpu.HBM)
 
 
 def params(mib):
     return pltpu.CompilerParams(vmem_limit_bytes=mib << 20)
 
 
-def attend_kernel(
-    length_ref, q_hbm, kv_hbm, new_ref, out_ref,
-    q_t, q_rows, kv_t, new_rows, scores, recent, weights, row_max, sems, *, chunk, block,
-):
+def fetch(stored, held, sems, first):
+    copies = [
+        pltpu.make_async_copy(a, b, sems.at[first + i])
+        for i, (a, b) in enumerate(zip(stored, held))
+    ]
+    for copy in copies:
+        copy.start()
+    return copies
+
+
+def in_hbm(x):
+    return pltpu.with_memory_space_constraint(x, pltpu.HBM)
+
+
+def like(x):
+    return jax.ShapeDtypeStruct(x.shape, x.dtype)
+
+
+def attend_kernel(length_ref, q_hbm, kv_hbm, new_hbm, *refs, chunk, block, ahead):
+    stored, out_ref, held = refs[:ahead], refs[ahead], refs[ahead + 1 : 2 * ahead + 1]
+    new_ref, q_t, q_rows, kv_t, new_rows, scores, recent, weights, row_max, sems = (
+        refs[2 * ahead + 1 :]
+    )
     steps, width, heads = q_t.shape
     positions = kv_t.shape[1]
     rows = steps * heads
     q_copy = pltpu.make_async_copy(q_hbm, q_t, sems.at[0])
     q_copy.start()
+    new_copy = pltpu.make_async_copy(new_hbm, new_ref, sems.at[sems.shape[0] - 1])
+    new_copy.start()
     copies = []
     for c in range(positions // chunk):
         span = pl.ds(c * chunk, chunk)
@@ -44,6 +65,7 @@
         )
         copies[-1].start()
     new_rows[...] = jnp.zeros_like(new_rows)
+    new_copy.wait()
     new_rows[0:steps, :] = new_ref[...]
     q_copy.wait()
     for s in range(steps):
@@ -60,8 +82,11 @@
     )
     recent[...] = fresh
     row_max[...] = fresh
+    fetches = []
     for c in range(positions // chunk):
         copies[c].wait()
+        if c + 1 == positions // chunk:
+            fetches = fetch(stored, held, sems, 1 + positions // chunk)
         live = (lax.broadcasted_iota(jnp.int32, (1, chunk), 1) + c * chunk) < length
         for b in range(rows // block):
             span = slice(b * block, (b + 1) * block)
@@ -99,9 +124,11 @@
             out_ref[:, s * per_owner : (s + 1) * per_owner, :] = part.reshape(
                 heads // per_owner, per_owner, LAT
             ).astype(jnp.bfloat16)
-
-
-def attend(queries, kv_cache, new_kv, lengths, owners):
+    for copy in fetches:
+        copy.wait()
+
+
+def attend(queries, kv_cache, new_kv, lengths, owners, ahead):
     _, steps, heads, width = queries.shape
     positions = kv_cache.shape[1]
     rows = steps * heads
@@ -109,11 +136,13 @@
     lanes = 128
     block = 2 * heads
     return pl.pallas_call(
-        functools.partial(attend_kernel, chunk=chunk, block=block),
-        out_shape=jax.ShapeDtypeStruct((owners, rows // owners, LAT), jnp.bfloat16),
-        in_specs=[SMEM, ANY, ANY, VMEM],
-        out_specs=VMEM,
+        functools.partial(attend_kernel, chunk=chunk, block=block, ahead=len(ahead)),
+        out_shape=[jax.ShapeDtypeStruct((owners, rows // owners, LAT), jnp.bfloat16)]
+        + [like(x) for x in ahead],
+        in_specs=[SMEM] + [HBM] * (3 + len(ahead)),
+        out_specs=[VMEM] * (1 + len(ahead)),
         scratch_shapes=[
+            pltpu.VMEM((steps, width), jnp.bfloat16),
             pltpu.VMEM((steps, width, heads), jnp.bfloat16),
             pltpu.VMEM((rows, width), jnp.bfloat16),
             pltpu.VMEM((width, positions), jnp.bfloat16),
@@ -122,26 +151,30 @@
             pltpu.VMEM((rows, lanes), jnp.float32),
             pltpu.VMEM((rows, positions), jnp.bfloat16),
             pltpu.VMEM((rows, lanes), jnp.float32),
-            pltpu.SemaphoreType.DMA((1 + positions // chunk,)),
+            pltpu.SemaphoreType.DMA((2 + positions // chunk + len(ahead),)),
         ],
-        compiler_params=params(24),
+        compiler_params=params(16),
         name="attend",
     )(
         lengths,
-        jnp.swapaxes(queries[0], 1, 2),
-        jnp.swapaxes(kv_cache[0], 0, 1),
-        new_kv[0],
+        in_hbm(jnp.swapaxes(queries[0], 1, 2)),
+        in_hbm(jnp.swapaxes(kv_cache[0], 0, 1)),
+        in_hbm(new_kv[0]),
+        *[in_hbm(x) for x in ahead],
     )
 
 
 def project_kernel(
-    core_ref, latent_ref, up_ref, down_ref, kept_ref, sent_ref, latents, *, depth, strip
+    latent_ref, up_ref, down_ref, *refs, depth, strip, ahead
 ):
+    stored, kept_ref, sent_ref = refs[:ahead], refs[ahead], refs[ahead + 1]
+    held, latents, sems = refs[ahead + 2 : 2 * ahead + 2], refs[2 * ahead + 2], refs[2 * ahead + 3]
+    fetches = fetch(stored, held, sems, 0)
     sources, owned, _ = latent_ref.shape
     heads = up_ref.shape[0]
     steps = owned // heads
     items = sources * steps
-    core = core_ref[0]
+    core = lax.axis_index("core")
     place = 0
     for side in (core, 1 - core):
         for column in range(sources // (2 * depth)):
@@ -169,25 +202,34 @@
         part = jnp.dot(vals, down_ref[:, cols], preferred_element_type=jnp.float32)
         kept_ref[:, cols] = part[:half]
         sent_ref[:, cols] = part[half:].astype(jnp.bfloat16)
-
-
-def project(by_head, value_up, out_proj, core, depth):
+    for copy in fetches:
+        copy.wait()
+
+
+def project(by_head, value_up, out_proj, depth, ahead):
     sources, owned, _ = by_head.shape
     heads, _, value_width = value_up.shape
     width = out_proj.shape[2]
     half = sources * owned // heads // 2
     return pl.pallas_call(
-        functools.partial(project_kernel, depth=depth, strip=512),
-        out_shape=(
+        functools.partial(project_kernel, depth=depth, strip=512, ahead=len(ahead)),
+        out_shape=[
             jax.ShapeDtypeStruct((half, width), jnp.float32),
             jax.ShapeDtypeStruct((half, width), jnp.bfloat16),
-        ),
-        in_specs=[SMEM, VMEM, VMEM, VMEM],
-        out_specs=(VMEM, VMEM),
-        scratch_shapes=[pltpu.VMEM((LAT // 128, sources * owned, 128), jnp.float32)],
-        compiler_params=params(24),
+        ]
+        + [like(x) for x in ahead],
+        in_specs=[VMEM, VMEM, VMEM] + [HBM] * len(ahead),
+        out_specs=[VMEM] * (2 + len(ahead)),
+        scratch_shapes=[
+            pltpu.VMEM((LAT // 128, sources * owned, 128), jnp.float32),
+            pltpu.SemaphoreType.DMA((max(1, len(ahead)),)),
+        ],
+        compiler_params=params(8),
         name="project",
-    )(core, by_head, value_up, out_proj.reshape(heads * value_width, width))
+    )(
+        by_head, value_up, out_proj.reshape(heads * value_width, width),
+        *[in_hbm(x) for x in ahead],
+    )
 
 
 def merge_kernel(kept_ref, got_ref, out_ref):
@@ -204,7 +246,7 @@
         out_shape=jax.ShapeDtypeStruct((chips, rows // chips, width), jnp.bfloat16),
         in_specs=[VMEM, VMEM],
         out_specs=VMEM,
-        compiler_params=params(8),
+        compiler_params=params(4),
         name="merge",
     )(kept, got)
 
@@ -214,6 +256,7 @@
     width = hidden_ref.shape[1]
     experts = router_ref.shape[0]
     spare = out_ref.shape[2] - width
+    place = lax.axis_index("tp")
     total = hidden_ref[...].astype(jnp.float32)
     attention = parts_ref[0].astype(jnp.float32)
     for j in range(1, chips):
@@ -221,7 +264,7 @@
     residual = total + attention
     residual_ref[...] = residual
     square = jnp.mean(residual * residual, axis=1, keepdims=True)
-    normed = (residual * lax.rsqrt(square + norm_eps) * gain_ref[...].astype(jnp.float32)).astype(
+    normed = (residual * lax.rsqrt(square + norm_eps) * gain_ref[...].astype(jnp.float32).reshape(1, width)).astype(
         jnp.bfloat16
     )
     logits = lax.dot_general(
@@ -233,7 +276,8 @@
     chosen = jnp.zeros((items, experts), jnp.float32)
     for i in range(items):
         for k in range(ids_ref.shape[1]):
-            chosen = chosen + jnp.where((item == i) & (lane == ids_ref[i, k]), 1.0, 0.0)
+            named = ids_ref[place, k, i]
+            chosen = chosen + jnp.where((item == i) & (lane == named), 1.0, 0.0)
     scored = chosen * affinity
     gates = route_scale * scored / jnp.sum(scored, axis=1, keepdims=True)
     high = gates.astype(jnp.bfloat16)
@@ -261,17 +305,17 @@
         out_specs=(VMEM, VMEM),
         compiler_params=params(8),
         name="norm_rows",
-    )(ids, parts, hidden, gain.reshape(1, width), router.T)
+    )(ids, parts, hidden, gain, router.T)
 
 
 def experts_kernel(
-    place_ref, mine_ref, other_ref, in_ref, out_w_ref, s_in_ref, s_out_ref,
+    mine_ref, other_ref, in_ref, out_w_ref, s_in_ref, s_out_ref,
     kept_ref, sent_ref, tokens, tails, own, *, depth, experts, strip,
 ):
     chips, items, padded = mine_ref.shape
     width = out_w_ref.shape[1]
     half = chips * items
-    core, column = place_ref[0], place_ref[1]
+    core, column = lax.axis_index("core"), lax.axis_index("epx")
     for side, ref in enumerate((mine_ref, other_ref)):
         for j in range(chips):
             rows = slice(side * half + j * items, side * half + (j + 1) * items)
@@ -304,9 +348,9 @@
         )
 
 
-def run_experts(mine, other, expert_in, expert_out, shared_in, shared_out, place, depth, experts):
+def run_experts(mine, other, expert_in, expert_out, shared_in, shared_out, depth, experts):
     chips, items, padded = mine.shape
-    width = expert_out.shape[2]
+    width = expert_out.shape[1]
     half = chips * items
     return pl.pallas_call(
         functools.partial(experts_kernel, depth=depth, experts=experts, strip=512),
@@ -314,16 +358,16 @@
             jax.ShapeDtypeStruct((half, width), jnp.float32),
             jax.ShapeDtypeStruct((half, width), jnp.bfloat16),
         ),
-        in_specs=[SMEM] + [VMEM] * 6,
+        in_specs=[VMEM] * 6,
         out_specs=(VMEM, VMEM),
         scratch_shapes=[
             pltpu.VMEM((2 * half, width), jnp.float32),
             pltpu.VMEM((2 * half, padded - width), jnp.float32),
             pltpu.VMEM((depth * items, width), jnp.bfloat16),
         ],
-        compiler_params=params(32),
+        compiler_params=params(8),
         name="experts",
-    )(place, mine, other, expert_in[0], expert_out[0], shared_in, shared_out)
+    )(mine, other, expert_in, expert_out, shared_in, shared_out)
 
 
 def finish_kernel(parts_ref, residual_ref, out_ref):
@@ -504,25 +548,23 @@
     depth = lax.axis_size("tp")
     chips = columns * depth
     owners = 2 * chips
-    core = lax.axis_index("core").astype(jnp.int32)
-    column = lax.axis_index("epx").astype(jnp.int32)
-    place = lax.axis_index("tp")
     experts = router.shape[1]
 
-    latent_out = attend(queries, kv_cache, new_kv, lengths, owners)
+    latent_out, out_proj, value_up, expert_in = attend(
+        queries, kv_cache, new_kv, lengths, owners, [out_proj, value_up, expert_in[0]]
+    )
     by_head = lax.all_to_all(latent_out, ALL, split_axis=0, concat_axis=0, tiled=True)
-    kept, sent = project(by_head, value_up, out_proj, core.reshape(1), depth)
+    kept, sent, expert_out, shared_in, shared_out = project(
+        by_head, value_up, out_proj, depth, [expert_out[0], shared_in, shared_out]
+    )
     parts = chip_exchange(merge(kept, swap_cores(sent), chips))
-    ids = lax.dynamic_slice_in_dim(expert_ids, place * rows_here, rows_here, 0).reshape(
-        items, expert_ids.shape[2]
-    )
+    ids = jnp.swapaxes(expert_ids, 1, 2)
     residual, handed = norm_rows(
         ids, parts, hidden_in.reshape(items, model_width), norm_gain, router
     )
     mine = chip_exchange(handed)
     kept, sent = run_experts(
-        mine, swap_cores(mine), expert_in, expert_out, shared_in, shared_out,
-        jnp.stack([core, column]), depth, experts,
+        mine, swap_cores(mine), expert_in, expert_out, shared_in, shared_out, depth, experts,
     )
     parts = chip_exchange(merge(kept, swap_cores(sent), chips))
     return finish(parts, residual).reshape(rows_here, steps_here, model_width)

time: 92.7 us -> 81.4 us (0.88)
  blocking collectives: 23.4 us -> 58.7 us
  waiting for transfers between devices: 29.2 us -> 4.32 us
  local copies, waits for them, and re-layouts: 13.8 us -> 0.01 us
  starting transfers between devices: 11.1 us -> 0.26 us
  Pallas kernels: 13.7 us -> 17.2 us
    all_to_all x2 -> x0, waiting for transfers between devices: 25 us -> none  [the longest x1 15.6 us: on_device(): lax.all_to_all(latent_out, ALL, split_axis=0, concat_axis=0, tiled=True)]
    all_to_all x0 -> x1, blocking collectives: none -> 22.7 us  [on_device(): lax.all_to_all(latent_out, ALL, split_axis=0, concat_axis=0, tiled=True)]
    unnamed x26 -> x8, local copies, waits for them, and re-layouts: 13.7 us -> 0.01 us
    all_to_all x2 -> x3, blocking collectives: 23.4 us -> 35.9 us  [chip_exchange(): return lax.all_to_all(x, CHIPS, split_axis=0, concat_axis=0, tiled=True)]
    all_to_all x2 -> x0, starting transfers between devices: 10.8 us -> none  [the longest x1 7.4 us: on_device(): lax.all_to_all(latent_out, ALL, split_axis=0, concat_axis=0, tiled=True)]
    pallas_call x2, Pallas kernels: 7.87 us -> 12.6 us  [the longest x1 8.85 us: attend(): pl.pallas_call(functools.partial(attend_kernel, chunk=chunk, block=block,...]
  transfers between devices with their start and end apart: 5 -> 3, of which waited for: 5 -> 3; matrix products, arithmetic and copies ran while one was open for 0% -> 0% of each run, Pallas kernels for 0% -> 0%
where the time goes in v3:
time: 81.4 us; the launch traced here: 81.1 us
  blocking collectives  58.7 us (72%)
  Pallas kernels  17.2 us (21%)
  waiting for transfers between devices  4.32 us (5%)
    all_to_all x3, blocking collectives, chip_exchange(): return lax.all_to_all(x, CHIPS, split_axis=0, concat_axis=0, tiled=True)  35.9 us
    all_to_all x1, blocking collectives, on_device(): lax.all_to_all(latent_out, ALL, split_axis=0, concat_axis=0, tiled=True)  22.7 us
    pallas_call x1, Pallas kernels, attend(): pl.pallas_call(functools.partial(attend_kernel, chunk=chunk, block=block,...  8.85 us
    ppermute x3, waiting for transfers between devices, swap_cores(): return lax.ppermute(x, 'core', [(0, 1), (1, 0)])  4.32 us
    pallas_call x1, Pallas kernels, project(): pl.pallas_call(functools.partial(project_kernel, depth=depth, strip=512,...  3.73 us
    pallas_call x1, Pallas kernels, run_experts(): pl.pallas_call(functools.partial(experts_kernel, depth=depth, experts=exp...  2.76 us
  transfers between devices with their start and end apart: 3, of which 3 were waited for; matrix products, arithmetic and copies ran while one was open for 0% of the time, Pallas kernels for 0%

profile of v3, /device:TPU:0, one launch (start us, length us, event | category | flops | bytes accessed | tf_op | source)
XLA Modules:
  0.0 81.1 jit_solution(9051673773217932867)
XLA Ops:
  0.7 8.9 %attend.1 = (bf16[16,32,512]{2,1,0:T(8,128)(2,1)S(1)}, bf16[8,128,3584]{2,1,0:T(8,128)(2,1)S(1)}, bf16[8,512,128]{2,1,0:T(8,128)(2,1)S(1)}, bf16[2,3584,512]{2,1,0:T(8,128)(2,1)S(1)}) custom-call(s32[1]{0:T(128)S(6)} %copy.15.length_ref, bf16[4,576,128]{2,1,0:T(8,128)(2,1)} %bitcast.21, bf16[576,2048]{1,0:T(8,128)(2,1)} %bitcast.20, ...), custom_call_target="tpu_custom_call" | custom-call | tf_op jit(solution)/shard_map/attend/pallas_call | solution.py:138
  9.5 22.7 %all_to_all.20.latent_ref = bf16[16,32,512]{2,1,0:T(8,128)(2,1)S(1)} all-to-all(bf16[16,32,512]{2,1,0:T(8,128)(2,1)S(1)} %get-tuple-element.18), channel_id=1, replica_groups=mesh['groups'=2,'epx'=2,'core'=2,'tp'=4] {'epx','core','tp'}, dimensions={0} | all-to-all | bytes 1048576 | tf_op jit(solution)/shard_map/all_to_all | solution.py:556
  32.3 0.0 copy-start
  32.3 0.0 copy-start.1
  32.3 0.0 copy-start.2
  32.3 0.0 copy-start.3
  32.3 3.7 %project.1 = (f32[32,3584]{1,0:T(8,128)S(1)}, bf16[32,3584]{1,0:T(8,128)(2,1)S(1)}, bf16[512,3584]{1,0:T(8,128)(2,1)S(1)}, bf16[2,3584,256]{2,1,0:T(8,128)(2,1)S(1)}, bf16[256,3584]{1,0:T(8,128)(2,1)S(1)}) custom-call(bf16[16,32,512]{2,1,0:T(8,128)(2,1)S(1)} %all_to_all.20.latent_ref, bf16[8,512,128]{2,1,0:T(8,128)(2,1)S(1)} %get-tuple-element.19.up_ref, ...), custom_call_target="tpu_custom_call" | custom-call | tf_op jit(solution)/shard_map/project/pallas_call | solution.py:214
  36.0 0.1 collective-permute-start
  36.1 1.5 %collective-permute-done.got_ref = bf16[32,3584]{1,0:T(8,128)(2,1)S(1)} collective-permute-done((bf16[32,3584]{1,0:T(8,128)(2,1)S(1)}, bf16[32,3584]{1,0:T(8,128)(2,1)S(1)}, u32[]{:S(2)}, u32[]{:S(2)}) %collective-permute-start) | collective-permute-done | bytes 229408 | tf_op jit(solution)/shard_map/ppermute | solution.py:392
  37.6 0.1 merge.2
  37.6 12.5 %all_to_all.21.parts_ref = bf16[8,4,3584]{2,1,0:T(4,128)(2,1)S(1)} all-to-all(bf16[8,4,3584]{2,1,0:T(4,128)(2,1)S(1)} %merge.2), channel_id=1, replica_groups=mesh['groups'=2,'epx'=2,'core'=2,'tp'=4] {'epx','tp'}, dimensions={0} | all-to-all | bytes 458752 | tf_op jit(solution)/shard_map/all_to_all | solution.py:396
  50.1 0.0 copy-done
  50.1 0.0 copy-done.1
  50.1 0.0 copy-done.2
  50.2 0.0 copy-done.3
  50.2 1.1 %norm_rows.1 = (f32[4,3584]{1,0:T(4,128)S(1)}, bf16[8,4,3712]{2,1,0:T(4,128)(2,1)S(1)}) custom-call(s32[4,2,4]{2,1,0:T(2,128)S(1)} %bitcast.17, bf16[8,4,3584]{2,1,0:T(4,128)(2,1)S(1)} %all_to_all.21.parts_ref, bf16[4,3584]{1,0:T(4,128)(2,1)S(1)} %bitcast.15, bf16[3584]{0:T(1024)(128)(2,1)S(1)} %copy-done.2, bf16[4,3584]{1,0:T(4,128)(2,1)S(1)} %bitcast.16), custom_call_target="tpu_custom_call" | custom-call | tf_op jit(solution)/shard_map/norm_rows/pallas_call | solution.py:298
  51.2 11.3 %all_to_all.22.mine_ref = bf16[8,4,3712]{2,1,0:T(4,128)(2,1)S(1)} all-to-all(bf16[8,4,3712]{2,1,0:T(4,128)(2,1)S(1)} %get-tuple-element.23), channel_id=1, replica_groups=mesh['groups'=2,'epx'=2,'core'=2,'tp'=4] {'epx','tp'}, dimensions={0} | all-to-all | bytes 475136 | tf_op jit(solution)/shard_map/all_to_all | solution.py:396
  62.6 0.0 collective-permute-start.1
  62.6 1.5 %collective-permute-done.1.other_ref = bf16[8,4,3712]{2,1,0:T(4,128)(2,1)S(1)} collective-permute-done((bf16[8,4,3712]{2,1,0:T(4,128)(2,1)S(1)}, bf16[8,4,3712]{2,1,0:T(4,128)(2,1)S(1)}, u32[]{:S(2)}, u32[]{:S(2)}) %collective-permute-start.1) | collective-permute-done | bytes 237600 | tf_op jit(solution)/shard_map/ppermute | solution.py:392
  64.1 2.8 %experts.1 = (f32[32,3584]{1,0:T(8,128)S(1)}, bf16[32,3584]{1,0:T(8,128)(2,1)S(1)}) custom-call(bf16[8,4,3712]{2,1,0:T(4,128)(2,1)S(1)} %all_to_all.22.mine_ref, bf16[8,4,3712]{2,1,0:T(4,128)(2,1)S(1)} %collective-permute-done.1.other_ref, bf16[2,3584,512]{2,1,0:T(8,128)(2,1)S(1)} %get-tuple-element.24.in_ref, ...), custom_call_target="tpu_custom_call" | custom-call | tf_op jit(solution)/shard_map/experts/pallas_call | solution.py:355
  66.8 0.2 collective-permute-start.2
  67.0 1.3 %collective-permute-done.2.got_ref = bf16[32,3584]{1,0:T(8,128)(2,1)S(1)} collective-permute-done((bf16[32,3584]{1,0:T(8,128)(2,1)S(1)}, bf16[32,3584]{1,0:T(8,128)(2,1)S(1)}, u32[]{:S(2)}, u32[]{:S(2)}) %collective-permute-start.2) | collective-permute-done | bytes 229408 | tf_op jit(solution)/shard_map/ppermute | solution.py:392
  68.4 0.1 merge.3
  68.4 12.1 %all_to_all.23.parts_ref = bf16[8,4,3584]{2,1,0:T(4,128)(2,1)S(1)} all-to-all(bf16[8,4,3584]{2,1,0:T(4,128)(2,1)S(1)} %merge.3), channel_id=1, replica_groups=mesh['groups'=2,'epx'=2,'core'=2,'tp'=4] {'epx','tp'}, dimensions={0} | all-to-all | bytes 458752 | tf_op jit(solution)/shard_map/all_to_all | solution.py:396
  80.5 0.7 finish.1
Async XLA Ops:
  32.3 17.9 %copy-start = (bf16[1,4,3584]{2,1,0:T(4,128)(2,1)S(1)}, bf16[1,4,3584]{2,1,0:T(4,128)(2,1)}, u32[]{:S(2)}) copy-start(bf16[1,4,3584]{2,1,0:T(4,128)(2,1)} %param.14) | copy-start | bytes 86020
  32.3 17.9 %copy-start.1 = (bf16[3584,4]{0,1:T(4,128)(2,1)S(1)}, bf16[3584,4]{0,1:T(4,128)(2,1)}, u32[]{:S(2)}) copy-start(bf16[3584,4]{0,1:T(4,128)(2,1)} %param.23) | copy-start | bytes 86020
  32.3 17.9 %copy-start.2 = (bf16[3584]{0:T(1024)(128)(2,1)S(1)}, bf16[3584]{0:T(1024)(128)(2,1)}, u32[]{:S(2)}) copy-start(bf16[3584]{0:T(1024)(128)(2,1)} %gain_ref.1) | copy-start | bytes 21508
  32.3 17.9 %copy-start.3 = (s32[4,4,2]{1,2,0:T(2,128)S(1)}, s32[4,4,2]{1,2,0:T(2,128)}, u32[]{:S(2)}) copy-start(s32[4,4,2]{1,2,0:T(2,128)} %param.19) | copy-start | bytes 388
  36.0 1.6 %collective-permute-start = (bf16[32,3584]{1,0:T(8,128)(2,1)S(1)}, bf16[32,3584]{1,0:T(8,128)(2,1)S(1)}, u32[]{:S(2)}, u32[]{:S(2)}) collective-permute-start(bf16[32,3584]{1,0:T(8,128)(2,1)S(1)} %get-tuple-element.22), channel_id=1, source_target_pairs={{0,4},{4,0},{1,5},{5,1},{2,6},{6,2},{3,7},{7,3},{8,12},{12,8},{9,1... | collective-permute-start | bytes 688136 | tf_op jit(solution)/shard_map/ppermute | solution.py:392
  62.6 1.5 %collective-permute-start.1 = (bf16[8,4,3712]{2,1,0:T(4,128)(2,1)S(1)}, bf16[8,4,3712]{2,1,0:T(4,128)(2,1)S(1)}, u32[]{:S(2)}, u32[]{:S(2)}) collective-permute-start(bf16[8,4,3712]{2,1,0:T(4,128)(2,1)S(1)} %all_to_all.22.mine_ref), channel_id=1, source_target_pairs={{0,4},{4,0},{1,5},{5,1},{2,6},{6,2},{3,7},{7,3},{8,12},{12,8},{9,1... | collective-permute-start | bytes 712712 | tf_op jit(solution)/shard_map/ppermute | solution.py:392
  66.8 1.5 %collective-permute-start.2 = (bf16[32,3584]{1,0:T(8,128)(2,1)S(1)}, bf16[32,3584]{1,0:T(8,128)(2,1)S(1)}, u32[]{:S(2)}, u32[]{:S(2)}) collective-permute-start(bf16[32,3584]{1,0:T(8,128)(2,1)S(1)} %get-tuple-element.29), channel_id=1, source_target_pairs={{0,4},{4,0},{1,5},{5,1},{2,6},{6,2},{3,7},{7,3},{8,12},{12,8},{9,1... | collective-permute-start | bytes 688136 | tf_op jit(solution)/shard_map/ppermute | solution.py:392

commit v4 on v3

--- a/solution.py
+++ b/solution.py
@@ -85,7 +85,7 @@
     fetches = []
     for c in range(positions // chunk):
         copies[c].wait()
-        if c + 1 == positions // chunk:
+        if c == 0:
             fetches = fetch(stored, held, sems, 1 + positions // chunk)
         live = (lax.broadcasted_iota(jnp.int32, (1, chunk), 1) + c * chunk) < length
         for b in range(rows // block):
@@ -267,17 +267,21 @@
     normed = (residual * lax.rsqrt(square + norm_eps) * gain_ref[...].astype(jnp.float32).reshape(1, width)).astype(
         jnp.bfloat16
     )
-    logits = lax.dot_general(
-        normed, router_ref[...], (((1,), (1,)), ((), ())), preferred_element_type=jnp.float32
-    )
+    lane = lax.broadcasted_iota(jnp.int32, (items, experts), 1)
+    exact = normed.astype(jnp.float32)
+    logits = jnp.zeros((items, experts), jnp.float32)
+    for e in range(experts):
+        column = router_ref[e : e + 1, :].astype(jnp.float32)
+        logits = jnp.where(lane == e, jnp.sum(exact * column, axis=1, keepdims=True), logits)
     affinity = 1.0 / (1.0 + jnp.exp(-logits))
-    item = lax.broadcasted_iota(jnp.int32, (items, experts), 0)
-    lane = lax.broadcasted_iota(jnp.int32, (items, experts), 1)
+    ids = ids_ref[place]
+    own = lax.broadcasted_iota(jnp.int32, (items, items), 0) == lax.broadcasted_iota(
+        jnp.int32, (items, items), 1
+    )
     chosen = jnp.zeros((items, experts), jnp.float32)
-    for i in range(items):
-        for k in range(ids_ref.shape[1]):
-            named = ids_ref[place, k, i]
-            chosen = chosen + jnp.where((item == i) & (lane == named), 1.0, 0.0)
+    for k in range(ids.shape[0]):
+        named = jnp.sum(jnp.where(own, ids[k : k + 1, :], 0), axis=1, keepdims=True)
+        chosen = chosen + (lane == named).astype(jnp.float32)
     scored = chosen * affinity
     gates = route_scale * scored / jnp.sum(scored, axis=1, keepdims=True)
     high = gates.astype(jnp.bfloat16)
@@ -301,7 +305,7 @@
             jax.ShapeDtypeStruct((items, width), jnp.float32),
             jax.ShapeDtypeStruct((chips, items, width + spare), jnp.bfloat16),
         ),
-        in_specs=[SMEM, VMEM, VMEM, VMEM, VMEM],
+        in_specs=[VMEM] * 5,
         out_specs=(VMEM, VMEM),
         compiler_params=params(8),
         name="norm_rows",
@@ -550,12 +554,13 @@
     owners = 2 * chips
     experts = router.shape[1]
 
-    latent_out, out_proj, value_up, expert_in = attend(
-        queries, kv_cache, new_kv, lengths, owners, [out_proj, value_up, expert_in[0]]
-    )
+    latent_out, out_proj, value_up = attend(
+        queries, kv_cache, new_kv, lengths, owners, [out_proj, value_up]
+    )
+    expert_in, expert_out = expert_in[0], expert_out[0]
     by_head = lax.all_to_all(latent_out, ALL, split_axis=0, concat_axis=0, tiled=True)
-    kept, sent, expert_out, shared_in, shared_out = project(
-        by_head, value_up, out_proj, depth, [expert_out[0], shared_in, shared_out]
+    kept, sent = project(
+        by_head, value_up, out_proj, depth, []
     )
     parts = chip_exchange(merge(kept, swap_cores(sent), chips))
     ids = jnp.swapaxes(expert_ids, 1, 2)

time: 81.4 us -> 76.2 us (0.936)
  Pallas kernels: 17.2 us -> 11.6 us
    pallas_call x1, Pallas kernels: 8.85 us -> 5.91 us  [attend(): pl.pallas_call(functools.partial(attend_kernel, chunk=chunk, block=block,...]
    pallas_call x1, Pallas kernels: 3.73 us -> 1.72 us  [project(): pl.pallas_call(functools.partial(project_kernel, depth=depth, strip=512,...]
where the time goes in v4:
time: 76.2 us; the launch traced here: 75.9 us
  blocking collectives  58.9 us (77%)
  Pallas kernels  11.6 us (15%)
  waiting for transfers between devices  4.33 us (6%)
  between operations  0.77 us (1%)
    all_to_all x3, blocking collectives, chip_exchange(): return lax.all_to_all(x, CHIPS, split_axis=0, concat_axis=0, tiled=True)  35.9 us
    all_to_all x1, blocking collectives, on_device(): lax.all_to_all(latent_out, ALL, split_axis=0, concat_axis=0, tiled=True)  23 us
    pallas_call x1, Pallas kernels, attend(): pl.pallas_call(functools.partial(attend_kernel, chunk=chunk, block=block,...  5.91 us
    ppermute x3, waiting for transfers between devices, swap_cores(): return lax.ppermute(x, 'core', [(0, 1), (1, 0)])  4.33 us
    pallas_call x1, Pallas kernels, run_experts(): pl.pallas_call(functools.partial(experts_kernel, depth=depth, experts=exp...  2.76 us
    pallas_call x1, Pallas kernels, project(): pl.pallas_call(functools.partial(project_kernel, depth=depth, strip=512,...  1.72 us
  transfers between devices with their start and end apart: 3, of which 3 were waited for; matrix products, arithmetic and copies ran while one was open for 0% of the time, Pallas kernels for 0%

profile of v4, /device:TPU:0, one launch (start us, length us, event | category | flops | bytes accessed | tf_op | source)
XLA Modules:
  0.0 75.9 jit_solution(16511011958847667818)
XLA Ops:
  0.7 0.0 slice-start
  0.7 0.0 copy-start.2
  0.7 5.9 %attend.1 = (bf16[16,32,512]{2,1,0:T(8,128)(2,1)S(1)}, bf16[8,128,3584]{2,1,0:T(8,128)(2,1)S(1)}, bf16[8,512,128]{2,1,0:T(8,128)(2,1)S(1)}) custom-call(s32[1]{0:T(128)S(6)} %copy.15.length_ref, bf16[4,576,128]{2,1,0:T(8,128)(2,1)} %bitcast.23, bf16[576,2048]{1,0:T(8,128)(2,1)} %bitcast.22, bf16[4,576]{1,0:T(4,128)(2,1)} %bitcast.24, ...), custom_call_target="tpu_custom_call" | custom-call | tf_op jit(solution)/shard_map/attend/pallas_call | solution.py:138
  6.6 0.0 slice-start.1
  6.6 23.0 %all_to_all.20.latent_ref = bf16[16,32,512]{2,1,0:T(8,128)(2,1)S(1)} all-to-all(bf16[16,32,512]{2,1,0:T(8,128)(2,1)S(1)} %get-tuple-element.14), channel_id=1, replica_groups=mesh['groups'=2,'epx'=2,'core'=2,'tp'=4] {'epx','core','tp'}, dimensions={0} | all-to-all | bytes 1048576 | tf_op jit(solution)/shard_map/all_to_all | solution.py:561
  29.6 0.0 copy-start.3
  29.6 0.0 copy-start.4
  29.6 0.0 copy-start.5
  29.6 0.0 copy-start.6
  29.6 0.0 copy-start
  29.6 0.0 copy-start.1
  29.7 1.7 %project.1 = (f32[32,3584]{1,0:T(8,128)S(1)}, bf16[32,3584]{1,0:T(8,128)(2,1)S(1)}) custom-call(bf16[16,32,512]{2,1,0:T(8,128)(2,1)S(1)} %all_to_all.20.latent_ref, bf16[8,512,128]{2,1,0:T(8,128)(2,1)S(1)} %get-tuple-element.15.up_ref, bf16[1024,3584]{1,0:T(8,128)(2,1)S(1)} %bitcast.17), custom_call_target="tpu_custom_call" | custom-call | tf_op jit(solution)/shard_map/project/pallas_call | solution.py:214
  31.4 0.1 collective-permute-start
  31.5 1.5 %collective-permute-done.got_ref = bf16[32,3584]{1,0:T(8,128)(2,1)S(1)} collective-permute-done((bf16[32,3584]{1,0:T(8,128)(2,1)S(1)}, bf16[32,3584]{1,0:T(8,128)(2,1)S(1)}, u32[]{:S(2)}, u32[]{:S(2)}) %collective-permute-start) | collective-permute-done | bytes 229408 | tf_op jit(solution)/shard_map/ppermute | solution.py:396
  32.9 0.1 merge.2
  33.0 12.5 %all_to_all.21.parts_ref = bf16[8,4,3584]{2,1,0:T(4,128)(2,1)S(1)} all-to-all(bf16[8,4,3584]{2,1,0:T(4,128)(2,1)S(1)} %merge.2), channel_id=1, replica_groups=mesh['groups'=2,'epx'=2,'core'=2,'tp'=4] {'epx','tp'}, dimensions={0} | all-to-all | bytes 458752 | tf_op jit(solution)/shard_map/all_to_all | solution.py:400
  45.5 0.0 copy-done.3
  45.5 0.0 copy-done.4
  45.5 0.0 copy-done.5
  45.5 0.0 copy-done.6
  45.5 0.4 norm_rows.1
  46.0 11.3 %all_to_all.22.mine_ref = bf16[8,4,3712]{2,1,0:T(4,128)(2,1)S(1)} all-to-all(bf16[8,4,3712]{2,1,0:T(4,128)(2,1)S(1)} %get-tuple-element.19), channel_id=1, replica_groups=mesh['groups'=2,'epx'=2,'core'=2,'tp'=4] {'epx','tp'}, dimensions={0} | all-to-all | bytes 475136 | tf_op jit(solution)/shard_map/all_to_all | solution.py:400
  57.3 0.0 collective-permute-start.1
  57.3 1.5 %collective-permute-done.1.other_ref = bf16[8,4,3712]{2,1,0:T(4,128)(2,1)S(1)} collective-permute-done((bf16[8,4,3712]{2,1,0:T(4,128)(2,1)S(1)}, bf16[8,4,3712]{2,1,0:T(4,128)(2,1)S(1)}, u32[]{:S(2)}, u32[]{:S(2)}) %collective-permute-start.1) | collective-permute-done | bytes 237600 | tf_op jit(solution)/shard_map/ppermute | solution.py:396
  58.8 0.0 slice-done
  58.8 0.0 copy-done.2
  58.8 0.0 slice-done.1
  58.8 0.0 copy-done
  58.8 0.0 copy-done.1
  58.9 2.8 %experts.1 = (f32[32,3584]{1,0:T(8,128)S(1)}, bf16[32,3584]{1,0:T(8,128)(2,1)S(1)}) custom-call(bf16[8,4,3712]{2,1,0:T(4,128)(2,1)S(1)} %all_to_all.22.mine_ref, bf16[8,4,3712]{2,1,0:T(4,128)(2,1)S(1)} %collective-permute-done.1.other_ref, bf16[2,3584,512]{2,1,0:T(8,128)(2,1)S(1)} %bitcast.16, bf16[512,3584]{1,0:T(8,128)(2,1)S(1)} %bitcast.18, ...), custom_call_target="tpu_custom_call" | custom-call | tf_op jit(solution)/shard_map/experts/pallas_call | solution.py:359
  61.6 0.2 collective-permute-start.2
  61.8 1.4 %collective-permute-done.2.got_ref = bf16[32,3584]{1,0:T(8,128)(2,1)S(1)} collective-permute-done((bf16[32,3584]{1,0:T(8,128)(2,1)S(1)}, bf16[32,3584]{1,0:T(8,128)(2,1)S(1)}, u32[]{:S(2)}, u32[]{:S(2)}) %collective-permute-start.2) | collective-permute-done | bytes 229408 | tf_op jit(solution)/shard_map/ppermute | solution.py:396
  63.1 0.1 merge.3
  63.2 12.1 %all_to_all.23.parts_ref = bf16[8,4,3584]{2,1,0:T(4,128)(2,1)S(1)} all-to-all(bf16[8,4,3584]{2,1,0:T(4,128)(2,1)S(1)} %merge.3), channel_id=1, replica_groups=mesh['groups'=2,'epx'=2,'core'=2,'tp'=4] {'epx','tp'}, dimensions={0} | all-to-all | bytes 458752 | tf_op jit(solution)/shard_map/all_to_all | solution.py:400
  75.3 0.7 finish.1
  (1 shorter events, 0.0 us)
Async XLA Ops:
  0.7 58.2 %slice-start = ((s8[7340032]{0:T(1024)(128)(4,1)}), s8[4194304]{0:T(1024)(128)(4,1)S(1)}, s32[]{:S(2)}) async-start(s8[7340032]{0:T(1024)(128)(4,1)} %bitcast.14), calls=%async_computation.4 | async-start | bytes 8388608
  0.7 58.2 %copy-start.2 = (bf16[256,3584]{1,0:T(8,128)(2,1)S(1)}, bf16[256,3584]{1,0:T(8,128)(2,1)}, u32[]{:S(2)}) copy-start(bf16[256,3584]{1,0:T(8,128)(2,1)} %s_out_ref.1) | copy-start | bytes 5505028
  6.6 52.2 %slice-start.1 = ((s8[7340032]{0:T(1024)(128)(4,1)}), s8[3145728]{0:T(1024)(128)(4,1)S(1)}, s32[]{:S(2)}) async-start(s8[7340032]{0:T(1024)(128)(4,1)} %bitcast.14), calls=%async_computation.5 | async-start | bytes 6291456
  29.6 15.9 %copy-start.3 = (bf16[1,4,3584]{2,1,0:T(4,128)(2,1)S(1)}, bf16[1,4,3584]{2,1,0:T(4,128)(2,1)}, u32[]{:S(2)}) copy-start(bf16[1,4,3584]{2,1,0:T(4,128)(2,1)} %param.14) | copy-start | bytes 86020
  29.6 15.9 %copy-start.4 = (bf16[3584,4]{0,1:T(4,128)(2,1)S(1)}, bf16[3584,4]{0,1:T(4,128)(2,1)}, u32[]{:S(2)}) copy-start(bf16[3584,4]{0,1:T(4,128)(2,1)} %param.23) | copy-start | bytes 86020
  29.6 15.9 %copy-start.5 = (bf16[3584]{0:T(1024)(128)(2,1)S(1)}, bf16[3584]{0:T(1024)(128)(2,1)}, u32[]{:S(2)}) copy-start(bf16[3584]{0:T(1024)(128)(2,1)} %gain_ref.1) | copy-start | bytes 21508
  29.6 15.9 %copy-start.6 = (s32[4,4,2]{1,2,0:T(2,128)S(1)}, s32[4,4,2]{1,2,0:T(2,128)}, u32[]{:S(2)}) copy-start(s32[4,4,2]{1,2,0:T(2,128)} %param.19) | copy-start | bytes 388
  29.6 29.2 %copy-start = (bf16[1,512,3584]{2,1,0:T(8,128)(2,1)S(1)}, bf16[1,512,3584]{2,1,0:T(8,128)(2,1)}, u32[]{:S(2)}) copy-start(bf16[1,512,3584]{2,1,0:T(8,128)(2,1)} %param.25) | copy-start | bytes 11010052
  29.6 29.2 %copy-start.1 = (bf16[2,3584,256]{2,1,0:T(8,128)(2,1)S(1)}, bf16[2,3584,256]{2,1,0:T(8,128)(2,1)}, u32[]{:S(2)}) copy-start(bf16[2,3584,256]{2,1,0:T(8,128)(2,1)} %s_in_ref.1) | copy-start | bytes 11010052
  31.4 1.6 %collective-permute-start = (bf16[32,3584]{1,0:T(8,128)(2,1)S(1)}, bf16[32,3584]{1,0:T(8,128)(2,1)S(1)}, u32[]{:S(2)}, u32[]{:S(2)}) collective-permute-start(bf16[32,3584]{1,0:T(8,128)(2,1)S(1)} %get-tuple-element.18), channel_id=1, source_target_pairs={{0,4},{4,0},{1,5},{5,1},{2,6},{6,2},{3,7},{7,3},{8,12},{12,8},{9,1... | collective-permute-start | bytes 688136 | tf_op jit(solution)/shard_map/ppermute | solution.py:396
  57.3 1.5 %collective-permute-start.1 = (bf16[8,4,3712]{2,1,0:T(4,128)(2,1)S(1)}, bf16[8,4,3712]{2,1,0:T(4,128)(2,1)S(1)}, u32[]{:S(2)}, u32[]{:S(2)}) collective-permute-start(bf16[8,4,3712]{2,1,0:T(4,128)(2,1)S(1)} %all_to_all.22.mine_ref), channel_id=1, source_target_pairs={{0,4},{4,0},{1,5},{5,1},{2,6},{6,2},{3,7},{7,3},{8,12},{12,8},{9,1... | collective-permute-start | bytes 712712 | tf_op jit(solution)/shard_map/ppermute | solution.py:396
  61.6 1.5 %collective-permute-start.2 = (bf16[32,3584]{1,0:T(8,128)(2,1)S(1)}, bf16[32,3584]{1,0:T(8,128)(2,1)S(1)}, u32[]{:S(2)}, u32[]{:S(2)}) collective-permute-start(bf16[32,3584]{1,0:T(8,128)(2,1)S(1)} %get-tuple-element.21), channel_id=1, source_target_pairs={{0,4},{4,0},{1,5},{5,1},{2,6},{6,2},{3,7},{7,3},{8,12},{12,8},{9,1... | collective-permute-start | bytes 688136 | tf_op jit(solution)/shard_map/ppermute | solution.py:396

commit v5 on v4

--- a/solution.py
+++ b/solution.py
@@ -45,99 +45,154 @@
     return jax.ShapeDtypeStruct(x.shape, x.dtype)
 
 
-def attend_kernel(length_ref, q_hbm, kv_hbm, new_hbm, *refs, chunk, block, ahead):
+def attend_kernel(length_ref, q_hbm, kv_hbm, new_hbm, *refs, chunk, block, depth, ahead):
     stored, out_ref, held = refs[:ahead], refs[ahead], refs[ahead + 1 : 2 * ahead + 1]
-    new_ref, q_t, q_rows, kv_t, new_rows, scores, recent, weights, row_max, sems = (
-        refs[2 * ahead + 1 :]
-    )
+    new_ref, q_t, q_rows, kv_t, new_rows, scores, weights, row_max, mixed, sems = refs[
+        2 * ahead + 1 :
+    ]
     steps, width, heads = q_t.shape
     positions = kv_t.shape[1]
     rows = steps * heads
-    q_copy = pltpu.make_async_copy(q_hbm, q_t, sems.at[0])
-    q_copy.start()
-    new_copy = pltpu.make_async_copy(new_hbm, new_ref, sems.at[sems.shape[0] - 1])
+    blocks = rows // block
+    per_block = block // heads
+    chunks = positions // chunk
+    lanes = new_rows.shape[0]
+    q_copies = [
+        pltpu.make_async_copy(
+            q_hbm.at[pl.ds(b * per_block, per_block)],
+            q_t.at[pl.ds(b * per_block, per_block)],
+            sems.at[b],
+        )
+        for b in range(blocks)
+    ]
+    kv_copies = [
+        pltpu.make_async_copy(
+            kv_hbm.at[:, pl.ds(c * chunk, chunk)],
+            kv_t.at[:, pl.ds(c * chunk, chunk)],
+            sems.at[blocks + c],
+        )
+        for c in range(chunks)
+    ]
+    new_copy = pltpu.make_async_copy(new_hbm, new_ref, sems.at[blocks + chunks])
+    q_copies[0].start()
+    kv_copies[0].start()
     new_copy.start()
-    copies = []
-    for c in range(positions // chunk):
-        span = pl.ds(c * chunk, chunk)
-        copies.append(
-            pltpu.make_async_copy(kv_hbm.at[:, span], kv_t.at[:, span], sems.at[1 + c])
-        )
-        copies[-1].start()
+    for copy in q_copies[1:] + kv_copies[1:]:
+        copy.start()
     new_rows[...] = jnp.zeros_like(new_rows)
     new_copy.wait()
     new_rows[0:steps, :] = new_ref[...]
-    q_copy.wait()
-    for s in range(steps):
-        q_rows[s * heads : (s + 1) * heads, :] = q_t[s].T
     length = length_ref[0]
-    lanes = new_rows.shape[0]
-    fresh = lax.dot_general(
-        q_rows[...], new_rows[...], (((1,), (1,)), ((), ())),
-        preferred_element_type=jnp.float32,
-    )
-    step_of = lax.broadcasted_iota(jnp.int32, (rows, lanes), 0) // heads
-    fresh = jnp.where(
-        lax.broadcasted_iota(jnp.int32, (rows, lanes), 1) <= step_of, fresh, -1e30
-    )
-    recent[...] = fresh
-    row_max[...] = fresh
+    rate = score_scale * log2_e
+    per_owner = out_ref.shape[1] // (2 * steps)
+
+    def turn(b):
+        q_copies[b].wait()
+        for i in range(per_block):
+            s = b * per_block + i
+            q_rows[s * heads : (s + 1) * heads, :] = q_t[s].T
+
+    def score(b, c):
+        span = slice(b * block, (b + 1) * block)
+        s = jnp.dot(
+            q_rows[span, :], kv_t[:, c * chunk : (c + 1) * chunk],
+            preferred_element_type=jnp.float32,
+        )
+        live = (lax.broadcasted_iota(jnp.int32, (1, chunk), 1) + c * chunk) < length
+        s = jnp.where(live, s, -1e30)
+        scores[span, c * chunk : (c + 1) * chunk] = s
+        best = s[:, 0:lanes] if c == 0 else jnp.maximum(row_max[span, :], s[:, 0:lanes])
+        for j in range(1, chunk // lanes):
+            best = jnp.maximum(best, s[:, j * lanes : (j + 1) * lanes])
+        row_max[span, :] = best
+
+    def peak(b):
+        span = slice(b * block, (b + 1) * block)
+        fresh = lax.dot_general(
+            q_rows[span, :], new_rows[...], (((1,), (1,)), ((), ())),
+            preferred_element_type=jnp.float32,
+        )
+        step_of = b * per_block + lax.broadcasted_iota(jnp.int32, (block, lanes), 0) // heads
+        fresh = jnp.where(
+            lax.broadcasted_iota(jnp.int32, (block, lanes), 1) <= step_of, fresh, -1e30
+        )
+        top = jnp.max(jnp.maximum(row_max[span, :], fresh), axis=1, keepdims=True) * rate
+        fresh = jnp.exp2(fresh * rate - top)
+        return [top, fresh, fresh.astype(jnp.bfloat16)]
+
+    def soften(b, c, state):
+        span = slice(b * block, (b + 1) * block)
+        e = jnp.exp2(scores[span, c * chunk : (c + 1) * chunk] * rate - state[0])
+        for j in range(chunk // lanes):
+            state[1] = state[1] + e[:, j * lanes : (j + 1) * lanes]
+        weights[span, c * chunk : (c + 1) * chunk] = e.astype(jnp.bfloat16)
+
+    def mix(b, first, last, state):
+        span = slice(b * block, (b + 1) * block)
+        part = lax.dot_general(
+            weights[span, first * chunk : last * chunk],
+            kv_t[0:LAT, first * chunk : last * chunk],
+            (((1,), (1,)), ((), ())),
+            preferred_element_type=jnp.float32,
+        )
+        if first == 0:
+            part = part + jnp.dot(
+                state[2], new_rows[:, 0:LAT], preferred_element_type=jnp.float32
+            )
+        else:
+            part = part + mixed[...]
+        if last < chunks:
+            mixed[...] = part
+            return
+        part = part * (1.0 / jnp.sum(state[1], axis=1, keepdims=True))
+        for i in range(per_block):
+            s = b * per_block + i
+            for d in range(heads // per_owner):
+                column, side, t = d // (2 * depth), d // depth % 2, d % depth
+                row = (side * steps + s) * per_owner
+                first_row = i * heads + d * per_owner
+                out_ref[column * depth + t, row : row + per_owner, :] = part[
+                    first_row : first_row + per_owner, :
+                ].astype(jnp.bfloat16)
+
+    states = {}
     fetches = []
-    for c in range(positions // chunk):
-        copies[c].wait()
-        if c == 0:
-            fetches = fetch(stored, held, sems, 1 + positions // chunk)
-        live = (lax.broadcasted_iota(jnp.int32, (1, chunk), 1) + c * chunk) < length
-        for b in range(rows // block):
-            span = slice(b * block, (b + 1) * block)
-            s = jnp.dot(
-                q_rows[span, :], kv_t[:, c * chunk : (c + 1) * chunk],
-                preferred_element_type=jnp.float32,
-            )
-            s = jnp.where(live, s, -1e30)
-            scores[span, c * chunk : (c + 1) * chunk] = s
-            best = row_max[span, :]
-            for j in range(chunk // lanes):
-                best = jnp.maximum(best, s[:, j * lanes : (j + 1) * lanes])
-            row_max[span, :] = best
-    rate = score_scale * log2_e
-    per_owner = out_ref.shape[1] // steps
-    for b in range(rows // block):
-        span = slice(b * block, (b + 1) * block)
-        top = jnp.max(row_max[span, :], axis=1, keepdims=True) * rate
-        fresh = jnp.exp2(recent[span, :] * rate - top)
-        total = fresh
-        fresh = fresh.astype(jnp.bfloat16)
-        for c in range(positions // chunk):
-            e = jnp.exp2(scores[span, c * chunk : (c + 1) * chunk] * rate - top)
-            for j in range(chunk // lanes):
-                total = total + e[:, j * lanes : (j + 1) * lanes]
-            weights[span, c * chunk : (c + 1) * chunk] = e.astype(jnp.bfloat16)
-        mixed = lax.dot_general(
-            weights[span, :], kv_t[0:LAT, :], (((1,), (1,)), ((), ())),
-            preferred_element_type=jnp.float32,
-        ) + jnp.dot(fresh, new_rows[:, 0:LAT], preferred_element_type=jnp.float32)
-        mixed = mixed / jnp.sum(total, axis=1, keepdims=True)
-        for i in range(block // heads):
-            s = b * (block // heads) + i
-            part = mixed[i * heads : (i + 1) * heads, :]
-            out_ref[:, s * per_owner : (s + 1) * per_owner, :] = part.reshape(
-                heads // per_owner, per_owner, LAT
-            ).astype(jnp.bfloat16)
+    turn(0)
+    for stage in range(blocks + 2):
+        mixing = stage - 2
+        if mixing >= 0 and stage - 1 >= blocks:
+            mix(mixing, 0, chunks, states[mixing])
+            continue
+        for c in range(chunks):
+            if stage < blocks:
+                if stage == 0:
+                    kv_copies[c].wait()
+                    if c == 0:
+                        fetches = fetch(stored, held, sems, blocks + chunks + 1)
+                score(stage, c)
+                if c == 0 and stage + 1 < blocks:
+                    turn(stage + 1)
+            if 0 <= stage - 1 < blocks:
+                soften(stage - 1, c, states[stage - 1])
+            if mixing >= 0 and c % 2 == 1:
+                mix(mixing, c - 1, c + 1, states[mixing])
+        if stage < blocks:
+            states[stage] = peak(stage)
     for copy in fetches:
         copy.wait()
 
 
-def attend(queries, kv_cache, new_kv, lengths, owners, ahead):
+def attend(queries, kv_cache, new_kv, lengths, chips, depth, ahead, chunk=512):
     _, steps, heads, width = queries.shape
     positions = kv_cache.shape[1]
     rows = steps * heads
-    chunk = 512
     lanes = 128
     block = 2 * heads
     return pl.pallas_call(
-        functools.partial(attend_kernel, chunk=chunk, block=block, ahead=len(ahead)),
-        out_shape=[jax.ShapeDtypeStruct((owners, rows // owners, LAT), jnp.bfloat16)]
+        functools.partial(
+            attend_kernel, chunk=chunk, block=block, depth=depth, ahead=len(ahead)
+        ),
+        out_shape=[jax.ShapeDtypeStruct((chips, rows // chips, LAT), jnp.bfloat16)]
         + [like(x) for x in ahead],
         in_specs=[SMEM] + [HBM] * (3 + len(ahead)),
         out_specs=[VMEM] * (1 + len(ahead)),
@@ -148,12 +203,12 @@
             pltpu.VMEM((width, positions), jnp.bfloat16),
             pltpu.VMEM((lanes, width), jnp.bfloat16),
             pltpu.VMEM((rows, positions), jnp.float32),
-            pltpu.VMEM((rows, lanes), jnp.float32),
             pltpu.VMEM((rows, positions), jnp.bfloat16),
             pltpu.VMEM((rows, lanes), jnp.float32),
-            pltpu.SemaphoreType.DMA((2 + positions // chunk + len(ahead),)),
+            pltpu.VMEM((block, LAT), jnp.float32),
+            pltpu.SemaphoreType.DMA((rows // block + positions // chunk + 1 + len(ahead),)),
         ],
-        compiler_params=params(16),
+        compiler_params=params(20),
         name="attend",
     )(
         lengths,
@@ -164,91 +219,61 @@
     )
 
 
-def project_kernel(
-    latent_ref, up_ref, down_ref, *refs, depth, strip, ahead
-):
-    stored, kept_ref, sent_ref = refs[:ahead], refs[ahead], refs[ahead + 1]
-    held, latents, sems = refs[ahead + 2 : 2 * ahead + 2], refs[2 * ahead + 2], refs[2 * ahead + 3]
-    fetches = fetch(stored, held, sems, 0)
+def project_kernel(latent_ref, up_ref, up2_ref, down_ref, down2_ref, out_ref, latents, *, strip):
     sources, owned, _ = latent_ref.shape
     heads = up_ref.shape[0]
+    owned = owned // 2
     steps = owned // heads
     items = sources * steps
     core = lax.axis_index("core")
-    place = 0
-    for side in (core, 1 - core):
-        for column in range(sources // (2 * depth)):
-            for t in range(depth):
-                source = (column * 2 + side) * depth + t
-                block = latent_ref[source].astype(jnp.float32)
-                for j in range(LAT // 128):
-                    latents[j, place * owned : (place + 1) * owned, :] = block[
-                        :, j * 128 : (j + 1) * 128
-                    ]
-                place += 1
+    blocks = LAT // 128
     vals = []
-    for h in range(heads):
-        x = jnp.concatenate(
-            [latents[j, pl.ds(h, items, stride=heads), :] for j in range(LAT // 128)], axis=1
-        ).astype(jnp.bfloat16)
-        vals.append(
-            jnp.dot(x, up_ref[h], preferred_element_type=jnp.float32).astype(jnp.bfloat16)
-        )
-    vals = jnp.concatenate(vals, axis=1)
+    for side, w_ref in enumerate((up_ref, up2_ref)):
+        start = pl.multiple_of((core if side == 0 else 1 - core) * owned, owned)
+        for source in range(sources):
+            block = latent_ref[source, pl.ds(start, owned), :].astype(jnp.float32)
+            for j in range(blocks):
+                latents[side * blocks + j, source * owned : (source + 1) * owned, :] = block[
+                    :, j * 128 : (j + 1) * 128
+                ]
+        for h in range(heads):
+            x = jnp.concatenate(
+                [
+                    latents[side * blocks + j, pl.ds(h, items, stride=heads), :]
+                    for j in range(blocks)
+                ],
+                axis=1,
+            ).astype(jnp.bfloat16)
+            vals.append(
+                jnp.dot(x, w_ref[h], preferred_element_type=jnp.float32).astype(jnp.bfloat16)
+            )
+    own = jnp.concatenate(vals[:heads], axis=1)
+    partner = jnp.concatenate(vals[heads:], axis=1)
     width = down_ref.shape[1]
-    half = items // 2
     for n in range(width // strip):
         cols = slice(n * strip, (n + 1) * strip)
-        part = jnp.dot(vals, down_ref[:, cols], preferred_element_type=jnp.float32)
-        kept_ref[:, cols] = part[:half]
-        sent_ref[:, cols] = part[half:].astype(jnp.bfloat16)
-    for copy in fetches:
-        copy.wait()
-
-
-def project(by_head, value_up, out_proj, depth, ahead):
+        part = jnp.dot(own, down_ref[:, cols], preferred_element_type=jnp.float32)
+        part = part + jnp.dot(partner, down2_ref[:, cols], preferred_element_type=jnp.float32)
+        for j in range(sources):
+            out_ref[j, :, cols] = part[j * steps : (j + 1) * steps].astype(jnp.bfloat16)
+
+
+def project(by_head, value_up, value_up2, out_proj, out_proj2):
     sources, owned, _ = by_head.shape
     heads, _, value_width = value_up.shape
     width = out_proj.shape[2]
-    half = sources * owned // heads // 2
+    flat = (heads * value_width, width)
     return pl.pallas_call(
-        functools.partial(project_kernel, depth=depth, strip=512, ahead=len(ahead)),
-        out_shape=[
-            jax.ShapeDtypeStruct((half, width), jnp.float32),
-            jax.ShapeDtypeStruct((half, width), jnp.bfloat16),
-        ]
-        + [like(x) for x in ahead],
-        in_specs=[VMEM, VMEM, VMEM] + [HBM] * len(ahead),
-        out_specs=[VMEM] * (2 + len(ahead)),
+        functools.partial(project_kernel, strip=512),
+        out_shape=jax.ShapeDtypeStruct((sources, owned // (2 * heads), width), jnp.bfloat16),
+        in_specs=[VMEM] * 5,
+        out_specs=VMEM,
         scratch_shapes=[
-            pltpu.VMEM((LAT // 128, sources * owned, 128), jnp.float32),
-            pltpu.SemaphoreType.DMA((max(1, len(ahead)),)),
+            pltpu.VMEM((2 * LAT // 128, sources * owned // 2, 128), jnp.float32),
         ],
         compiler_params=params(8),
         name="project",
-    )(
-        by_head, value_up, out_proj.reshape(heads * value_width, width),
-        *[in_hbm(x) for x in ahead],
-    )
-
-
-def merge_kernel(kept_ref, got_ref, out_ref):
-    chips, items, _ = out_ref.shape
-    total = kept_ref[...] + got_ref[...].astype(jnp.float32)
-    for j in range(chips):
-        out_ref[j] = total[j * items : (j + 1) * items, :].astype(jnp.bfloat16)
-
-
-def merge(kept, got, chips):
-    rows, width = kept.shape
-    return pl.pallas_call(
-        merge_kernel,
-        out_shape=jax.ShapeDtypeStruct((chips, rows // chips, width), jnp.bfloat16),
-        in_specs=[VMEM, VMEM],
-        out_specs=VMEM,
-        compiler_params=params(4),
-        name="merge",
-    )(kept, got)
+    )(by_head, value_up, value_up2, out_proj.reshape(flat), out_proj2.reshape(flat))
 
 
 def norm_kernel(ids_ref, parts_ref, hidden_ref, gain_ref, router_ref, residual_ref, out_ref):
@@ -312,20 +337,79 @@
     )(ids, parts, hidden, gain, router.T)
 
 
-def experts_kernel(
-    mine_ref, other_ref, in_ref, out_w_ref, s_in_ref, s_out_ref,
-    kept_ref, sent_ref, tokens, tails, own, *, depth, experts, strip,
+def merge_kernel(kept_ref, got_ref, out_ref):
+    chips, items, _ = out_ref.shape
+    total = kept_ref[...] + got_ref[...].astype(jnp.float32)
+    for j in range(chips):
+        out_ref[j] = total[j * items : (j + 1) * items, :].astype(jnp.bfloat16)
+
+
+def merge(kept, got, chips):
+    rows, width = kept.shape
+    return pl.pallas_call(
+        merge_kernel,
+        out_shape=jax.ShapeDtypeStruct((chips, rows // chips, width), jnp.bfloat16),
+        in_specs=[VMEM, VMEM],
+        out_specs=VMEM,
+        compiler_params=params(4),
+        name="merge",
+    )(kept, got)
+
+
+def silu_gate(g, u):
+    return (g / (1.0 + jnp.exp(-g)) * u).astype(jnp.bfloat16)
+
+
+def gather_rows(ref, first, tokens, tails):
+    items = ref.shape[1]
+    width = tokens.shape[1]
+    for j in range(ref.shape[0]):
+        rows = slice(first + j * items, first + (j + 1) * items)
+        block = ref[j].astype(jnp.float32)
+        tokens[rows, :] = block[:, :width]
+        if tails is not None:
+            tails[rows, :] = block[:, width:]
+
+
+def shared_kernel(mine_ref, in_ref, out_w_ref, out_ref, tokens, *, strip):
+    rows, width = out_ref.shape
+    depth = rows // mine_ref.shape[1]
+    column = lax.axis_index("epx")
+    for t in range(depth):
+        items = mine_ref.shape[1]
+        tokens[t * items : (t + 1) * items, :] = mine_ref[column * depth + t].astype(
+            jnp.float32
+        )[:, :width]
+    x = tokens[...].astype(jnp.bfloat16)
+    g = jnp.dot(x, in_ref[0], preferred_element_type=jnp.float32)
+    u = jnp.dot(x, in_ref[1], preferred_element_type=jnp.float32)
+    act = silu_gate(g, u)
+    for n in range(width // strip):
+        cols = slice(n * strip, (n + 1) * strip)
+        out_ref[:, cols] = jnp.dot(act, out_w_ref[:, cols], preferred_element_type=jnp.float32)
+
+
+def run_shared(mine, shared_in, shared_out, depth):
+    rows, width = depth * mine.shape[1], shared_out.shape[1]
+    return pl.pallas_call(
+        functools.partial(shared_kernel, strip=512),
+        out_shape=jax.ShapeDtypeStruct((rows, width), jnp.float32),
+        in_specs=[VMEM] * 3,
+        out_specs=VMEM,
+        scratch_shapes=[pltpu.VMEM((rows, width), jnp.float32)],
+        compiler_params=params(6),
+        name="shared",
+    )(mine, shared_in, shared_out)
+
+
+def routed_kernel(
+    mine_ref, other_ref, in_ref, out_w_ref, sent_ref, act_ref, gate_ref, tokens, tails,
+    *, experts, strip,
 ):
-    chips, items, padded = mine_ref.shape
-    width = out_w_ref.shape[1]
-    half = chips * items
+    half, width = sent_ref.shape
     core, column = lax.axis_index("core"), lax.axis_index("epx")
-    for side, ref in enumerate((mine_ref, other_ref)):
-        for j in range(chips):
-            rows = slice(side * half + j * items, side * half + (j + 1) * items)
-            block = ref[j].astype(jnp.float32)
-            tokens[rows, :] = block[:, :width]
-            tails[rows, :] = block[:, width:]
+    gather_rows(mine_ref, 0, tokens, tails)
+    gather_rows(other_ref, half, tokens, tails)
     x = tokens[...].astype(jnp.bfloat16)
     here = column * 2 + core
     lane = lax.broadcasted_iota(jnp.int32, tails.shape, 1)
@@ -335,43 +419,61 @@
     )
     g = jnp.dot(x, in_ref[0], preferred_element_type=jnp.float32)
     u = jnp.dot(x, in_ref[1], preferred_element_type=jnp.float32)
-    act = (g / (1.0 + jnp.exp(-g)) * u).astype(jnp.bfloat16)
-    start = pl.multiple_of(column * (depth * items), depth * items)
-    xs = tokens[pl.ds(start, depth * items), :].astype(jnp.bfloat16)
-    sg = jnp.dot(xs, s_in_ref[0], preferred_element_type=jnp.float32)
-    su = jnp.dot(xs, s_in_ref[1], preferred_element_type=jnp.float32)
-    s_act = (sg / (1.0 + jnp.exp(-sg)) * su).astype(jnp.bfloat16)
+    act = silu_gate(g, u)
+    act_ref[...] = act[:half]
+    gate_ref[...] = jnp.broadcast_to(gate[:half], gate_ref.shape)
     for n in range(width // strip):
         cols = slice(n * strip, (n + 1) * strip)
-        y = gate * jnp.dot(act, out_w_ref[:, cols], preferred_element_type=jnp.float32)
-        ys = jnp.dot(s_act, s_out_ref[:, cols], preferred_element_type=jnp.float32)
-        sent_ref[:, cols] = y[half:].astype(jnp.bfloat16)
-        kept_ref[:, cols] = y[:half]
-        kept_ref[pl.ds(start, depth * items), cols] = (
-            kept_ref[pl.ds(start, depth * items), cols] + ys
+        y = gate[half:] * jnp.dot(
+            act[half:], out_w_ref[:, cols], preferred_element_type=jnp.float32
         )
-
-
-def run_experts(mine, other, expert_in, expert_out, shared_in, shared_out, depth, experts):
+        sent_ref[:, cols] = y.astype(jnp.bfloat16)
+
+
+def run_routed(mine, other, expert_in, expert_out, experts):
     chips, items, padded = mine.shape
-    width = expert_out.shape[1]
+    hidden, width = expert_out.shape
     half = chips * items
     return pl.pallas_call(
-        functools.partial(experts_kernel, depth=depth, experts=experts, strip=512),
+        functools.partial(routed_kernel, experts=experts, strip=512),
         out_shape=(
-            jax.ShapeDtypeStruct((half, width), jnp.float32),
             jax.ShapeDtypeStruct((half, width), jnp.bfloat16),
+            jax.ShapeDtypeStruct((half, hidden), jnp.bfloat16),
+            jax.ShapeDtypeStruct((half, 128), jnp.float32),
         ),
-        in_specs=[VMEM] * 6,
-        out_specs=(VMEM, VMEM),
+        in_specs=[VMEM] * 4,
+        out_specs=(VMEM, VMEM, VMEM),
         scratch_shapes=[
             pltpu.VMEM((2 * half, width), jnp.float32),
             pltpu.VMEM((2 * half, padded - width), jnp.float32),
-            pltpu.VMEM((depth * items, width), jnp.bfloat16),
         ],
         compiler_params=params(8),
-        name="experts",
-    )(mine, other, expert_in, expert_out, shared_in, shared_out)
+        name="routed",
+    )(mine, other, expert_in, expert_out)
+
+
+def keep_kernel(act_ref, gate_ref, out_w_ref, shared_ref, kept_ref, *, strip):
+    width = kept_ref.shape[1]
+    rows = shared_ref.shape[0]
+    start = pl.multiple_of(lax.axis_index("epx") * rows, rows)
+    gate = gate_ref[:, 0:1]
+    for n in range(width // strip):
+        cols = slice(n * strip, (n + 1) * strip)
+        kept_ref[:, cols] = gate * jnp.dot(
+            act_ref[...], out_w_ref[:, cols], preferred_element_type=jnp.float32
+        )
+    kept_ref[pl.ds(start, rows), :] = kept_ref[pl.ds(start, rows), :] + shared_ref[...]
+
+
+def run_keep(act, gate, expert_out, shared):
+    return pl.pallas_call(
+        functools.partial(keep_kernel, strip=512),
+        out_shape=jax.ShapeDtypeStruct((act.shape[0], expert_out.shape[1]), jnp.float32),
+        in_specs=[VMEM] * 4,
+        out_specs=VMEM,
+        compiler_params=params(6),
+        name="keep",
+    )(act, gate, expert_out, shared)
 
 
 def finish_kernel(parts_ref, residual_ref, out_ref):
@@ -551,27 +653,28 @@
     columns = lax.axis_size("epx")
     depth = lax.axis_size("tp")
     chips = columns * depth
-    owners = 2 * chips
     experts = router.shape[1]
 
+    value_up2 = swap_cores(value_up)
+    out_proj2 = swap_cores(out_proj)
+    expert_in, expert_out = expert_in[0], expert_out[0]
     latent_out, out_proj, value_up = attend(
-        queries, kv_cache, new_kv, lengths, owners, [out_proj, value_up]
-    )
-    expert_in, expert_out = expert_in[0], expert_out[0]
-    by_head = lax.all_to_all(latent_out, ALL, split_axis=0, concat_axis=0, tiled=True)
-    kept, sent = project(
-        by_head, value_up, out_proj, depth, []
-    )
-    parts = chip_exchange(merge(kept, swap_cores(sent), chips))
+        queries, kv_cache, new_kv, lengths, chips, depth, [out_proj, value_up]
+    )
+    by_head = chip_exchange(latent_out)
+    parts = chip_exchange(project(by_head, value_up, value_up2, out_proj, out_proj2))
     ids = jnp.swapaxes(expert_ids, 1, 2)
     residual, handed = norm_rows(
         ids, parts, hidden_in.reshape(items, model_width), norm_gain, router
     )
     mine = chip_exchange(handed)
-    kept, sent = run_experts(
-        mine, swap_cores(mine), expert_in, expert_out, shared_in, shared_out, depth, experts,
-    )
-    parts = chip_exchange(merge(kept, swap_cores(sent), chips))
+    other = swap_cores(mine)
+    shared = run_shared(mine, shared_in, shared_out, depth)
+    other, shared = lax.optimization_barrier((other, shared))
+    sent, act, gate = run_routed(mine, other, expert_in, expert_out, experts)
+    got = swap_cores(sent)
+    kept = run_keep(act, gate, expert_out, shared)
+    parts = chip_exchange(merge(kept, got, chips))
     return finish(parts, residual).reshape(rows_here, steps_here, model_width)
 
 

time: 76.2 us -> 73.4 us (0.963)
  waiting for transfers between devices: 4.33 us -> 1.19 us
  blocking collectives: 58.9 us -> 56.9 us
  Pallas kernels: 11.6 us -> 13.5 us
    all_to_all x1 -> x0, blocking collectives: 23 us -> none  [on_device(): lax.all_to_all(latent_out, ALL, split_axis=0, concat_axis=0, tiled=True)]
    all_to_all x3 -> x4, blocking collectives: 35.9 us -> 56.9 us  [chip_exchange(): return lax.all_to_all(x, CHIPS, split_axis=0, concat_axis=0, tiled=True)]
    ppermute x3 -> x4, waiting for transfers between devices: 4.33 us -> 1.19 us  [swap_cores(): return lax.ppermute(x, 'core', [(0, 1), (1, 0)])]
    pallas_call x2 -> x4, Pallas kernels: 4.48 us -> 6.79 us  [the longest x1 3.03 us: project(): pl.pallas_call(functools.partial(project_kernel, strip=512), out_shape=ja...]
  transfers between devices with their start and end apart: 3 -> 4, of which waited for: 3 -> 2; matrix products, arithmetic and copies ran while one was open for 0% -> 0% of each run, Pallas kernels for 0% -> 10%
where the time goes in v5:
time: 73.4 us; the launch traced here: 73.1 us
  blocking collectives  56.9 us (78%)
  Pallas kernels  13.5 us (18%)
  waiting for transfers between devices  1.19 us (2%)
  between operations  0.78 us (1%)
    all_to_all x4, blocking collectives, chip_exchange(): return lax.all_to_all(x, CHIPS, split_axis=0, concat_axis=0, tiled=True)  56.9 us
    pallas_call x1, Pallas kernels, attend(): pl.pallas_call(functools.partial(attend_kernel, chunk=chunk, block=block,...  5.52 us
    pallas_call x1, Pallas kernels, project(): pl.pallas_call(functools.partial(project_kernel, strip=512), out_shape=ja...  3.03 us
    pallas_call x1, Pallas kernels, run_routed(): pl.pallas_call(functools.partial(routed_kernel, experts=experts, strip=51...  2.1 us
  transfers between devices with their start and end apart: 4, of which 2 were waited for; matrix products, arithmetic and copies ran while one was open for 0% of the time, Pallas kernels for 10%

profile of v5, /device:TPU:0, one launch (start us, length us, event | category | flops | bytes accessed | tf_op | source)
XLA Modules:
  0.0 73.1 jit_solution(9345170298540352825)
XLA Ops:
  0.0 0.5 collective-permute-start.1
  0.5 0.0 collective-permute-start
  1.2 5.5 %attend.1 = (bf16[8,64,512]{2,1,0:T(8,128)(2,1)S(1)}, bf16[8,128,3584]{2,1,0:T(8,128)(2,1)S(1)}, bf16[8,512,128]{2,1,0:T(8,128)(2,1)S(1)}) custom-call(s32[1]{0:T(128)S(6)} %copy.15.length_ref, bf16[4,576,128]{2,1,0:T(8,128)(2,1)} %bitcast.26, bf16[576,2048]{1,0:T(8,128)(2,1)} %bitcast.25, bf16[4,576]{1,0:T(4,128)(2,1)} %bitcast.27, ...), custom_call_target="tpu_custom_call" | custom-call | tf_op jit(solution)/shard_map/attend/pallas_call | solution.py:191
  6.7 22.6 %all_to_all.20.latent_ref = bf16[8,64,512]{2,1,0:T(8,128)(2,1)S(1)} all-to-all(bf16[8,64,512]{2,1,0:T(8,128)(2,1)S(1)} %get-tuple-element.15), channel_id=1, replica_groups=mesh['groups'=2,'epx'=2,'core'=2,'tp'=4] {'epx','tp'}, dimensions={0} | all-to-all | bytes 1048576 | tf_op jit(solution)/shard_map/all_to_all | solution.py:502
  29.3 0.0 collective-permute-done.up2_ref
  29.3 0.0 collective-permute-done.1
  29.3 0.0 slice-start
  29.3 0.0 copy-start.3
  29.3 0.0 copy-start.4
  29.4 0.0 copy-start.5
  29.4 0.0 copy-start.6
  29.4 0.0 copy-start.1
  29.4 0.0 copy-start.2
  29.4 0.0 slice-start.1
  29.4 3.0 %project.1 = bf16[8,4,3584]{2,1,0:T(4,128)(2,1)S(1)} custom-call(bf16[8,64,512]{2,1,0:T(8,128)(2,1)S(1)} %all_to_all.20.latent_ref, bf16[8,512,128]{2,1,0:T(8,128)(2,1)S(1)} %get-tuple-element.16.up_ref, bf16[8,512,128]{2,1,0:T(8,128)(2,1)S(1)} %collective-permute-done.up2_ref, bf16[1024,3584]{1,0:T(8,128)(2,1)S(1)} %bitcast.21, bf16[1024,3584]{1,0:T(8,128)(2,1)S(1)} %bitcast.20), custom_call_target="tpu_custom_call" | custom-call | tf_op jit(solution)/shard_map/project/pallas_call | solution.py:266
  32.4 0.0 copy-start
  32.5 11.4 %all_to_all.21.parts_ref = bf16[8,4,3584]{2,1,0:T(4,128)(2,1)S(1)} all-to-all(bf16[8,4,3584]{2,1,0:T(4,128)(2,1)S(1)} %project.1), channel_id=1, replica_groups=mesh['groups'=2,'epx'=2,'core'=2,'tp'=4] {'epx','tp'}, dimensions={0} | all-to-all | bytes 458752 | tf_op jit(solution)/shard_map/all_to_all | solution.py:502
  43.9 0.0 copy-done.3
  43.9 0.0 copy-done.4
  43.9 0.0 copy-done.5
  43.9 0.0 copy-done.6
  43.9 0.4 norm_rows.1
  44.4 10.8 %all_to_all.22.mine_ref = bf16[8,4,3712]{2,1,0:T(4,128)(2,1)S(1)} all-to-all(bf16[8,4,3712]{2,1,0:T(4,128)(2,1)S(1)} %get-tuple-element.18), channel_id=1, replica_groups=mesh['groups'=2,'epx'=2,'core'=2,'tp'=4] {'epx','tp'}, dimensions={0} | all-to-all | bytes 475136 | tf_op jit(solution)/shard_map/all_to_all | solution.py:502
  55.1 0.0 collective-permute-start.2
  55.1 0.0 copy-done.1
  55.1 0.0 copy-done.2
  55.2 0.9 %shared.1.shared_ref = f32[16,3584]{1,0:T(8,128)S(1)} custom-call(bf16[8,4,3712]{2,1,0:T(4,128)(2,1)S(1)} %all_to_all.22.mine_ref, bf16[2,3584,256]{2,1,0:T(8,128)(2,1)S(1)} %copy-done.1, bf16[256,3584]{1,0:T(8,128)(2,1)S(1)} %copy-done.2), custom_call_target="tpu_custom_call" | custom-call | tf_op jit(solution)/shard_map/shared/pallas_call | solution.py:394
  56.1 0.6 collective-permute-done.2.other_ref
  56.6 0.0 slice-done
  56.6 0.0 slice-done.1
  56.6 0.0 copy-done
  56.7 2.1 %routed.1 = (bf16[32,3584]{1,0:T(8,128)(2,1)S(1)}, bf16[32,512]{1,0:T(8,128)(2,1)S(1)}, f32[32,128]{1,0:T(8,128)S(1)}) custom-call(bf16[8,4,3712]{2,1,0:T(4,128)(2,1)S(1)} %all_to_all.22.mine_ref, bf16[8,4,3712]{2,1,0:T(4,128)(2,1)S(1)} %collective-permute-done.2.other_ref, bf16[2,3584,512]{2,1,0:T(8,128)(2,1)S(1)} %bitcast.19, bf16[512,3584]{1,0:T(8,128)(2,1)S(1)} %bitcast.15), custom_call_target="tpu_custom_call" | custom-call | tf_op jit(solution)/shard_map/routed/pallas_call | solution.py:437
  58.8 0.2 collective-permute-start.3
  59.0 0.7 %keep.1.kept_ref = f32[32,3584]{1,0:T(8,128)S(1)} custom-call(bf16[32,512]{1,0:T(8,128)(2,1)S(1)} %get-tuple-element.20.act_ref, f32[32,128]{1,0:T(8,128)S(1)} %get-tuple-element.21.gate_ref, bf16[512,3584]{1,0:T(8,128)(2,1)S(1)} %bitcast.16, f32[16,3584]{1,0:T(8,128)S(1)} %shared.1.shared_ref), custom_call_target="tpu_custom_call" | custom-call | tf_op jit(solution)/shard_map/keep/pallas_call | solution.py:469
  59.7 0.6 collective-permute-done.3.got_ref
  60.3 0.1 merge.1
  60.4 12.1 %all_to_all.23.parts_ref = bf16[8,4,3584]{2,1,0:T(4,128)(2,1)S(1)} all-to-all(bf16[8,4,3584]{2,1,0:T(4,128)(2,1)S(1)} %merge.1), channel_id=1, replica_groups=mesh['groups'=2,'epx'=2,'core'=2,'tp'=4] {'epx','tp'}, dimensions={0} | all-to-all | bytes 458752 | tf_op jit(solution)/shard_map/all_to_all | solution.py:502
  72.4 0.7 finish.1
  (1 shorter events, 0.0 us)
Async XLA Ops:
  0.0 29.3 %collective-permute-start.1 = (bf16[8,128,3584]{2,1,0:T(8,128)(2,1)}, bf16[8,128,3584]{2,1,0:T(8,128)(2,1)S(1)}, u32[]{:S(2)}, u32[]{:S(2)}) collective-permute-start(bf16[8,128,3584]{2,1,0:T(8,128)(2,1)} %refs_0_.1), channel_id=1, source_target_pairs={{0,4},{4,0},{1,5},{5,1},{2,6},{6,2},{3,7},{7,3},{8,12},{12,8},{9,1... | collective-permute-start | bytes 22020104 | tf_op jit(solution)/shard_map/ppermute | solution.py:498
  0.5 28.8 %collective-permute-start = (bf16[8,512,128]{2,1,0:T(8,128)(2,1)}, bf16[8,512,128]{2,1,0:T(8,128)(2,1)S(1)}, u32[]{:S(2)}, u32[]{:S(2)}) collective-permute-start(bf16[8,512,128]{2,1,0:T(8,128)(2,1)} %refs_1_.1), channel_id=1, source_target_pairs={{0,4},{4,0},{1,5},{5,1},{2,6},{6,2},{3,7},{7,3},{8,12},{12,8},{9,1... | collective-permute-start | bytes 3145736 | tf_op jit(solution)/shard_map/ppermute | solution.py:498
  29.3 27.3 %slice-start = ((s8[7340032]{0:T(1024)(128)(4,1)}), s8[4194304]{0:T(1024)(128)(4,1)S(1)}, s32[]{:S(2)}) async-start(s8[7340032]{0:T(1024)(128)(4,1)} %bitcast.17), calls=%async_computation.4 | async-start | bytes 8388608
  29.3 14.6 %copy-start.3 = (bf16[1,4,3584]{2,1,0:T(4,128)(2,1)S(1)}, bf16[1,4,3584]{2,1,0:T(4,128)(2,1)}, u32[]{:S(2)}) copy-start(bf16[1,4,3584]{2,1,0:T(4,128)(2,1)} %param.14) | copy-start | bytes 86020
  29.3 14.5 %copy-start.4 = (bf16[3584,4]{0,1:T(4,128)(2,1)S(1)}, bf16[3584,4]{0,1:T(4,128)(2,1)}, u32[]{:S(2)}) copy-start(bf16[3584,4]{0,1:T(4,128)(2,1)} %param.23) | copy-start | bytes 86020
  29.4 14.5 %copy-start.5 = (bf16[3584]{0:T(1024)(128)(2,1)S(1)}, bf16[3584]{0:T(1024)(128)(2,1)}, u32[]{:S(2)}) copy-start(bf16[3584]{0:T(1024)(128)(2,1)} %gain_ref.1) | copy-start | bytes 21508
  29.4 14.5 %copy-start.6 = (s32[4,4,2]{1,2,0:T(2,128)S(1)}, s32[4,4,2]{1,2,0:T(2,128)}, u32[]{:S(2)}) copy-start(s32[4,4,2]{1,2,0:T(2,128)} %param.19) | copy-start | bytes 388
  29.4 25.8 %copy-start.1 = (bf16[2,3584,256]{2,1,0:T(8,128)(2,1)S(1)}, bf16[2,3584,256]{2,1,0:T(8,128)(2,1)}, u32[]{:S(2)}) copy-start(bf16[2,3584,256]{2,1,0:T(8,128)(2,1)} %in_ref.1) | copy-start | bytes 11010052
  29.4 25.8 %copy-start.2 = (bf16[256,3584]{1,0:T(8,128)(2,1)S(1)}, bf16[256,3584]{1,0:T(8,128)(2,1)}, u32[]{:S(2)}) copy-start(bf16[256,3584]{1,0:T(8,128)(2,1)} %out_w_ref.1) | copy-start | bytes 5505028
  29.4 27.2 %slice-start.1 = ((s8[7340032]{0:T(1024)(128)(4,1)}), s8[3145728]{0:T(1024)(128)(4,1)S(1)}, s32[]{:S(2)}) async-start(s8[7340032]{0:T(1024)(128)(4,1)} %bitcast.17), calls=%async_computation.5 | async-start | bytes 6291456
  32.4 24.2 %copy-start = (bf16[1,512,3584]{2,1,0:T(8,128)(2,1)S(1)}, bf16[1,512,3584]{2,1,0:T(8,128)(2,1)}, u32[]{:S(2)}) copy-start(bf16[1,512,3584]{2,1,0:T(8,128)(2,1)} %param.25) | copy-start | bytes 11010052
  55.1 1.5 %collective-permute-start.2 = (bf16[8,4,3712]{2,1,0:T(4,128)(2,1)S(1)}, bf16[8,4,3712]{2,1,0:T(4,128)(2,1)S(1)}, u32[]{:S(2)}, u32[]{:S(2)}) collective-permute-start(bf16[8,4,3712]{2,1,0:T(4,128)(2,1)S(1)} %all_to_all.22.mine_ref), channel_id=1, source_target_pairs={{0,4},{4,0},{1,5},{5,1},{2,6},{6,2},{3,7},{7,3},{8,12},{12,8},{9,1... | collective-permute-start | bytes 712712 | tf_op jit(solution)/shard_map/ppermute | solution.py:498
  58.8 1.6 %collective-permute-start.3 = (bf16[32,3584]{1,0:T(8,128)(2,1)S(1)}, bf16[32,3584]{1,0:T(8,128)(2,1)S(1)}, u32[]{:S(2)}, u32[]{:S(2)}) collective-permute-start(bf16[32,3584]{1,0:T(8,128)(2,1)S(1)} %get-tuple-element.23), channel_id=1, source_target_pairs={{0,4},{4,0},{1,5},{5,1},{2,6},{6,2},{3,7},{7,3},{8,12},{12,8},{9,1... | collective-permute-start | bytes 688136 | tf_op jit(solution)/shard_map/ppermute | solution.py:498

commit v6 on v5

--- a/solution.py
+++ b/solution.py
@@ -174,15 +174,15 @@
                     turn(stage + 1)
             if 0 <= stage - 1 < blocks:
                 soften(stage - 1, c, states[stage - 1])
-            if mixing >= 0 and c % 2 == 1:
-                mix(mixing, c - 1, c + 1, states[mixing])
+            if mixing >= 0:
+                mix(mixing, c, c + 1, states[mixing])
         if stage < blocks:
             states[stage] = peak(stage)
     for copy in fetches:
         copy.wait()
 
 
-def attend(queries, kv_cache, new_kv, lengths, chips, depth, ahead, chunk=512):
+def attend(queries, kv_cache, new_kv, lengths, chips, depth, ahead, chunk=1024):
     _, steps, heads, width = queries.shape
     positions = kv_cache.shape[1]
     rows = steps * heads

time: 73.4 us -> 73.2 us (level)
  no operation moved by 1% of the time
where the time goes in v6:
time: 73.2 us; the launch traced here: 73 us
  blocking collectives  56.9 us (78%)
  Pallas kernels  13.3 us (18%)
  waiting for transfers between devices  1.18 us (2%)
  between operations  0.77 us (1%)
    all_to_all x4, blocking collectives, chip_exchange(): return lax.all_to_all(x, CHIPS, split_axis=0, concat_axis=0, tiled=True)  56.9 us
    pallas_call x1, Pallas kernels, attend(): pl.pallas_call(functools.partial(attend_kernel, chunk=chunk, block=block,...  5.39 us
    pallas_call x1, Pallas kernels, project(): pl.pallas_call(functools.partial(project_kernel, strip=512), out_shape=ja...  3.03 us
    pallas_call x1, Pallas kernels, run_routed(): pl.pallas_call(functools.partial(routed_kernel, experts=experts, strip=51...  2.09 us
  transfers between devices with their start and end apart: 4, of which 2 were waited for; matrix products, arithmetic and copies ran while one was open for 0% of the time, Pallas kernels for 10%

profile of v6, /device:TPU:0, one launch (start us, length us, event | category | flops | bytes accessed | tf_op | source)
XLA Modules:
  0.0 73.0 jit_solution(18372976573140803508)
XLA Ops:
  0.0 0.5 collective-permute-start.1
  0.5 0.0 collective-permute-start
  1.2 5.4 %attend.1 = (bf16[8,64,512]{2,1,0:T(8,128)(2,1)S(1)}, bf16[8,128,3584]{2,1,0:T(8,128)(2,1)S(1)}, bf16[8,512,128]{2,1,0:T(8,128)(2,1)S(1)}) custom-call(s32[1]{0:T(128)S(6)} %copy.15.length_ref, bf16[4,576,128]{2,1,0:T(8,128)(2,1)} %bitcast.26, bf16[576,2048]{1,0:T(8,128)(2,1)} %bitcast.25, bf16[4,576]{1,0:T(4,128)(2,1)} %bitcast.27, ...), custom_call_target="tpu_custom_call" | custom-call | tf_op jit(solution)/shard_map/attend/pallas_call | solution.py:191
  6.6 22.6 %all_to_all.20.latent_ref = bf16[8,64,512]{2,1,0:T(8,128)(2,1)S(1)} all-to-all(bf16[8,64,512]{2,1,0:T(8,128)(2,1)S(1)} %get-tuple-element.15), channel_id=1, replica_groups=mesh['groups'=2,'epx'=2,'core'=2,'tp'=4] {'epx','tp'}, dimensions={0} | all-to-all | bytes 1048576 | tf_op jit(solution)/shard_map/all_to_all | solution.py:502
  29.2 0.0 collective-permute-done.up2_ref
  29.2 0.0 collective-permute-done.1
  29.2 0.0 slice-start
  29.2 0.0 copy-start.3
  29.2 0.0 copy-start.4
  29.2 0.0 copy-start.5
  29.2 0.0 copy-start.6
  29.3 0.0 copy-start.1
  29.3 0.0 copy-start.2
  29.3 0.0 slice-start.1
  29.3 3.0 %project.1 = bf16[8,4,3584]{2,1,0:T(4,128)(2,1)S(1)} custom-call(bf16[8,64,512]{2,1,0:T(8,128)(2,1)S(1)} %all_to_all.20.latent_ref, bf16[8,512,128]{2,1,0:T(8,128)(2,1)S(1)} %get-tuple-element.16.up_ref, bf16[8,512,128]{2,1,0:T(8,128)(2,1)S(1)} %collective-permute-done.up2_ref, bf16[1024,3584]{1,0:T(8,128)(2,1)S(1)} %bitcast.21, bf16[1024,3584]{1,0:T(8,128)(2,1)S(1)} %bitcast.20), custom_call_target="tpu_custom_call" | custom-call | tf_op jit(solution)/shard_map/project/pallas_call | solution.py:266
  32.3 0.0 copy-start
  32.3 11.4 %all_to_all.21.parts_ref = bf16[8,4,3584]{2,1,0:T(4,128)(2,1)S(1)} all-to-all(bf16[8,4,3584]{2,1,0:T(4,128)(2,1)S(1)} %project.1), channel_id=1, replica_groups=mesh['groups'=2,'epx'=2,'core'=2,'tp'=4] {'epx','tp'}, dimensions={0} | all-to-all | bytes 458752 | tf_op jit(solution)/shard_map/all_to_all | solution.py:502
  43.8 0.0 copy-done.3
  43.8 0.0 copy-done.4
  43.8 0.0 copy-done.5
  43.8 0.0 copy-done.6
  43.8 0.4 norm_rows.1
  44.2 10.8 %all_to_all.22.mine_ref = bf16[8,4,3712]{2,1,0:T(4,128)(2,1)S(1)} all-to-all(bf16[8,4,3712]{2,1,0:T(4,128)(2,1)S(1)} %get-tuple-element.18), channel_id=1, replica_groups=mesh['groups'=2,'epx'=2,'core'=2,'tp'=4] {'epx','tp'}, dimensions={0} | all-to-all | bytes 475136 | tf_op jit(solution)/shard_map/all_to_all | solution.py:502
  55.0 0.0 collective-permute-start.2
  55.0 0.0 copy-done.1
  55.0 0.0 copy-done.2
  55.0 0.9 %shared.1.shared_ref = f32[16,3584]{1,0:T(8,128)S(1)} custom-call(bf16[8,4,3712]{2,1,0:T(4,128)(2,1)S(1)} %all_to_all.22.mine_ref, bf16[2,3584,256]{2,1,0:T(8,128)(2,1)S(1)} %copy-done.1, bf16[256,3584]{1,0:T(8,128)(2,1)S(1)} %copy-done.2), custom_call_target="tpu_custom_call" | custom-call | tf_op jit(solution)/shard_map/shared/pallas_call | solution.py:394
  56.0 0.6 collective-permute-done.2.other_ref
  56.5 0.0 slice-done
  56.5 0.0 slice-done.1
  56.5 0.0 copy-done
  56.5 2.1 %routed.1 = (bf16[32,3584]{1,0:T(8,128)(2,1)S(1)}, bf16[32,512]{1,0:T(8,128)(2,1)S(1)}, f32[32,128]{1,0:T(8,128)S(1)}) custom-call(bf16[8,4,3712]{2,1,0:T(4,128)(2,1)S(1)} %all_to_all.22.mine_ref, bf16[8,4,3712]{2,1,0:T(4,128)(2,1)S(1)} %collective-permute-done.2.other_ref, bf16[2,3584,512]{2,1,0:T(8,128)(2,1)S(1)} %bitcast.19, bf16[512,3584]{1,0:T(8,128)(2,1)S(1)} %bitcast.15), custom_call_target="tpu_custom_call" | custom-call | tf_op jit(solution)/shard_map/routed/pallas_call | solution.py:437
  58.6 0.2 collective-permute-start.3
  58.8 0.7 %keep.1.kept_ref = f32[32,3584]{1,0:T(8,128)S(1)} custom-call(bf16[32,512]{1,0:T(8,128)(2,1)S(1)} %get-tuple-element.20.act_ref, f32[32,128]{1,0:T(8,128)S(1)} %get-tuple-element.21.gate_ref, bf16[512,3584]{1,0:T(8,128)(2,1)S(1)} %bitcast.16, f32[16,3584]{1,0:T(8,128)S(1)} %shared.1.shared_ref), custom_call_target="tpu_custom_call" | custom-call | tf_op jit(solution)/shard_map/keep/pallas_call | solution.py:469
  59.6 0.6 collective-permute-done.3.got_ref
  60.2 0.1 merge.1
  60.3 12.1 %all_to_all.23.parts_ref = bf16[8,4,3584]{2,1,0:T(4,128)(2,1)S(1)} all-to-all(bf16[8,4,3584]{2,1,0:T(4,128)(2,1)S(1)} %merge.1), channel_id=1, replica_groups=mesh['groups'=2,'epx'=2,'core'=2,'tp'=4] {'epx','tp'}, dimensions={0} | all-to-all | bytes 458752 | tf_op jit(solution)/shard_map/all_to_all | solution.py:502
  72.3 0.7 finish.1
  (1 shorter events, 0.0 us)
Async XLA Ops:
  0.0 29.2 %collective-permute-start.1 = (bf16[8,128,3584]{2,1,0:T(8,128)(2,1)}, bf16[8,128,3584]{2,1,0:T(8,128)(2,1)S(1)}, u32[]{:S(2)}, u32[]{:S(2)}) collective-permute-start(bf16[8,128,3584]{2,1,0:T(8,128)(2,1)} %refs_0_.1), channel_id=1, source_target_pairs={{0,4},{4,0},{1,5},{5,1},{2,6},{6,2},{3,7},{7,3},{8,12},{12,8},{9,1... | collective-permute-start | bytes 22020104 | tf_op jit(solution)/shard_map/ppermute | solution.py:498
  0.5 28.7 %collective-permute-start = (bf16[8,512,128]{2,1,0:T(8,128)(2,1)}, bf16[8,512,128]{2,1,0:T(8,128)(2,1)S(1)}, u32[]{:S(2)}, u32[]{:S(2)}) collective-permute-start(bf16[8,512,128]{2,1,0:T(8,128)(2,1)} %refs_1_.1), channel_id=1, source_target_pairs={{0,4},{4,0},{1,5},{5,1},{2,6},{6,2},{3,7},{7,3},{8,12},{12,8},{9,1... | collective-permute-start | bytes 3145736 | tf_op jit(solution)/shard_map/ppermute | solution.py:498
  29.2 27.3 %slice-start = ((s8[7340032]{0:T(1024)(128)(4,1)}), s8[4194304]{0:T(1024)(128)(4,1)S(1)}, s32[]{:S(2)}) async-start(s8[7340032]{0:T(1024)(128)(4,1)} %bitcast.17), calls=%async_computation.4 | async-start | bytes 8388608
  29.2 14.6 %copy-start.3 = (bf16[1,4,3584]{2,1,0:T(4,128)(2,1)S(1)}, bf16[1,4,3584]{2,1,0:T(4,128)(2,1)}, u32[]{:S(2)}) copy-start(bf16[1,4,3584]{2,1,0:T(4,128)(2,1)} %param.14) | copy-start | bytes 86020
  29.2 14.6 %copy-start.4 = (bf16[3584,4]{0,1:T(4,128)(2,1)S(1)}, bf16[3584,4]{0,1:T(4,128)(2,1)}, u32[]{:S(2)}) copy-start(bf16[3584,4]{0,1:T(4,128)(2,1)} %param.23) | copy-start | bytes 86020
  29.2 14.5 %copy-start.5 = (bf16[3584]{0:T(1024)(128)(2,1)S(1)}, bf16[3584]{0:T(1024)(128)(2,1)}, u32[]{:S(2)}) copy-start(bf16[3584]{0:T(1024)(128)(2,1)} %gain_ref.1) | copy-start | bytes 21508
  29.2 14.5 %copy-start.6 = (s32[4,4,2]{1,2,0:T(2,128)S(1)}, s32[4,4,2]{1,2,0:T(2,128)}, u32[]{:S(2)}) copy-start(s32[4,4,2]{1,2,0:T(2,128)} %param.19) | copy-start | bytes 388
  29.3 25.8 %copy-start.1 = (bf16[2,3584,256]{2,1,0:T(8,128)(2,1)S(1)}, bf16[2,3584,256]{2,1,0:T(8,128)(2,1)}, u32[]{:S(2)}) copy-start(bf16[2,3584,256]{2,1,0:T(8,128)(2,1)} %in_ref.1) | copy-start | bytes 11010052
  29.3 25.8 %copy-start.2 = (bf16[256,3584]{1,0:T(8,128)(2,1)S(1)}, bf16[256,3584]{1,0:T(8,128)(2,1)}, u32[]{:S(2)}) copy-start(bf16[256,3584]{1,0:T(8,128)(2,1)} %out_w_ref.1) | copy-start | bytes 5505028
  29.3 27.2 %slice-start.1 = ((s8[7340032]{0:T(1024)(128)(4,1)}), s8[3145728]{0:T(1024)(128)(4,1)S(1)}, s32[]{:S(2)}) async-start(s8[7340032]{0:T(1024)(128)(4,1)} %bitcast.17), calls=%async_computation.5 | async-start | bytes 6291456
  32.3 24.2 %copy-start = (bf16[1,512,3584]{2,1,0:T(8,128)(2,1)S(1)}, bf16[1,512,3584]{2,1,0:T(8,128)(2,1)}, u32[]{:S(2)}) copy-start(bf16[1,512,3584]{2,1,0:T(8,128)(2,1)} %param.25) | copy-start | bytes 11010052
  55.0 1.5 %collective-permute-start.2 = (bf16[8,4,3712]{2,1,0:T(4,128)(2,1)S(1)}, bf16[8,4,3712]{2,1,0:T(4,128)(2,1)S(1)}, u32[]{:S(2)}, u32[]{:S(2)}) collective-permute-start(bf16[8,4,3712]{2,1,0:T(4,128)(2,1)S(1)} %all_to_all.22.mine_ref), channel_id=1, source_target_pairs={{0,4},{4,0},{1,5},{5,1},{2,6},{6,2},{3,7},{7,3},{8,12},{12,8},{9,1... | collective-permute-start | bytes 712712 | tf_op jit(solution)/shard_map/ppermute | solution.py:498
  58.6 1.6 %collective-permute-start.3 = (bf16[32,3584]{1,0:T(8,128)(2,1)S(1)}, bf16[32,3584]{1,0:T(8,128)(2,1)S(1)}, u32[]{:S(2)}, u32[]{:S(2)}) collective-permute-start(bf16[32,3584]{1,0:T(8,128)(2,1)S(1)} %get-tuple-element.23), channel_id=1, source_target_pairs={{0,4},{4,0},{1,5},{5,1},{2,6},{6,2},{3,7},{7,3},{8,12},{12,8},{9,1... | collective-permute-start | bytes 688136 | tf_op jit(solution)/shard_map/ppermute | solution.py:498

commit v7 on v6

--- a/solution.py
+++ b/solution.py
@@ -2,6 +2,7 @@
 
 import jax
 import jax.numpy as jnp
+import numpy as np
 from jax import lax
 from jax.experimental import pallas as pl
 from jax.experimental.pallas import tpu as pltpu
@@ -45,7 +46,7 @@
     return jax.ShapeDtypeStruct(x.shape, x.dtype)
 
 
-def attend_kernel(length_ref, q_hbm, kv_hbm, new_hbm, *refs, chunk, block, depth, ahead):
+def attend_kernel(length_ref, q_hbm, kv_hbm, new_hbm, *refs, chunk, block, depth, places, ahead):
     stored, out_ref, held = refs[:ahead], refs[ahead], refs[ahead + 1 : 2 * ahead + 1]
     new_ref, q_t, q_rows, kv_t, new_rows, scores, weights, row_max, mixed, sems = refs[
         2 * ahead + 1 :
@@ -151,7 +152,7 @@
                 column, side, t = d // (2 * depth), d // depth % 2, d % depth
                 row = (side * steps + s) * per_owner
                 first_row = i * heads + d * per_owner
-                out_ref[column * depth + t, row : row + per_owner, :] = part[
+                out_ref[places[column * depth + t], row : row + per_owner, :] = part[
                     first_row : first_row + per_owner, :
                 ].astype(jnp.bfloat16)
 
@@ -182,15 +183,21 @@
         copy.wait()
 
 
-def attend(queries, kv_cache, new_kv, lengths, chips, depth, ahead, chunk=1024):
+def attend(queries, kv_cache, new_kv, lengths, places, depth, ahead, chunk=1024):
     _, steps, heads, width = queries.shape
     positions = kv_cache.shape[1]
     rows = steps * heads
     lanes = 128
     block = 2 * heads
+    chips = len(places)
     return pl.pallas_call(
         functools.partial(
-            attend_kernel, chunk=chunk, block=block, depth=depth, ahead=len(ahead)
+            attend_kernel,
+            chunk=chunk,
+            block=block,
+            depth=depth,
+            places=places,
+            ahead=len(ahead),
         ),
         out_shape=[jax.ShapeDtypeStruct((chips, rows // chips, LAT), jnp.bfloat16)]
         + [like(x) for x in ahead],
@@ -371,15 +378,17 @@
             tails[rows, :] = block[:, width:]
 
 
-def shared_kernel(mine_ref, in_ref, out_w_ref, out_ref, tokens, *, strip):
+def shared_kernel(mine_ref, in_ref, out_w_ref, out_ref, tokens, *, strip, places):
     rows, width = out_ref.shape
     depth = rows // mine_ref.shape[1]
     column = lax.axis_index("epx")
+    items = mine_ref.shape[1]
     for t in range(depth):
-        items = mine_ref.shape[1]
-        tokens[t * items : (t + 1) * items, :] = mine_ref[column * depth + t].astype(
-            jnp.float32
-        )[:, :width]
+        place = sum(
+            jnp.where(column == x, places[x * depth + t], 0)
+            for x in range(len(places) // depth)
+        )
+        tokens[t * items : (t + 1) * items, :] = mine_ref[place].astype(jnp.float32)[:, :width]
     x = tokens[...].astype(jnp.bfloat16)
     g = jnp.dot(x, in_ref[0], preferred_element_type=jnp.float32)
     u = jnp.dot(x, in_ref[1], preferred_element_type=jnp.float32)
@@ -389,10 +398,10 @@
         out_ref[:, cols] = jnp.dot(act, out_w_ref[:, cols], preferred_element_type=jnp.float32)
 
 
-def run_shared(mine, shared_in, shared_out, depth):
+def run_shared(mine, shared_in, shared_out, places, depth):
     rows, width = depth * mine.shape[1], shared_out.shape[1]
     return pl.pallas_call(
-        functools.partial(shared_kernel, strip=512),
+        functools.partial(shared_kernel, strip=512, places=places),
         out_shape=jax.ShapeDtypeStruct((rows, width), jnp.float32),
         in_specs=[VMEM] * 3,
         out_specs=VMEM,
@@ -452,22 +461,30 @@
     )(mine, other, expert_in, expert_out)
 
 
-def keep_kernel(act_ref, gate_ref, out_w_ref, shared_ref, kept_ref, *, strip):
+def keep_kernel(act_ref, gate_ref, out_w_ref, shared_ref, kept_ref, *, strip, places):
     width = kept_ref.shape[1]
     rows = shared_ref.shape[0]
-    start = pl.multiple_of(lax.axis_index("epx") * rows, rows)
+    items = kept_ref.shape[0] // len(places)
+    depth = rows // items
+    column = lax.axis_index("epx")
     gate = gate_ref[:, 0:1]
     for n in range(width // strip):
         cols = slice(n * strip, (n + 1) * strip)
         kept_ref[:, cols] = gate * jnp.dot(
             act_ref[...], out_w_ref[:, cols], preferred_element_type=jnp.float32
         )
-    kept_ref[pl.ds(start, rows), :] = kept_ref[pl.ds(start, rows), :] + shared_ref[...]
-
-
-def run_keep(act, gate, expert_out, shared):
+    for x in range(len(places) // depth):
+        for t in range(depth):
+            first = places[x * depth + t] * items
+            part = shared_ref[t * items : (t + 1) * items, :]
+            kept_ref[first : first + items, :] = kept_ref[first : first + items, :] + jnp.where(
+                column == x, part, 0.0
+            )
+
+
+def run_keep(act, gate, expert_out, shared, places):
     return pl.pallas_call(
-        functools.partial(keep_kernel, strip=512),
+        functools.partial(keep_kernel, strip=512, places=places),
         out_shape=jax.ShapeDtypeStruct((act.shape[0], expert_out.shape[1]), jnp.float32),
         in_specs=[VMEM] * 4,
         out_specs=VMEM,
@@ -500,6 +517,19 @@
 
 def chip_exchange(x):
     return lax.all_to_all(x, CHIPS, split_axis=0, concat_axis=0, tiled=True)
+
+
+def order_of_chips(chips):
+    return [int(chip) for chip in np.random.RandomState(28286).permutation(chips)]
+
+
+def plane_exchange(x, order, depth):
+    groups = [
+        [(chip // depth * 2 + core) * depth + chip % depth for chip in order] for core in range(2)
+    ]
+    return lax.all_to_all(
+        x, ALL, split_axis=0, concat_axis=0, axis_index_groups=groups, tiled=True
+    )
 
 
 def attend_block(queries, kv_cache, new_kv, lengths):
@@ -653,28 +683,32 @@
     columns = lax.axis_size("epx")
     depth = lax.axis_size("tp")
     chips = columns * depth
+    order = order_of_chips(chips)
+    places = [order.index(chip) for chip in range(chips)]
     experts = router.shape[1]
 
     value_up2 = swap_cores(value_up)
     out_proj2 = swap_cores(out_proj)
     expert_in, expert_out = expert_in[0], expert_out[0]
     latent_out, out_proj, value_up = attend(
-        queries, kv_cache, new_kv, lengths, chips, depth, [out_proj, value_up]
-    )
-    by_head = chip_exchange(latent_out)
-    parts = chip_exchange(project(by_head, value_up, value_up2, out_proj, out_proj2))
+        queries, kv_cache, new_kv, lengths, places, depth, [out_proj, value_up]
+    )
+    by_head = plane_exchange(latent_out, order, depth)
+    parts = plane_exchange(
+        project(by_head, value_up, value_up2, out_proj, out_proj2), order, depth
+    )
     ids = jnp.swapaxes(expert_ids, 1, 2)
     residual, handed = norm_rows(
         ids, parts, hidden_in.reshape(items, model_width), norm_gain, router
     )
-    mine = chip_exchange(handed)
+    mine = plane_exchange(handed, order, depth)
     other = swap_cores(mine)
-    shared = run_shared(mine, shared_in, shared_out, depth)
+    shared = run_shared(mine, shared_in, shared_out, places, depth)
     other, shared = lax.optimization_barrier((other, shared))
     sent, act, gate = run_routed(mine, other, expert_in, expert_out, experts)
     got = swap_cores(sent)
-    kept = run_keep(act, gate, expert_out, shared)
-    parts = chip_exchange(merge(kept, got, chips))
+    kept = run_keep(act, gate, expert_out, shared, places)
+    parts = plane_exchange(merge(kept, got, chips), order, depth)
     return finish(parts, residual).reshape(rows_here, steps_here, model_width)
 
 

time: 73.2 us -> 67.7 us (0.925)
  blocking collectives: 56.9 us -> 51.4 us
    all_to_all x4, blocking collectives: 56.9 us -> 51.4 us  [plane_exchange(): lax.all_to_all(x, ALL, split_axis=0, concat_axis=0, axis_index_groups=gro...]
where the time goes in v7:
time: 67.7 us; the launch traced here: 67.5 us
  blocking collectives  51.4 us (76%)
  Pallas kernels  13.4 us (20%)
  waiting for transfers between devices  1.15 us (2%)
  between operations  0.78 us (1%)
  starting transfers between devices  0.71 us (1%)
    all_to_all x4, blocking collectives, plane_exchange(): lax.all_to_all(x, ALL, split_axis=0, concat_axis=0, axis_index_groups=gro...  51.4 us
    pallas_call x1, Pallas kernels, attend(): pl.pallas_call(functools.partial(attend_kernel, chunk=chunk, block=block,...  5.39 us
    pallas_call x1, Pallas kernels, project(): pl.pallas_call(functools.partial(project_kernel, strip=512), out_shape=ja...  3.03 us
    pallas_call x1, Pallas kernels, run_routed(): pl.pallas_call(functools.partial(routed_kernel, experts=experts, strip=51...  2.09 us
  transfers between devices with their start and end apart: 4, of which 2 were waited for; matrix products, arithmetic and copies ran while one was open for 0% of the time, Pallas kernels for 10%

profile of v7, /device:TPU:0, one launch (start us, length us, event | category | flops | bytes accessed | tf_op | source)
XLA Modules:
  0.0 67.5 jit_solution(4685627579645136606)
XLA Ops:
  0.0 0.5 collective-permute-start.1
  0.5 0.0 collective-permute-start
  1.2 5.4 %attend.1 = (bf16[8,64,512]{2,1,0:T(8,128)(2,1)S(1)}, bf16[8,128,3584]{2,1,0:T(8,128)(2,1)S(1)}, bf16[8,512,128]{2,1,0:T(8,128)(2,1)S(1)}) custom-call(s32[1]{0:T(128)S(6)} %copy.15.length_ref, bf16[4,576,128]{2,1,0:T(8,128)(2,1)} %bitcast.26, bf16[576,2048]{1,0:T(8,128)(2,1)} %bitcast.25, bf16[4,576]{1,0:T(4,128)(2,1)} %bitcast.27, ...), custom_call_target="tpu_custom_call" | custom-call | tf_op jit(solution)/shard_map/attend/pallas_call | solution.py:193
  6.6 20.1 %all_to_all.20.latent_ref = bf16[8,64,512]{2,1,0:T(8,128)(2,1)S(1)} all-to-all(bf16[8,64,512]{2,1,0:T(8,128)(2,1)S(1)} %get-tuple-element.15), channel_id=1, replica_groups={{9,3,0,10,11,1,8,2},{13,7,4,14,15,5,12,6},{25,19,16,26,27,17,24,18},{29..., dimensions={0} | all-to-all | bytes 1048576 | tf_op jit(solution)/shard_map/all_to_all | solution.py:530
  26.7 0.0 collective-permute-done.up2_ref
  26.7 0.0 collective-permute-done.1
  26.7 0.0 slice-start
  26.7 0.0 copy-start.3
  26.7 0.0 copy-start.4
  26.7 0.0 copy-start.5
  26.7 0.0 copy-start.6
  26.8 0.0 copy-start.1
  26.8 0.0 copy-start.2
  26.8 0.0 slice-start.1
  26.8 3.0 %project.1 = bf16[8,4,3584]{2,1,0:T(4,128)(2,1)S(1)} custom-call(bf16[8,64,512]{2,1,0:T(8,128)(2,1)S(1)} %all_to_all.20.latent_ref, bf16[8,512,128]{2,1,0:T(8,128)(2,1)S(1)} %get-tuple-element.16.up_ref, bf16[8,512,128]{2,1,0:T(8,128)(2,1)S(1)} %collective-permute-done.up2_ref, bf16[1024,3584]{1,0:T(8,128)(2,1)S(1)} %bitcast.21, bf16[1024,3584]{1,0:T(8,128)(2,1)S(1)} %bitcast.20), custom_call_target="tpu_custom_call" | custom-call | tf_op jit(solution)/shard_map/project/pallas_call | solution.py:273
  29.8 0.0 copy-start
  29.8 10.7 %all_to_all.21.parts_ref = bf16[8,4,3584]{2,1,0:T(4,128)(2,1)S(1)} all-to-all(bf16[8,4,3584]{2,1,0:T(4,128)(2,1)S(1)} %project.1), channel_id=1, replica_groups={{9,3,0,10,11,1,8,2},{13,7,4,14,15,5,12,6},{25,19,16,26,27,17,24,18},{29..., dimensions={0} | all-to-all | bytes 458752 | tf_op jit(solution)/shard_map/all_to_all | solution.py:530
  40.5 0.0 copy-done.3
  40.5 0.0 copy-done.4
  40.5 0.0 copy-done.5
  40.5 0.0 copy-done.6
  40.6 0.4 norm_rows.1
  41.0 10.2 %all_to_all.22.mine_ref = bf16[8,4,3712]{2,1,0:T(4,128)(2,1)S(1)} all-to-all(bf16[8,4,3712]{2,1,0:T(4,128)(2,1)S(1)} %get-tuple-element.18), channel_id=1, replica_groups={{9,3,0,10,11,1,8,2},{13,7,4,14,15,5,12,6},{25,19,16,26,27,17,24,18},{29..., dimensions={0} | all-to-all | bytes 475136 | tf_op jit(solution)/shard_map/all_to_all | solution.py:530
  51.2 0.0 collective-permute-start.2
  51.2 0.0 copy-done.1
  51.2 0.0 copy-done.2
  51.2 0.9 %shared.1.shared_ref = f32[16,3584]{1,0:T(8,128)S(1)} custom-call(bf16[8,4,3712]{2,1,0:T(4,128)(2,1)S(1)} %all_to_all.22.mine_ref, bf16[2,3584,256]{2,1,0:T(8,128)(2,1)S(1)} %copy-done.1, bf16[256,3584]{1,0:T(8,128)(2,1)S(1)} %copy-done.2), custom_call_target="tpu_custom_call" | custom-call | tf_op jit(solution)/shard_map/shared/pallas_call | solution.py:403
  52.2 0.6 collective-permute-done.2.other_ref
  52.7 0.0 slice-done
  52.7 0.0 slice-done.1
  52.7 0.0 copy-done
  52.8 2.1 %routed.1 = (bf16[32,3584]{1,0:T(8,128)(2,1)S(1)}, bf16[32,512]{1,0:T(8,128)(2,1)S(1)}, f32[32,128]{1,0:T(8,128)S(1)}) custom-call(bf16[8,4,3712]{2,1,0:T(4,128)(2,1)S(1)} %all_to_all.22.mine_ref, bf16[8,4,3712]{2,1,0:T(4,128)(2,1)S(1)} %collective-permute-done.2.other_ref, bf16[2,3584,512]{2,1,0:T(8,128)(2,1)S(1)} %bitcast.19, bf16[512,3584]{1,0:T(8,128)(2,1)S(1)} %bitcast.15), custom_call_target="tpu_custom_call" | custom-call | tf_op jit(solution)/shard_map/routed/pallas_call | solution.py:446
  54.8 0.2 collective-permute-start.3
  55.0 0.8 %keep.1.kept_ref = f32[32,3584]{1,0:T(8,128)S(1)} custom-call(bf16[32,512]{1,0:T(8,128)(2,1)S(1)} %get-tuple-element.20.act_ref, f32[32,128]{1,0:T(8,128)S(1)} %get-tuple-element.21.gate_ref, bf16[512,3584]{1,0:T(8,128)(2,1)S(1)} %bitcast.16, f32[16,3584]{1,0:T(8,128)S(1)} %shared.1.shared_ref), custom_call_target="tpu_custom_call" | custom-call | tf_op jit(solution)/shard_map/keep/pallas_call | solution.py:486
  55.8 0.6 collective-permute-done.3.got_ref
  56.4 0.1 merge.1
  56.5 10.4 %all_to_all.23.parts_ref = bf16[8,4,3584]{2,1,0:T(4,128)(2,1)S(1)} all-to-all(bf16[8,4,3584]{2,1,0:T(4,128)(2,1)S(1)} %merge.1), channel_id=1, replica_groups={{9,3,0,10,11,1,8,2},{13,7,4,14,15,5,12,6},{25,19,16,26,27,17,24,18},{29..., dimensions={0} | all-to-all | bytes 458752 | tf_op jit(solution)/shard_map/all_to_all | solution.py:530
  66.8 0.7 finish.1
  (1 shorter events, 0.0 us)
Async XLA Ops:
  0.0 26.7 %collective-permute-start.1 = (bf16[8,128,3584]{2,1,0:T(8,128)(2,1)}, bf16[8,128,3584]{2,1,0:T(8,128)(2,1)S(1)}, u32[]{:S(2)}, u32[]{:S(2)}) collective-permute-start(bf16[8,128,3584]{2,1,0:T(8,128)(2,1)} %refs_0_.1), channel_id=1, source_target_pairs={{0,4},{4,0},{1,5},{5,1},{2,6},{6,2},{3,7},{7,3},{8,12},{12,8},{9,1... | collective-permute-start | bytes 22020104 | tf_op jit(solution)/shard_map/ppermute | solution.py:515
  0.5 26.2 %collective-permute-start = (bf16[8,512,128]{2,1,0:T(8,128)(2,1)}, bf16[8,512,128]{2,1,0:T(8,128)(2,1)S(1)}, u32[]{:S(2)}, u32[]{:S(2)}) collective-permute-start(bf16[8,512,128]{2,1,0:T(8,128)(2,1)} %refs_1_.1), channel_id=1, source_target_pairs={{0,4},{4,0},{1,5},{5,1},{2,6},{6,2},{3,7},{7,3},{8,12},{12,8},{9,1... | collective-permute-start | bytes 3145736 | tf_op jit(solution)/shard_map/ppermute | solution.py:515
  26.7 26.0 %slice-start = ((s8[7340032]{0:T(1024)(128)(4,1)}), s8[4194304]{0:T(1024)(128)(4,1)S(1)}, s32[]{:S(2)}) async-start(s8[7340032]{0:T(1024)(128)(4,1)} %bitcast.17), calls=%async_computation.4 | async-start | bytes 8388608
  26.7 13.8 %copy-start.3 = (bf16[1,4,3584]{2,1,0:T(4,128)(2,1)S(1)}, bf16[1,4,3584]{2,1,0:T(4,128)(2,1)}, u32[]{:S(2)}) copy-start(bf16[1,4,3584]{2,1,0:T(4,128)(2,1)} %param.14) | copy-start | bytes 86020
  26.7 13.8 %copy-start.4 = (bf16[3584,4]{0,1:T(4,128)(2,1)S(1)}, bf16[3584,4]{0,1:T(4,128)(2,1)}, u32[]{:S(2)}) copy-start(bf16[3584,4]{0,1:T(4,128)(2,1)} %param.23) | copy-start | bytes 86020
  26.7 13.8 %copy-start.5 = (bf16[3584]{0:T(1024)(128)(2,1)S(1)}, bf16[3584]{0:T(1024)(128)(2,1)}, u32[]{:S(2)}) copy-start(bf16[3584]{0:T(1024)(128)(2,1)} %gain_ref.1) | copy-start | bytes 21508
  26.7 13.8 %copy-start.6 = (s32[4,4,2]{1,2,0:T(2,128)S(1)}, s32[4,4,2]{1,2,0:T(2,128)}, u32[]{:S(2)}) copy-start(s32[4,4,2]{1,2,0:T(2,128)} %param.19) | copy-start | bytes 388
  26.8 24.5 %copy-start.1 = (bf16[2,3584,256]{2,1,0:T(8,128)(2,1)S(1)}, bf16[2,3584,256]{2,1,0:T(8,128)(2,1)}, u32[]{:S(2)}) copy-start(bf16[2,3584,256]{2,1,0:T(8,128)(2,1)} %in_ref.1) | copy-start | bytes 11010052
  26.8 24.5 %copy-start.2 = (bf16[256,3584]{1,0:T(8,128)(2,1)S(1)}, bf16[256,3584]{1,0:T(8,128)(2,1)}, u32[]{:S(2)}) copy-start(bf16[256,3584]{1,0:T(8,128)(2,1)} %out_w_ref.1) | copy-start | bytes 5505028
  26.8 26.0 %slice-start.1 = ((s8[7340032]{0:T(1024)(128)(4,1)}), s8[3145728]{0:T(1024)(128)(4,1)S(1)}, s32[]{:S(2)}) async-start(s8[7340032]{0:T(1024)(128)(4,1)} %bitcast.17), calls=%async_computation.5 | async-start | bytes 6291456
  29.8 22.9 %copy-start = (bf16[1,512,3584]{2,1,0:T(8,128)(2,1)S(1)}, bf16[1,512,3584]{2,1,0:T(8,128)(2,1)}, u32[]{:S(2)}) copy-start(bf16[1,512,3584]{2,1,0:T(8,128)(2,1)} %param.25) | copy-start | bytes 11010052
  51.2 1.5 %collective-permute-start.2 = (bf16[8,4,3712]{2,1,0:T(4,128)(2,1)S(1)}, bf16[8,4,3712]{2,1,0:T(4,128)(2,1)S(1)}, u32[]{:S(2)}, u32[]{:S(2)}) collective-permute-start(bf16[8,4,3712]{2,1,0:T(4,128)(2,1)S(1)} %all_to_all.22.mine_ref), channel_id=1, source_target_pairs={{0,4},{4,0},{1,5},{5,1},{2,6},{6,2},{3,7},{7,3},{8,12},{12,8},{9,1... | collective-permute-start | bytes 712712 | tf_op jit(solution)/shard_map/ppermute | solution.py:515
  54.8 1.6 %collective-permute-start.3 = (bf16[32,3584]{1,0:T(8,128)(2,1)S(1)}, bf16[32,3584]{1,0:T(8,128)(2,1)S(1)}, u32[]{:S(2)}, u32[]{:S(2)}) collective-permute-start(bf16[32,3584]{1,0:T(8,128)(2,1)S(1)} %get-tuple-element.23), channel_id=1, source_target_pairs={{0,4},{4,0},{1,5},{5,1},{2,6},{6,2},{3,7},{7,3},{8,12},{12,8},{9,1... | collective-permute-start | bytes 688136 | tf_op jit(solution)/shard_map/ppermute | solution.py:515

commit v8 on v7

--- a/solution.py
+++ b/solution.py
@@ -520,7 +520,7 @@
 
 
 def order_of_chips(chips):
-    return [int(chip) for chip in np.random.RandomState(28286).permutation(chips)]
+    return [int(chip) for chip in np.random.RandomState(98737).permutation(chips)]
 
 
 def plane_exchange(x, order, depth):

time: 67.7 us -> 65.7 us (0.970)
  blocking collectives: 51.4 us -> 49.4 us
    all_to_all x4, blocking collectives: 51.4 us -> 49.4 us  [plane_exchange(): lax.all_to_all(x, ALL, split_axis=0, concat_axis=0, axis_index_groups=gro...]
  transfers between devices with their start and end apart: 4 -> 4, of which waited for: 2 -> 2; matrix products, arithmetic and copies ran while one was open for 0% -> 0% of each run, Pallas kernels for 10% -> 11%
where the time goes in v8:
time: 65.7 us; the launch traced here: 65.4 us
  blocking collectives  49.4 us (75%)
  Pallas kernels  13.4 us (20%)
  waiting for transfers between devices  1.16 us (2%)
  between operations  0.78 us (1%)
  starting transfers between devices  0.71 us (1%)
    all_to_all x4, blocking collectives, plane_exchange(): lax.all_to_all(x, ALL, split_axis=0, concat_axis=0, axis_index_groups=gro...  49.4 us
    pallas_call x1, Pallas kernels, attend(): pl.pallas_call(functools.partial(attend_kernel, chunk=chunk, block=block,...  5.39 us
    pallas_call x1, Pallas kernels, project(): pl.pallas_call(functools.partial(project_kernel, strip=512), out_shape=ja...  3.03 us
    pallas_call x1, Pallas kernels, run_routed(): pl.pallas_call(functools.partial(routed_kernel, experts=experts, strip=51...  2.09 us
  transfers between devices with their start and end apart: 4, of which 2 were waited for; matrix products, arithmetic and copies ran while one was open for 0% of the time, Pallas kernels for 11%

profile of v8, /device:TPU:0, one launch (start us, length us, event | category | flops | bytes accessed | tf_op | source)
XLA Modules:
  0.0 65.4 jit_solution(15225813118387937865)
XLA Ops:
  0.0 0.5 collective-permute-start.1
  0.5 0.0 collective-permute-start
  1.2 5.4 %attend.1 = (bf16[8,64,512]{2,1,0:T(8,128)(2,1)S(1)}, bf16[8,128,3584]{2,1,0:T(8,128)(2,1)S(1)}, bf16[8,512,128]{2,1,0:T(8,128)(2,1)S(1)}) custom-call(s32[1]{0:T(128)S(6)} %copy.15.length_ref, bf16[4,576,128]{2,1,0:T(8,128)(2,1)} %bitcast.26, bf16[576,2048]{1,0:T(8,128)(2,1)} %bitcast.25, bf16[4,576]{1,0:T(4,128)(2,1)} %bitcast.27, ...), custom_call_target="tpu_custom_call" | custom-call | tf_op jit(solution)/shard_map/attend/pallas_call | solution.py:193
  6.6 19.4 %all_to_all.20.latent_ref = bf16[8,64,512]{2,1,0:T(8,128)(2,1)S(1)} all-to-all(bf16[8,64,512]{2,1,0:T(8,128)(2,1)S(1)} %get-tuple-element.15), channel_id=1, replica_groups={{10,0,2,11,8,1,9,3},{14,4,6,15,12,5,13,7},{26,16,18,27,24,17,25,19},{30..., dimensions={0} | all-to-all | bytes 1048576 | tf_op jit(solution)/shard_map/all_to_all | solution.py:530
  25.9 0.0 collective-permute-done.up2_ref
  26.0 0.0 collective-permute-done.1
  26.0 0.0 slice-start
  26.0 0.0 copy-start.3
  26.0 0.0 copy-start.4
  26.0 0.0 copy-start.5
  26.0 0.0 copy-start.6
  26.0 0.0 copy-start.1
  26.0 0.0 copy-start.2
  26.0 0.0 slice-start.1
  26.0 3.0 %project.1 = bf16[8,4,3584]{2,1,0:T(4,128)(2,1)S(1)} custom-call(bf16[8,64,512]{2,1,0:T(8,128)(2,1)S(1)} %all_to_all.20.latent_ref, bf16[8,512,128]{2,1,0:T(8,128)(2,1)S(1)} %get-tuple-element.16.up_ref, bf16[8,512,128]{2,1,0:T(8,128)(2,1)S(1)} %collective-permute-done.up2_ref, bf16[1024,3584]{1,0:T(8,128)(2,1)S(1)} %bitcast.21, bf16[1024,3584]{1,0:T(8,128)(2,1)S(1)} %bitcast.20), custom_call_target="tpu_custom_call" | custom-call | tf_op jit(solution)/shard_map/project/pallas_call | solution.py:273
  29.1 0.0 copy-start
  29.1 9.9 %all_to_all.21.parts_ref = bf16[8,4,3584]{2,1,0:T(4,128)(2,1)S(1)} all-to-all(bf16[8,4,3584]{2,1,0:T(4,128)(2,1)S(1)} %project.1), channel_id=1, replica_groups={{10,0,2,11,8,1,9,3},{14,4,6,15,12,5,13,7},{26,16,18,27,24,17,25,19},{30..., dimensions={0} | all-to-all | bytes 458752 | tf_op jit(solution)/shard_map/all_to_all | solution.py:530
  39.0 0.0 copy-done.3
  39.0 0.0 copy-done.4
  39.0 0.0 copy-done.5
  39.0 0.0 copy-done.6
  39.0 0.4 norm_rows.1
  39.4 9.7 %all_to_all.22.mine_ref = bf16[8,4,3712]{2,1,0:T(4,128)(2,1)S(1)} all-to-all(bf16[8,4,3712]{2,1,0:T(4,128)(2,1)S(1)} %get-tuple-element.18), channel_id=1, replica_groups={{10,0,2,11,8,1,9,3},{14,4,6,15,12,5,13,7},{26,16,18,27,24,17,25,19},{30..., dimensions={0} | all-to-all | bytes 475136 | tf_op jit(solution)/shard_map/all_to_all | solution.py:530
  49.1 0.0 collective-permute-start.2
  49.1 0.0 copy-done.1
  49.1 0.0 copy-done.2
  49.1 0.9 %shared.1.shared_ref = f32[16,3584]{1,0:T(8,128)S(1)} custom-call(bf16[8,4,3712]{2,1,0:T(4,128)(2,1)S(1)} %all_to_all.22.mine_ref, bf16[2,3584,256]{2,1,0:T(8,128)(2,1)S(1)} %copy-done.1, bf16[256,3584]{1,0:T(8,128)(2,1)S(1)} %copy-done.2), custom_call_target="tpu_custom_call" | custom-call | tf_op jit(solution)/shard_map/shared/pallas_call | solution.py:403
  50.1 0.6 collective-permute-done.2.other_ref
  50.6 0.0 slice-done
  50.6 0.0 slice-done.1
  50.6 0.0 copy-done
  50.6 2.1 %routed.1 = (bf16[32,3584]{1,0:T(8,128)(2,1)S(1)}, bf16[32,512]{1,0:T(8,128)(2,1)S(1)}, f32[32,128]{1,0:T(8,128)S(1)}) custom-call(bf16[8,4,3712]{2,1,0:T(4,128)(2,1)S(1)} %all_to_all.22.mine_ref, bf16[8,4,3712]{2,1,0:T(4,128)(2,1)S(1)} %collective-permute-done.2.other_ref, bf16[2,3584,512]{2,1,0:T(8,128)(2,1)S(1)} %bitcast.19, bf16[512,3584]{1,0:T(8,128)(2,1)S(1)} %bitcast.15), custom_call_target="tpu_custom_call" | custom-call | tf_op jit(solution)/shard_map/routed/pallas_call | solution.py:446
  52.7 0.2 collective-permute-start.3
  52.9 0.8 %keep.1.kept_ref = f32[32,3584]{1,0:T(8,128)S(1)} custom-call(bf16[32,512]{1,0:T(8,128)(2,1)S(1)} %get-tuple-element.20.act_ref, f32[32,128]{1,0:T(8,128)S(1)} %get-tuple-element.21.gate_ref, bf16[512,3584]{1,0:T(8,128)(2,1)S(1)} %bitcast.16, f32[16,3584]{1,0:T(8,128)S(1)} %shared.1.shared_ref), custom_call_target="tpu_custom_call" | custom-call | tf_op jit(solution)/shard_map/keep/pallas_call | solution.py:486
  53.7 0.6 collective-permute-done.3.got_ref
  54.3 0.1 merge.1
  54.4 10.4 %all_to_all.23.parts_ref = bf16[8,4,3584]{2,1,0:T(4,128)(2,1)S(1)} all-to-all(bf16[8,4,3584]{2,1,0:T(4,128)(2,1)S(1)} %merge.1), channel_id=1, replica_groups={{10,0,2,11,8,1,9,3},{14,4,6,15,12,5,13,7},{26,16,18,27,24,17,25,19},{30..., dimensions={0} | all-to-all | bytes 458752 | tf_op jit(solution)/shard_map/all_to_all | solution.py:530
  64.8 0.7 finish.1
  (1 shorter events, 0.0 us)
Async XLA Ops:
  0.0 26.0 %collective-permute-start.1 = (bf16[8,128,3584]{2,1,0:T(8,128)(2,1)}, bf16[8,128,3584]{2,1,0:T(8,128)(2,1)S(1)}, u32[]{:S(2)}, u32[]{:S(2)}) collective-permute-start(bf16[8,128,3584]{2,1,0:T(8,128)(2,1)} %refs_0_.1), channel_id=1, source_target_pairs={{0,4},{4,0},{1,5},{5,1},{2,6},{6,2},{3,7},{7,3},{8,12},{12,8},{9,1... | collective-permute-start | bytes 22020104 | tf_op jit(solution)/shard_map/ppermute | solution.py:515
  0.5 25.5 %collective-permute-start = (bf16[8,512,128]{2,1,0:T(8,128)(2,1)}, bf16[8,512,128]{2,1,0:T(8,128)(2,1)S(1)}, u32[]{:S(2)}, u32[]{:S(2)}) collective-permute-start(bf16[8,512,128]{2,1,0:T(8,128)(2,1)} %refs_1_.1), channel_id=1, source_target_pairs={{0,4},{4,0},{1,5},{5,1},{2,6},{6,2},{3,7},{7,3},{8,12},{12,8},{9,1... | collective-permute-start | bytes 3145736 | tf_op jit(solution)/shard_map/ppermute | solution.py:515
  26.0 24.7 %slice-start = ((s8[7340032]{0:T(1024)(128)(4,1)}), s8[4194304]{0:T(1024)(128)(4,1)S(1)}, s32[]{:S(2)}) async-start(s8[7340032]{0:T(1024)(128)(4,1)} %bitcast.17), calls=%async_computation.4 | async-start | bytes 8388608
  26.0 13.0 %copy-start.3 = (bf16[1,4,3584]{2,1,0:T(4,128)(2,1)S(1)}, bf16[1,4,3584]{2,1,0:T(4,128)(2,1)}, u32[]{:S(2)}) copy-start(bf16[1,4,3584]{2,1,0:T(4,128)(2,1)} %param.14) | copy-start | bytes 86020
  26.0 13.0 %copy-start.4 = (bf16[3584,4]{0,1:T(4,128)(2,1)S(1)}, bf16[3584,4]{0,1:T(4,128)(2,1)}, u32[]{:S(2)}) copy-start(bf16[3584,4]{0,1:T(4,128)(2,1)} %param.23) | copy-start | bytes 86020
  26.0 13.0 %copy-start.5 = (bf16[3584]{0:T(1024)(128)(2,1)S(1)}, bf16[3584]{0:T(1024)(128)(2,1)}, u32[]{:S(2)}) copy-start(bf16[3584]{0:T(1024)(128)(2,1)} %gain_ref.1) | copy-start | bytes 21508
  26.0 13.0 %copy-start.6 = (s32[4,4,2]{1,2,0:T(2,128)S(1)}, s32[4,4,2]{1,2,0:T(2,128)}, u32[]{:S(2)}) copy-start(s32[4,4,2]{1,2,0:T(2,128)} %param.19) | copy-start | bytes 388
  26.0 23.1 %copy-start.1 = (bf16[2,3584,256]{2,1,0:T(8,128)(2,1)S(1)}, bf16[2,3584,256]{2,1,0:T(8,128)(2,1)}, u32[]{:S(2)}) copy-start(bf16[2,3584,256]{2,1,0:T(8,128)(2,1)} %in_ref.1) | copy-start | bytes 11010052
  26.0 23.1 %copy-start.2 = (bf16[256,3584]{1,0:T(8,128)(2,1)S(1)}, bf16[256,3584]{1,0:T(8,128)(2,1)}, u32[]{:S(2)}) copy-start(bf16[256,3584]{1,0:T(8,128)(2,1)} %out_w_ref.1) | copy-start | bytes 5505028
  26.0 24.6 %slice-start.1 = ((s8[7340032]{0:T(1024)(128)(4,1)}), s8[3145728]{0:T(1024)(128)(4,1)S(1)}, s32[]{:S(2)}) async-start(s8[7340032]{0:T(1024)(128)(4,1)} %bitcast.17), calls=%async_computation.5 | async-start | bytes 6291456
  29.1 21.6 %copy-start = (bf16[1,512,3584]{2,1,0:T(8,128)(2,1)S(1)}, bf16[1,512,3584]{2,1,0:T(8,128)(2,1)}, u32[]{:S(2)}) copy-start(bf16[1,512,3584]{2,1,0:T(8,128)(2,1)} %param.25) | copy-start | bytes 11010052
  49.1 1.5 %collective-permute-start.2 = (bf16[8,4,3712]{2,1,0:T(4,128)(2,1)S(1)}, bf16[8,4,3712]{2,1,0:T(4,128)(2,1)S(1)}, u32[]{:S(2)}, u32[]{:S(2)}) collective-permute-start(bf16[8,4,3712]{2,1,0:T(4,128)(2,1)S(1)} %all_to_all.22.mine_ref), channel_id=1, source_target_pairs={{0,4},{4,0},{1,5},{5,1},{2,6},{6,2},{3,7},{7,3},{8,12},{12,8},{9,1... | collective-permute-start | bytes 712712 | tf_op jit(solution)/shard_map/ppermute | solution.py:515
  52.7 1.6 %collective-permute-start.3 = (bf16[32,3584]{1,0:T(8,128)(2,1)S(1)}, bf16[32,3584]{1,0:T(8,128)(2,1)S(1)}, u32[]{:S(2)}, u32[]{:S(2)}) collective-permute-start(bf16[32,3584]{1,0:T(8,128)(2,1)S(1)} %get-tuple-element.23), channel_id=1, source_target_pairs={{0,4},{4,0},{1,5},{5,1},{2,6},{6,2},{3,7},{7,3},{8,12},{12,8},{9,1... | collective-permute-start | bytes 688136 | tf_op jit(solution)/shard_map/ppermute | solution.py:515
